TPU v7x, 512 devices: a whole 4x8x8 slice. The times are simulated.
512 devices in a mesh: dp: 128 (over z_lo, y, x, core), mp: 4 (over z_hi).
Axes of the slice: x: 4, y: 8, z: 8 (z_hi: 4, z_lo: 2; z = z_hi * 2 + z_lo), core: 2. Of those that a mesh axis runs over, the one named last changes fastest.
Arguments:
- feature_ids: int32 [16384, 128], P('dp'), may hold values from 0 to 8191
- emb_table: bfloat16 [8192, 128], P(('dp', 'mp')), may hold values from -6 to 6
- factor_machine_projection: bfloat16 [128, 32], replicated, may hold values from -0.5 to 0.5
- mlp_weight: float32 [4096, 1024], P('dp', 'mp'), may hold values from -0.09375 to 0.09375
- momentum: float32 [4096, 1024], P('dp', 'mp'), may hold values from -6 to 6
- hidden_grad: bfloat16 [16384, 1024], P('dp', 'mp'), may hold values from -0.125 to 0.125
- lcb_grad: bfloat16 [16384, 128, 128], P('dp', 'mp'), may hold values from -0.009765625 to 0.009765625
Outputs:
- new_weight: float32 [4096, 1024], P('dp', 'mp')
- new_momentum: float32 [4096, 1024], P('dp', 'mp')
- next_weight: bfloat16 [4096, 1024], P(None, 'mp')
- proj_grad: float32 [128, 32], replicated
- lcb_weight_grad: float32 [128, 128], P(None, 'mp')
All inputs are finite; a program needn't handle non-finite values.
Results may differ from a plain program's by a relative error of at most 0.0074.
Values may be sent and summed in bfloat16 or wider, within the bound.
No kernel may reach another device: no remote copies, remote signals or barrier semaphores. Data moves between devices by JAX's collectives and lax.ppermute only.
A program may use at most 64 MiB of HBM per device.

v0:
```python
import functools

import jax
import jax.numpy as jnp
from jax import lax
from jax.sharding import Mesh
from jax.sharding import PartitionSpec as P

DP = ("dp_0", "dp_1", "dp_2", "dp_3")
DP_MP = ("dp_0", "dp_1", "dp_2", "dp_3", "mp")


def from_everyone(x, axis):
    copies = jnp.broadcast_to(x, (lax.axis_size(axis), *x.shape))
    return lax.all_to_all(copies, axis, split_axis=0, concat_axis=0, tiled=True)


def joined_along(tiles, dim):
    tiles = jnp.moveaxis(tiles, 0, dim)
    lengths = tiles.shape
    return tiles.reshape(*lengths[:dim], lengths[dim] * lengths[dim + 1], *lengths[dim + 2 :])


def gather_directly(x, axis, dim):
    tiles = from_everyone(x, axis)
    return joined_along(tiles, dim)


def gathered_by_axis(x, axes, dim):
    far, near = axes
    initial = from_everyone(x, far)
    tiles = jnp.swapaxes(from_everyone(initial, near), 0, 1)
    return joined_along(tiles.reshape(-1, *x.shape), dim)


def in_blocks(x, dim, length):
    lengths = x.shape
    tiles = x.reshape(*lengths[:dim], length, lengths[dim] // length, *lengths[dim + 1 :])
    return jnp.moveaxis(tiles, dim, 0)


def sum_at_owner(x, axis, dim):
    tiles = in_blocks(x, dim, lax.axis_size(axis))
    arrived = lax.all_to_all(tiles, axis, split_axis=0, concat_axis=0, tiled=True)
    return arrived.astype(jnp.float32).sum(axis=0)


def sum_by_axis(x, axes, dim):
    far, near = axes
    own = sum_at_owner(in_blocks(x, dim, lax.axis_size(far)), near, dim + 1)
    return jnp.sum(
        lax.all_to_all(own.astype(jnp.bfloat16), far, 0, 0, tiled=True).astype(jnp.float32), axis=0
    )


def over_axes(x, axes):
    return functools.reduce(lax.psum, axes, x)


def over_copies(x, axis):
    everything = from_everyone(x, axis)
    return jnp.sum(everything, axis=0)


def by_axis(x, axes):
    far, near = axes
    nearer = over_copies(x, near)
    return over_copies(nearer, far)


def forward_features(embedded_rows, factor_machine_projection):
    examples = embedded_rows.shape[0]
    n_emb = embedded_rows.shape[1]
    rank = factor_machine_projection.shape[1]
    compressed_rows = jnp.einsum(
        "fpy,po->foy", embedded_rows, factor_machine_projection, preferred_element_type=jnp.float32
    ).astype(jnp.bfloat16)
    factor_machine_output = jnp.einsum(
        "cqr,cor->cqo", compressed_rows, embedded_rows, preferred_element_type=jnp.float32
    )
    factor_machine_output = factor_machine_output.reshape(examples, rank * n_emb)
    row_mean = jnp.mean(factor_machine_output, axis=1, keepdims=True)
    centered = factor_machine_output - row_mean
    row_var = jnp.mean(centered * centered, axis=1, keepdims=True)
    inv_scale = 1.0 / jnp.sqrt(row_var + 1.0)
    normed = centered * inv_scale
    return (normed, inv_scale)


def backward_features(embedded_rows, normed, inv_scale, normed_grad, rank):
    examples = embedded_rows.shape[0]
    n_emb = embedded_rows.shape[1]
    factor_machine_gradient = (
        normed_grad
        - jnp.mean(normed_grad, axis=1, keepdims=True)
        - normed * jnp.mean(normed_grad * normed, axis=1, keepdims=True)
    ) * inv_scale
    factor_machine_gradient = factor_machine_gradient.astype(jnp.bfloat16).reshape(
        examples, rank, n_emb
    )
    projection_backprop = jnp.einsum(
        "soe,sez->soz", factor_machine_gradient, embedded_rows, preferred_element_type=jnp.float32
    ).astype(jnp.bfloat16)
    return jnp.einsum(
        "jlh,jqh->lq", embedded_rows, projection_backprop, preferred_element_type=jnp.float32
    )


def per_device(
    feature_ids, emb_table, factor_machine_projection, mlp_weight, momentum, hidden_grad, lcb_grad
):
    table_group = gather_directly(emb_table, "mp", 0)
    table_full = gathered_by_axis(table_group, (("dp_0", "dp_1", "dp_2"), "dp_3"), 0)
    embedded_rows = jnp.take(table_full, feature_ids, axis=0)
    examples = embedded_rows.shape[0]
    rank = factor_machine_projection.shape[1]
    lcb_part = jnp.einsum(
        "bnd,bld->nl", embedded_rows, lcb_grad, preferred_element_type=jnp.float32
    )
    weight_bf = mlp_weight.astype(jnp.bfloat16)
    weights_full = gathered_by_axis(weight_bf, (("dp_0", "dp_1", "dp_2"), "dp_3"), 0)
    members = lax.axis_size("mp")
    share = examples // members
    begin_row = lax.axis_index("mp") * share
    embedded_share = lax.dynamic_slice_in_dim(embedded_rows, begin_row, share, 0)
    normed, inv_scale = forward_features(embedded_share, factor_machine_projection)
    normed_bf = normed.astype(jnp.bfloat16)
    normed_all = gather_directly(normed_bf, "mp", 0)
    preact = jnp.dot(normed_all, weights_full, preferred_element_type=jnp.float32)
    sigmoid_pre = jax.nn.sigmoid(preact)
    preact_grad = (
        hidden_grad.astype(jnp.float32) * sigmoid_pre * (1.0 + preact * (1.0 - sigmoid_pre))
    ).astype(jnp.bfloat16)
    weight_grad = sum_by_axis(
        lax.dot_general(
            normed_all, preact_grad, (((0,), (0,)), ((), ())), preferred_element_type=jnp.float32
        ).astype(jnp.bfloat16),
        (("dp_0", "dp_1", "dp_2"), "dp_3"),
        0,
    )
    new_momentum = 0.9 * momentum + weight_grad
    new_weight = mlp_weight - 0.01 * new_momentum
    next_weight = gathered_by_axis(
        new_weight.astype(jnp.bfloat16), (("dp_0", "dp_1", "dp_2"), "dp_3"), 0
    )
    normed_part = lax.dot_general(
        preact_grad, weights_full, (((1,), (1,)), ((), ())), preferred_element_type=jnp.float32
    )
    width_in = normed_part.shape[1]
    stacked = normed_part.reshape(members, share, width_in)
    received = lax.all_to_all(
        stacked.astype(jnp.bfloat16), "mp", split_axis=0, concat_axis=0, tiled=True
    ).astype(stacked.dtype)
    normed_grad = jnp.sum(received, axis=0)
    proj_part = backward_features(embedded_share, normed, inv_scale, normed_grad, rank)
    proj_grad = over_axes(proj_part, DP_MP)
    lcb_weight_grad = by_axis(lcb_part, (("dp_0", "dp_1"), ("dp_2", "dp_3")))
    return (new_weight, new_momentum, next_weight, proj_grad, lcb_weight_grad)


def solution(mesh):
    torus = Mesh(
        mesh.devices.reshape(2, 8, 4, 2, mesh.shape["mp"]), ("dp_0", "dp_1", "dp_2", "dp_3", "mp")
    )
    placed = (
        P(DP, None),
        P(DP_MP, None),
        P(),
        P(DP, "mp"),
        P(DP, "mp"),
        P(DP, "mp"),
        P(DP, "mp", None),
    )
    return jax.shard_map(
        per_device,
        mesh=torus,
        in_specs=placed,
        out_specs=(P(DP, "mp"), P(DP, "mp"), P(None, "mp"), P(), P(None, "mp")),
        check_vma=False,
    )
```

profile of v0, /device:TPU:1, one launch (start us, length us, event | category | flops | bytes accessed | tf_op | source)
XLA Modules:
  0.0 414.9 jit_solution(17189130337260080682)
XLA Ops:
  0.6 0.0 copy-start
  0.6 1.4 broadcast_in_dim.47
  2.0 10.8 %all-to-all-start = ((bf16[4,16,128]{2,1,0:T(8,128)(2,1)}), bf16[4,16,128]{2,1,0:T(8,128)(2,1)S(1)}, u32[]{:S(2)}, u32[]{:S(2)}) async-start(bf16[4,16,128]{2,1,0:T(8,128)(2,1)} %broadcast_in_dim.47), calls=%async_computation | async-start | bytes 32768 | tf_op jit(solution)/shard_map/all_to_all | solution.py:15
  12.9 0.8 convert_element_type.43
  13.6 5.9 %all-to-all-done = bf16[4,16,128]{2,1,0:T(8,128)(2,1)S(1)} async-done(((bf16[4,16,128]{2,1,0:T(8,128)(2,1)}), bf16[4,16,128]{2,1,0:T(8,128)(2,1)S(1)}, u32[]{:S(2)}, u32[]{:S(2)}) %all-to-all-start) | async-done | bytes 16416 | tf_op jit(solution)/shard_map/all_to_all | solution.py:15
  19.5 0.1 broadcast_in_dim.53
  19.6 36.6 %all_to_all.65 = bf16[64,32,256]{2,1,0:T(8,128)(2,1)S(1)} all-to-all(bf16[64,32,256]{2,1,0:T(8,128)(2,1)S(1)} %broadcast_in_dim.53), channel_id=1, replica_groups=mesh['dp_0'=2,'dp_1'=8,'dp_2'=4,'dp_3'=2,'mp'=4] {'dp_0','dp_1','dp_2'}, dimensions={0} | all-to-all | bytes 2097152 | tf_op jit(solution)/shard_map/all_to_all | solution.py:15
  56.2 1.2 broadcast_in_dim.48
  57.5 7.7 %all-to-all-start.1 = ((bf16[64,64,128]{2,1,0:T(8,128)(2,1)}), bf16[64,64,128]{2,1,0:T(8,128)(2,1)S(1)}, u32[]{:S(2)}, u32[]{:S(2)}) async-start(bf16[64,64,128]{2,1,0:T(8,128)(2,1)} %broadcast_in_dim.48), calls=%async_computation.1 | async-start | bytes 2097152 | tf_op jit(solution)/shard_map/all_to_all | solution.py:15
  65.2 25.6 %all-to-all-done.1 = bf16[64,64,128]{2,1,0:T(8,128)(2,1)S(1)} async-done(((bf16[64,64,128]{2,1,0:T(8,128)(2,1)}), bf16[64,64,128]{2,1,0:T(8,128)(2,1)S(1)}, u32[]{:S(2)}, u32[]{:S(2)}) %all-to-all-start.1) | async-done | bytes 1048608 | tf_op jit(solution)/shard_map/all_to_all | solution.py:15
  90.8 0.5 broadcast_in_dim.49
  91.3 9.4 %all_to_all.66 = bf16[2,64,64,128]{3,2,1,0:T(8,128)(2,1)} all-to-all(bf16[2,64,64,128]{3,2,1,0:T(8,128)(2,1)S(1)} %broadcast_in_dim.49), channel_id=1, replica_groups=mesh['dp_0'=2,'dp_1'=8,'dp_2'=4,'dp_3'=2,'mp'=4] {'dp_3'}, dimensions={0} | all-to-all | bytes 4194304 | tf_op jit(solution)/shard_map/all_to_all | solution.py:15
  100.7 1.6 broadcast_in_dim.54
  102.3 5.3 %all-to-all-start.5 = ((bf16[2,64,32,256]{3,2,1,0:T(8,128)(2,1)}), bf16[2,64,32,256]{3,2,1,0:T(8,128)(2,1)}, u32[]{:S(2)}, u32[]{:S(2)}) async-start(bf16[2,64,32,256]{3,2,1,0:T(8,128)(2,1)} %broadcast_in_dim.54), calls=%async_computation.5 | async-start | bytes 4194304 | tf_op jit(solution)/shard_map/all_to_all | solution.py:15
  107.5 1.8 copy.20
  109.4 57.4 %gather_fusion = bf16[16384,128]{1,0:T(8,128)(2,1)} fusion(bf16[8192,128]{1,0:T(8,128)(2,1)S(1)} %bitcast.56, s32[16384]{0:T(1024)S(1)} %bitcast_clamp_fusion), kind=kCustom, calls=%fused_computation | custom fusion | bytes 8454144 | tf_op jit(solution)/shard_map/jit(_take)/gather | solution.py:114
  166.8 7.6 %broadcast_select_fusion = bf16[128,128,128]{2,1,0:T(8,128)(2,1)} fusion(bf16[128,128,128]{2,1,0:T(8,128)(2,1)} %bitcast.57, pred[128,128]{1,0:T(8,128)(4,1)S(1)} %compare_and_fusion), kind=kLoop, calls=%fused_computation.3 | loop fusion | flops 2097152 | bytes 8404992 | tf_op jit(solution)/shard_map/jit(_take)/select_n | solution.py:114
  174.4 2.5 fusion.23
  176.9 0.5 multiply_reduce_fusion
  177.4 3.6 convolution_bitcast_fusion
  181.0 0.0 all-to-all-done.5
  181.1 0.7 broadcast_in_dim.57
  181.7 5.0 %all-to-all-start.11 = ((f32[8,128,32]{1,2,0:T(8,128)}), f32[8,128,32]{1,2,0:T(8,128)S(1)}, u32[]{:S(2)}, u32[]{:S(2)}) async-start(f32[8,128,32]{1,2,0:T(8,128)} %broadcast_in_dim.57), calls=%async_computation.11 | async-start | bytes 262144 | tf_op jit(solution)/shard_map/all_to_all | solution.py:15
  186.7 0.3 fusion.12
  187.0 4.9 %all-to-all-done.11 = f32[8,128,32]{1,2,0:T(8,128)S(1)} async-done(((f32[8,128,32]{1,2,0:T(8,128)}), f32[8,128,32]{1,2,0:T(8,128)S(1)}, u32[]{:S(2)}, u32[]{:S(2)}) %all-to-all-start.11) | async-done | bytes 131104 | tf_op jit(solution)/shard_map/all_to_all | solution.py:15
  191.9 1.1 broadcast_in_dim.52
  193.0 3.5 all-to-all-start.3
  196.5 0.0 copy-start.5
  196.6 3.2 copy.21
  199.8 22.4 %all-to-all-done.3 = bf16[4,32,4096]{2,1,0:T(8,128)(2,1)S(1)} async-done(((bf16[4,32,4096]{2,1,0:T(8,128)(2,1)}), bf16[4,32,4096]{2,1,0:T(8,128)(2,1)S(1)}, u32[]{:S(2)}, u32[]{:S(2)}) %all-to-all-start.3) | async-done | bytes 1048608 | tf_op jit(solution)/shard_map/all_to_all | solution.py:15
  222.2 2.1 multiply_convert_fusion
  224.2 0.8 convolution_convert_fusion
  225.0 0.2 copy.28
  225.2 6.4 %all_to_all.67 = bf16[2,64,32,256]{3,2,1,0:T(8,128)(2,1)} all-to-all(bf16[2,64,32,256]{3,2,1,0:T(8,128)(2,1)S(1)} %bitcast.63), channel_id=1, replica_groups=mesh['dp_0'=2,'dp_1'=8,'dp_2'=4,'dp_3'=2,'mp'=4] {'dp_3'}, dimensions={0} | all-to-all | bytes 4194304 | tf_op jit(solution)/shard_map/all_to_all | solution.py:44
  231.6 0.7 broadcast_in_dim.58
  232.4 6.1 %all-to-all-start.12 = ((f32[16,128,32]{1,2,0:T(8,128)}), f32[16,128,32]{1,2,0:T(8,128)S(1)}, u32[]{:S(2)}, u32[]{:S(2)}) async-start(f32[16,128,32]{1,2,0:T(8,128)} %broadcast_in_dim.58), calls=%async_computation.12 | async-start | bytes 524288 | tf_op jit(solution)/shard_map/all_to_all | solution.py:15
  238.4 3.4 reduce_sum.88
  241.8 5.6 %all-to-all-done.12 = f32[16,128,32]{1,2,0:T(8,128)S(1)} async-done(((f32[16,128,32]{1,2,0:T(8,128)}), f32[16,128,32]{1,2,0:T(8,128)S(1)}, u32[]{:S(2)}, u32[]{:S(2)}) %all-to-all-start.12) | async-done | bytes 262176 | tf_op jit(solution)/shard_map/all_to_all | solution.py:15
  247.4 6.9 %all-to-all-start.7 = ((bf16[64,32,256]{2,1,0:T(8,128)(2,1)}), bf16[64,32,256]{2,1,0:T(8,128)(2,1)S(1)}, u32[]{:S(2)}, u32[]{:S(2)}) async-start(bf16[64,32,256]{2,1,0:T(8,128)(2,1)} %reduce_sum.88), calls=%async_computation.7 | async-start | bytes 2097152 | tf_op jit(solution)/shard_map/all_to_all | solution.py:52
  254.3 3.4 convolution_convert_fusion.1
  257.7 23.4 %all-to-all-done.7 = bf16[64,32,256]{2,1,0:T(8,128)(2,1)S(1)} async-done(((bf16[64,32,256]{2,1,0:T(8,128)(2,1)}), bf16[64,32,256]{2,1,0:T(8,128)(2,1)S(1)}, u32[]{:S(2)}, u32[]{:S(2)}) %all-to-all-start.7) | async-done | bytes 1048608 | tf_op jit(solution)/shard_map/all_to_all | solution.py:52
  281.1 1.0 copy-done.2
  282.1 3.5 all-to-all-start.10
  285.6 1.4 convert_reduce_fusion.2
  287.0 0.6 fusion.22
  287.6 23.9 %all-to-all-done.10 = bf16[4,32,4096]{2,1,0:T(8,128)(2,1)S(1)} async-done(((bf16[4,32,4096]{2,1,0:T(8,128)(2,1)}), bf16[4,32,4096]{2,1,0:T(8,128)(2,1)S(1)}, u32[]{:S(2)}, u32[]{:S(2)}) %all-to-all-start.10) | async-done | bytes 1048608 | tf_op jit(solution)/shard_map/all_to_all | solution.py:151
  311.5 1.2 broadcast_in_dim.55
  312.7 0.1 copy-done.1
  312.8 8.0 %all-to-all-start.8 = ((bf16[64,32,256]{2,1,0:T(8,128)(2,1)}), bf16[64,32,256]{2,1,0:T(8,128)(2,1)S(1)}, u32[]{:S(2)}, u32[]{:S(2)}) async-start(bf16[64,32,256]{2,1,0:T(8,128)(2,1)} %broadcast_in_dim.55), calls=%async_computation.8 | async-start | bytes 2097152 | tf_op jit(solution)/shard_map/all_to_all | solution.py:15
  320.9 0.6 reduce_sum.95
  321.5 1.6 convert_reduce_fusion
  323.1 0.1 copy.25
  323.2 0.5 fusion.10
  323.7 0.2 fusion.9
  324.0 2.3 fusion.2
  326.2 6.5 %psum.35 = f32[128,32]{0,1:T(8,128)S(1)} all-reduce(f32[128,32]{0,1:T(8,128)S(1)} %fusion.2), channel_id=1, replica_groups=mesh['dp_0'=2,'dp_1'=8,'dp_2'=4,'dp_3'=2,'mp'=4] {'dp_0'}, use_global_device_ids=true, to_apply=%region_7.8 | all-reduce | flops 4096 | bytes 32768 | tf_op jit(solution)/shard_map/psum | solution.py:57
  332.7 28.6 %psum.36 = f32[128,32]{0,1:T(8,128)S(1)} all-reduce(f32[128,32]{0,1:T(8,128)S(1)} %psum.35), channel_id=1, replica_groups=mesh['dp_0'=2,'dp_1'=8,'dp_2'=4,'dp_3'=2,'mp'=4] {'dp_1'}, use_global_device_ids=true, to_apply=%region_8.9 | all-reduce | flops 4096 | bytes 32768 | tf_op jit(solution)/shard_map/psum | solution.py:57
  361.3 12.9 %psum.37 = f32[128,32]{0,1:T(8,128)S(1)} all-reduce(f32[128,32]{0,1:T(8,128)S(1)} %psum.36), channel_id=1, replica_groups=mesh['dp_0'=2,'dp_1'=8,'dp_2'=4,'dp_3'=2,'mp'=4] {'dp_2'}, use_global_device_ids=true, to_apply=%region_9.10 | all-reduce | flops 4096 | bytes 32768 | tf_op jit(solution)/shard_map/psum | solution.py:57
  374.2 14.7 %psum.38 = f32[128,32]{0,1:T(8,128)S(1)} all-reduce(f32[128,32]{0,1:T(8,128)S(1)} %psum.37), channel_id=1, replica_groups=mesh['dp_0'=2,'dp_1'=8,'dp_2'=4,'dp_3'=2,'mp'=4] {'dp_3'}, use_global_device_ids=true, to_apply=%region_10.11 | all-reduce | flops 4096 | bytes 32768 | tf_op jit(solution)/shard_map/psum | solution.py:57
  388.9 15.2 %psum.39 = f32[128,32]{0,1:T(8,128)} all-reduce(f32[128,32]{0,1:T(8,128)S(1)} %psum.38), channel_id=1, replica_groups=mesh['dp_0'=2,'dp_1'=8,'dp_2'=4,'dp_3'=2,'mp'=4] {'mp'}, use_global_device_ids=true, to_apply=%region_11.12 | all-reduce | flops 4096 | bytes 32768 | tf_op jit(solution)/shard_map/psum | solution.py:57
  404.2 0.0 all-to-all-done.8
  404.2 0.2 broadcast_in_dim.56
  404.4 9.0 %all_to_all.68 = bf16[2,64,32,256]{3,2,1,0:T(8,128)(2,1)S(1)} all-to-all(bf16[2,64,32,256]{3,2,1,0:T(8,128)(2,1)S(1)} %broadcast_in_dim.56), channel_id=1, replica_groups=mesh['dp_0'=2,'dp_1'=8,'dp_2'=4,'dp_3'=2,'mp'=4] {'dp_3'}, dimensions={0} | all-to-all | bytes 4194304 | tf_op jit(solution)/shard_map/all_to_all | solution.py:15
  413.4 1.5 copy.23
  (18 shorter events, 0.1 us)
Async XLA Ops:
  0.6 176.8 %copy-start = (bf16[128,32,128]{2,1,0:T(8,128)(2,1)S(1)}, bf16[128,32,128]{2,1,0:T(8,128)(2,1)}, u32[]{:S(2)}) copy-start(bf16[128,32,128]{2,1,0:T(8,128)(2,1)} %param.13) | copy-start | bytes 3145732
  2.0 17.5 %all-to-all-start = ((bf16[4,16,128]{2,1,0:T(8,128)(2,1)}), bf16[4,16,128]{2,1,0:T(8,128)(2,1)S(1)}, u32[]{:S(2)}, u32[]{:S(2)}) async-start(bf16[4,16,128]{2,1,0:T(8,128)(2,1)} %broadcast_in_dim.47), calls=%async_computation | async-start | bytes 32768 | tf_op jit(solution)/shard_map/all_to_all | solution.py:15
  56.2 8.9 %copy-start.3 = (s32[128,128]{1,0:T(8,128)S(1)}, s32[128,128]{1,0:T(8,128)}, u32[]{:S(2)}) copy-start(s32[128,128]{1,0:T(8,128)} %param.7) | copy-start | bytes 196612
  57.5 33.3 %all-to-all-start.1 = ((bf16[64,64,128]{2,1,0:T(8,128)(2,1)}), bf16[64,64,128]{2,1,0:T(8,128)(2,1)S(1)}, u32[]{:S(2)}, u32[]{:S(2)}) async-start(bf16[64,64,128]{2,1,0:T(8,128)(2,1)} %broadcast_in_dim.48), calls=%async_computation.1 | async-start | bytes 2097152 | tf_op jit(solution)/shard_map/all_to_all | solution.py:15
  102.3 78.8 %all-to-all-start.5 = ((bf16[2,64,32,256]{3,2,1,0:T(8,128)(2,1)}), bf16[2,64,32,256]{3,2,1,0:T(8,128)(2,1)}, u32[]{:S(2)}, u32[]{:S(2)}) async-start(bf16[2,64,32,256]{3,2,1,0:T(8,128)(2,1)} %broadcast_in_dim.54), calls=%async_computation.5 | async-start | bytes 4194304 | tf_op jit(solution)/shard_map/all_to_all | solution.py:15
  166.8 7.7 %copy-start.7 = (bf16[128,32]{0,1:T(8,128)(2,1)S(1)}, bf16[128,32]{0,1:T(8,128)(2,1)}, u32[]{:S(2)}) copy-start(bf16[128,32]{0,1:T(8,128)(2,1)} %param.9) | copy-start | bytes 24580
  181.7 10.2 %all-to-all-start.11 = ((f32[8,128,32]{1,2,0:T(8,128)}), f32[8,128,32]{1,2,0:T(8,128)S(1)}, u32[]{:S(2)}, u32[]{:S(2)}) async-start(f32[8,128,32]{1,2,0:T(8,128)} %broadcast_in_dim.57), calls=%async_computation.11 | async-start | bytes 262144 | tf_op jit(solution)/shard_map/all_to_all | solution.py:15
  193.0 29.1 %all-to-all-start.3 = ((bf16[4,32,4096]{2,1,0:T(8,128)(2,1)}), bf16[4,32,4096]{2,1,0:T(8,128)(2,1)S(1)}, u32[]{:S(2)}, u32[]{:S(2)}) async-start(bf16[4,32,4096]{2,1,0:T(8,128)(2,1)} %broadcast_in_dim.52), calls=%async_computation.3 | async-start | bytes 2097152 | tf_op jit(solution)/shard_map/all_to_all | solution.py:15
  196.5 25.6 %copy-start.5 = (bf16[128,256]{1,0:T(8,128)(2,1)S(1)}, bf16[128,256]{1,0:T(8,128)(2,1)}, u32[]{:S(2)}) copy-start(bf16[128,256]{1,0:T(8,128)(2,1)} %param.12) | copy-start | bytes 196612
  232.4 15.0 %all-to-all-start.12 = ((f32[16,128,32]{1,2,0:T(8,128)}), f32[16,128,32]{1,2,0:T(8,128)S(1)}, u32[]{:S(2)}, u32[]{:S(2)}) async-start(f32[16,128,32]{1,2,0:T(8,128)} %broadcast_in_dim.58), calls=%async_computation.12 | async-start | bytes 524288 | tf_op jit(solution)/shard_map/all_to_all | solution.py:15
  247.4 33.7 %all-to-all-start.7 = ((bf16[64,32,256]{2,1,0:T(8,128)(2,1)}), bf16[64,32,256]{2,1,0:T(8,128)(2,1)S(1)}, u32[]{:S(2)}, u32[]{:S(2)}) async-start(bf16[64,32,256]{2,1,0:T(8,128)(2,1)} %reduce_sum.88), calls=%async_computation.7 | async-start | bytes 2097152 | tf_op jit(solution)/shard_map/all_to_all | solution.py:52
  257.7 29.3 %copy-start.4 = (f32[32,256]{1,0:T(8,128)S(1)}, f32[32,256]{1,0:T(8,128)}, u32[]{:S(2)}) copy-start(f32[32,256]{1,0:T(8,128)} %param.10) | copy-start | bytes 98308
  257.7 29.3 %copy-start.6 = (f32[32,256]{1,0:T(8,128)S(1)}, f32[32,256]{1,0:T(8,128)}, u32[]{:S(2)}) copy-start(f32[32,256]{1,0:T(8,128)} %param.11) | copy-start | bytes 98308
  281.1 1.0 copy-start.2
  282.1 29.5 %all-to-all-start.10 = ((bf16[4,32,4096]{2,1,0:T(8,128)(2,1)}), bf16[4,32,4096]{2,1,0:T(8,128)(2,1)S(1)}, u32[]{:S(2)}, u32[]{:S(2)}) async-start(bf16[4,32,4096]{2,1,0:T(8,128)(2,1)} %convolution_convert_fusion.1), calls=%async_computation.10 | async-start | bytes 2097152 | tf_op jit(solution)/shard_map/all_to_all | solution.py:151
  311.5 1.3 copy-start.1
  312.8 91.3 %all-to-all-start.8 = ((bf16[64,32,256]{2,1,0:T(8,128)(2,1)}), bf16[64,32,256]{2,1,0:T(8,128)(2,1)S(1)}, u32[]{:S(2)}, u32[]{:S(2)}) async-start(bf16[64,32,256]{2,1,0:T(8,128)(2,1)} %broadcast_in_dim.55), calls=%async_computation.8 | async-start | bytes 2097152 | tf_op jit(solution)/shard_map/all_to_all | solution.py:15
where the time goes:
time: 417 us; the launch traced here: 415 us
  blocking collectives  139 us (33%)
  waiting for transfers between devices  112 us (27%)
  local copies, waits for them, and re-layouts  74 us (18%)
  starting transfers between devices  56.8 us (14%)
  other arithmetic  17.7 us (4%)
  matrix products  14.6 us (4%)
    psum x5, blocking collectives, over_axes(): return functools.reduce(lax.psum, axes, x)  77.9 us
    all_to_all x7, waiting for transfers between devices, from_everyone(): return lax.all_to_all(copies, axis, split_axis=0, concat_axis=0, tiled=True)  64.4 us
    gather x1, local copies, waits for them, and re-layouts, per_device(): embedded_rows = jnp.take(table_full, feature_ids, axis=0)  57.4 us
    all_to_all x3, blocking collectives, from_everyone(): return lax.all_to_all(copies, axis, split_axis=0, concat_axis=0, tiled=True)  55 us
    all_to_all x7, starting transfers between devices, from_everyone(): return lax.all_to_all(copies, axis, split_axis=0, concat_axis=0, tiled=True)  46.3 us
    all_to_all x1, waiting for transfers between devices, per_device(): lax.all_to_all(stacked.astype(jnp.bfloat16), 'mp', split_axis=0, concat_a...  23.9 us
    all_to_all x1, waiting for transfers between devices, sum_by_axis(): lax.all_to_all(own.astype(jnp.bfloat16), far, 0, 0, tiled=True)  23.4 us
    broadcast_in_dim x10, local copies, waits for them, and re-layouts, from_everyone(): copies = jnp.broadcast_to(x, (lax.axis_size(axis), *x.shape))  8.74 us
  transfers between devices with their start and end apart: 9, of which 7 were waited for; matrix products, arithmetic and copies ran while one was open for 22% of the time, Pallas kernels for 0%

commit v1 on v0

v1 whole, which is shorter than its diff:
```python
import jax
import jax.numpy as jnp
from jax import lax
from jax.experimental import pallas as pl
from jax.experimental.pallas import tpu as pltpu
from jax.sharding import Mesh
from jax.sharding import PartitionSpec as P

DP = ("zl", "y", "x", "c")
DP_MP = ("zl", "y", "x", "c", "mp")
GROUP = 8


def exchange(tiles, axis):
    return lax.all_to_all(tiles, axis, split_axis=0, concat_axis=0, tiled=True)


def from_everyone(x, axis):
    return exchange(jnp.broadcast_to(x, (lax.axis_size(axis), *x.shape)), axis)


def summed(tiles):
    return tiles.astype(jnp.float32).sum(axis=0)


def forward_kernel(ids_ref, table_ref, proj_ref, emb_ref, normed_ref, inv_ref, even_ref, odd_ref, fm_ref):
    rank, n_emb = proj_ref.shape
    proj = proj_ref[...]
    for e in range(GROUP):
        rows_ref = (even_ref, odd_ref)[e % 2]
        for r in range(n_emb):
            rows_ref[pl.ds(r, 1), :] = table_ref[ids_ref[e, r]]
        emb = rows_ref[...].astype(jnp.bfloat16)
        emb_ref[e] = emb
        compressed = jnp.dot(proj, emb, preferred_element_type=jnp.float32).astype(jnp.bfloat16)
        fm_ref[pl.ds(e * rank, rank), :] = lax.dot_general(
            compressed, emb, (((1,), (1,)), ((), ())), preferred_element_type=jnp.float32
        )
    scale = 1.0 / (rank * n_emb)
    parts = [fm_ref[pl.ds(k, GROUP, stride=rank), :] for k in range(rank)]
    mean = jnp.sum(sum(parts), axis=1, keepdims=True) * scale
    parts = [p - mean for p in parts]
    var = jnp.sum(sum(p * p for p in parts), axis=1, keepdims=True) * scale
    inv = 1.0 / jnp.sqrt(var + 1.0)
    for k in range(rank):
        normed_ref[:, k * n_emb : (k + 1) * n_emb] = (parts[k] * inv).astype(jnp.bfloat16)
    inv_ref[...] = jnp.broadcast_to(inv, inv_ref.shape)


def forward_features(ids, table, projection):
    examples, n_emb = ids.shape
    vocab, width = table.shape
    rank = projection.shape[1]
    rows = table.astype(jnp.float32).reshape(vocab, 1, width)
    return pl.pallas_call(
        forward_kernel,
        grid=(examples // GROUP,),
        in_specs=[
            pl.BlockSpec((GROUP, n_emb), lambda g: (g, 0), memory_space=pltpu.SMEM),
            pl.BlockSpec((vocab, 1, width), lambda g: (0, 0, 0)),
            pl.BlockSpec((rank, n_emb), lambda g: (0, 0)),
        ],
        out_specs=[
            pl.BlockSpec((GROUP, n_emb, width), lambda g: (g, 0, 0)),
            pl.BlockSpec((GROUP, rank * n_emb), lambda g: (g, 0)),
            pl.BlockSpec((GROUP, 128), lambda g: (g, 0)),
        ],
        out_shape=[
            jax.ShapeDtypeStruct((examples, n_emb, width), jnp.bfloat16),
            jax.ShapeDtypeStruct((examples, rank * n_emb), jnp.bfloat16),
            jax.ShapeDtypeStruct((examples, 128), jnp.float32),
        ],
        scratch_shapes=[
            pltpu.VMEM((n_emb, width), jnp.float32),
            pltpu.VMEM((n_emb, width), jnp.float32),
            pltpu.VMEM((GROUP * rank, n_emb), jnp.float32),
        ],
        cost_estimate=pl.CostEstimate(
            flops=64 * examples * rank * n_emb * width,
            bytes_accessed=vocab * width * 4 + examples * n_emb * width * 2,
            transcendentals=0,
        ),
        name="fm_forward",
    )(ids, rows, projection.T)


def backward_kernel(grad_ref, normed_ref, inv_ref, emb_ref, out_ref, fm_grad_ref):
    n_emb = emb_ref.shape[1]
    rank = out_ref.shape[0]

    @pl.when(pl.program_id(0) == 0)
    def _():
        out_ref[...] = jnp.zeros_like(out_ref)

    def cut(ref, k):
        return ref[:, k * n_emb : (k + 1) * n_emb].astype(jnp.float32)

    scale = 1.0 / (rank * n_emb)
    grads = [cut(grad_ref, k) for k in range(rank)]
    normed = [cut(normed_ref, k) for k in range(rank)]
    mean = jnp.sum(sum(grads), axis=1, keepdims=True) * scale
    along = jnp.sum(sum(g * x for g, x in zip(grads, normed)), axis=1, keepdims=True) * scale
    inv = inv_ref[:, :1]
    for k in range(rank):
        fm_grad_ref[pl.ds(k, GROUP, stride=rank), :] = (grads[k] - mean - normed[k] * along) * inv
    total = jnp.zeros(out_ref.shape, jnp.float32)
    for e in range(GROUP):
        fm_grad = fm_grad_ref[pl.ds(e * rank, rank), :].astype(jnp.bfloat16)
        emb = emb_ref[e]
        back = jnp.dot(fm_grad, emb, preferred_element_type=jnp.float32).astype(jnp.bfloat16)
        total += lax.dot_general(back, emb, (((1,), (1,)), ((), ())), preferred_element_type=jnp.float32)
    out_ref[...] += total


def backward_features(normed_grad, normed, inv_scale, embedded, rank):
    examples, n_emb, width = embedded.shape
    return pl.pallas_call(
        backward_kernel,
        grid=(examples // GROUP,),
        in_specs=[
            pl.BlockSpec((GROUP, rank * n_emb), lambda g: (g, 0)),
            pl.BlockSpec((GROUP, rank * n_emb), lambda g: (g, 0)),
            pl.BlockSpec((GROUP, 128), lambda g: (g, 0)),
            pl.BlockSpec((GROUP, n_emb, width), lambda g: (g, 0, 0)),
        ],
        out_specs=pl.BlockSpec((rank, n_emb), lambda g: (0, 0)),
        out_shape=jax.ShapeDtypeStruct((rank, n_emb), jnp.float32),
        scratch_shapes=[pltpu.VMEM((GROUP * rank, n_emb), jnp.float32)],
        cost_estimate=pl.CostEstimate(
            flops=24 * examples * rank * n_emb * width,
            bytes_accessed=examples * n_emb * (width * 2 + rank * 6),
            transcendentals=0,
        ),
        name="fm_backward",
    )(normed_grad, normed, inv_scale, embedded)


def rows_from_group(rows):
    return from_everyone(from_everyone(from_everyone(rows, ("zl", "y")), "x"), "c")


def in_row_order(tiles):
    c, x, zy, rows, width = tiles.shape
    return jnp.transpose(tiles, (2, 1, 0, 3, 4)).reshape(zy * x * c * rows, width)


def sum_at_row_owner(part):
    x, c, zy = lax.axis_size("x"), lax.axis_size("c"), lax.axis_size(("zl", "y"))
    width = part.shape[1]
    tiles = jnp.transpose(part.reshape(zy, x, c, -1, width), (2, 1, 0, 3, 4))
    tiles = summed(exchange(tiles, "c")).astype(jnp.bfloat16)
    tiles = summed(exchange(tiles, "x")).astype(jnp.bfloat16)
    return summed(exchange(tiles, ("zl", "y")))


def per_device(feature_ids, emb_table, factor_machine_projection, mlp_weight, momentum, hidden_grad, lcb_grad):
    mp, zl, y, x, c = (lax.axis_size(a) for a in ("mp", "zl", "y", "x", "c"))
    own = emb_table.shape[0]
    rank = factor_machine_projection.shape[1]

    table = from_everyone(from_everyone(from_everyone(emb_table, ("mp", "zl", "y")), "x"), "c")
    table = table.reshape(-1, emb_table.shape[1])
    owner, row = feature_ids // own, feature_ids % own
    owner, at_mp = owner // mp, owner % mp
    owner, at_c = owner // c, owner % c
    at_zy, at_x = owner // x, owner % x
    ids = (((at_c * x + at_x) * mp + at_mp) * (zl * y) + at_zy) * own + row

    weights = in_row_order(rows_from_group(mlp_weight.astype(jnp.bfloat16)))
    embedded, normed, inv_scale = forward_features(ids, table, factor_machine_projection)
    preact = jnp.dot(normed, weights, preferred_element_type=jnp.float32)
    sigmoid_pre = jax.nn.sigmoid(preact)
    preact_grad = (
        hidden_grad.astype(jnp.float32) * sigmoid_pre * (1.0 + preact * (1.0 - sigmoid_pre))
    ).astype(jnp.bfloat16)
    weight_grad = sum_at_row_owner(
        lax.dot_general(
            normed, preact_grad, (((0,), (0,)), ((), ())), preferred_element_type=jnp.float32
        ).astype(jnp.bfloat16)
    )
    new_momentum = 0.9 * momentum + weight_grad
    new_weight = mlp_weight - 0.01 * new_momentum
    next_weight = in_row_order(rows_from_group(new_weight.astype(jnp.bfloat16)))

    normed_part = lax.dot_general(
        preact_grad, weights, (((1,), (1,)), ((), ())), preferred_element_type=jnp.float32
    )
    proj_part = backward_features(normed_part, normed, inv_scale, embedded, rank)
    lcb_part = jnp.einsum("bld,bnd->ln", lcb_grad, embedded, preferred_element_type=jnp.float32)
    n_emb = lcb_part.shape[1]
    both = jnp.concatenate(
        [proj_part.reshape(x * c, -1, n_emb), lcb_part.reshape(x * c, -1, n_emb)], axis=1
    )
    each = rank // (x * c)
    both = summed(exchange(both, ("x", "c")))
    both = summed(from_everyone(both, ("zl", "y")))
    proj_sum = summed(from_everyone(both[:each], "mp"))
    both = from_everyone(jnp.concatenate([proj_sum, both[each:]], axis=0), ("x", "c"))
    proj_grad = both[:, :each].reshape(-1, n_emb).T
    lcb_weight_grad = both[:, each:].reshape(-1, n_emb).T
    return (new_weight, new_momentum, next_weight, proj_grad, lcb_weight_grad)


def solution(mesh):
    torus = Mesh(mesh.devices.reshape(2, 8, 4, 2, mesh.shape["mp"]), DP_MP)
    placed = (
        P(DP, None),
        P(DP_MP, None),
        P(),
        P(DP, "mp"),
        P(DP, "mp"),
        P(DP, "mp"),
        P(DP, "mp", None),
    )
    return jax.shard_map(
        per_device,
        mesh=torus,
        in_specs=placed,
        out_specs=(P(DP, "mp"), P(DP, "mp"), P(None, "mp"), P(), P(None, "mp")),
        check_vma=False,
    )
```

time: 417 us -> 279 us (0.67)
  blocking collectives: 139 us -> 71.7 us
  local copies, waits for them, and re-layouts: 74 us -> 15.7 us
  Pallas kernels: 0 us -> 45.2 us
  waiting for transfers between devices: 112 us -> 76 us
  other arithmetic: 17.7 us -> 8.79 us
  matrix products: 14.6 us -> 6.02 us
  starting transfers between devices: 56.8 us -> 52.6 us
    psum x5 -> x0, blocking collectives: 77.9 us -> none  [over_axes(): return functools.reduce(lax.psum, axes, x)]
    gather x1 -> x0, local copies, waits for them, and re-layouts: 57.4 us -> none  [per_device(): embedded_rows = jnp.take(table_full, feature_ids, axis=0)]
    pallas_call x0 -> x2, Pallas kernels: none -> 45.2 us  [the longest x1 28.8 us: forward_features(): pl.pallas_call(forward_kernel, grid=(examples // GROUP,), in_specs=[pl.Bl...]
    all_to_all x9 -> x10, waiting for transfers between devices: 112 us -> 76 us  [exchange(): return lax.all_to_all(tiles, axis, split_axis=0, concat_axis=0, tiled=True)]
    all_to_all x4 -> x6, blocking collectives: 61.4 us -> 71.7 us  [exchange(): return lax.all_to_all(tiles, axis, split_axis=0, concat_axis=0, tiled=True)]
    dot_general x6 -> x4, matrix products: 14.6 us -> 6.02 us  [the longest x1 2.13 us: per_device(): lax.dot_general(preact_grad, weights, (((1,), (1,)), ((), ())), preferred...]
    select_n x1 -> x0, other arithmetic: 7.65 us -> none  [per_device(): embedded_rows = jnp.take(table_full, feature_ids, axis=0)]
    reduce_sum x7 -> x6, other arithmetic: 8.04 us -> 2.75 us  [summed(): return tiles.astype(jnp.float32).sum(axis=0)]
  transfers between devices with their start and end apart: 9 -> 10, of which waited for: 7 -> 10; matrix products, arithmetic and copies ran while one was open for 22% -> 4% of each run, Pallas kernels for 0% -> 0%
where the time goes in v1:
time: 279 us; the launch traced here: 277 us
  waiting for transfers between devices  76 us (27%)
  blocking collectives  71.7 us (26%)
  starting transfers between devices  52.6 us (19%)
  Pallas kernels  45.2 us (16%)
  local copies, waits for them, and re-layouts  15.7 us (6%)
  other arithmetic  8.79 us (3%)
  matrix products  6.02 us (2%)
    all_to_all x10, waiting for transfers between devices, exchange(): return lax.all_to_all(tiles, axis, split_axis=0, concat_axis=0, tiled=True)  76 us
    all_to_all x6, blocking collectives, exchange(): return lax.all_to_all(tiles, axis, split_axis=0, concat_axis=0, tiled=True)  71.7 us
    all_to_all x10, starting transfers between devices, exchange(): return lax.all_to_all(tiles, axis, split_axis=0, concat_axis=0, tiled=True)  52.6 us
    pallas_call x1, Pallas kernels, forward_features(): pl.pallas_call(forward_kernel, grid=(examples // GROUP,), in_specs=[pl.Bl...  28.8 us
    pallas_call x1, Pallas kernels, backward_features(): pl.pallas_call(backward_kernel, grid=(examples // GROUP,), in_specs=[pl.B...  16.3 us
    broadcast_in_dim x12, local copies, waits for them, and re-layouts, from_everyone(): return exchange(jnp.broadcast_to(x, (lax.axis_size(axis), *x.shape)), axis)  6.98 us
  transfers between devices with their start and end apart: 10, of which 10 were waited for; matrix products, arithmetic and copies ran while one was open for 4% of the time, Pallas kernels for 0%

profile of v1, /device:TPU:1, one launch (start us, length us, event | category | flops | bytes accessed | tf_op | source)
XLA Modules:
  0.0 276.9 jit_solution(9176707125069548759)
XLA Ops:
  0.6 0.0 copy-start
  0.6 0.9 convert_element_type.38
  1.5 18.1 %all_to_all.80 = bf16[16,32,256]{2,1,0:T(8,128)(2,1)S(1)} all-to-all(bf16[16,32,256]{2,1,0:T(8,128)(2,1)S(1)} %broadcast_in_dim.39), channel_id=1, replica_groups=mesh['zl'=2,'y'=8,'x'=4,'c'=2,'mp'=4] {'zl','y'}, dimensions={0} | all-to-all | bytes 524288 | tf_op jit(solution)/shard_map/all_to_all | solution.py:15
  19.7 0.1 broadcast_in_dim.40
  19.8 16.4 %all_to_all.81 = bf16[4,16,32,256]{3,2,1,0:T(8,128)(2,1)S(1)} all-to-all(bf16[4,16,32,256]{3,2,1,0:T(8,128)(2,1)S(1)} %broadcast_in_dim.40), channel_id=1, replica_groups=mesh['zl'=2,'y'=8,'x'=4,'c'=2,'mp'=4] {'x'}, dimensions={0} | all-to-all | bytes 2097152 | tf_op jit(solution)/shard_map/all_to_all | solution.py:15
  36.2 0.0 copy-done.7
  36.2 0.7 broadcast_in_dim.36
  36.9 14.0 %all-to-all-start = ((bf16[64,16,128]{2,1,0:T(8,128)(2,1)}), bf16[64,16,128]{2,1,0:T(8,128)(2,1)S(1)}, u32[]{:S(2)}, u32[]{:S(2)}) async-start(bf16[64,16,128]{2,1,0:T(8,128)(2,1)} %broadcast_in_dim.36), calls=%async_computation | async-start | bytes 524288 | tf_op jit(solution)/shard_map/all_to_all | solution.py:15
  50.9 0.1 copy.30
  51.0 12.5 %all-to-all-done = bf16[64,16,128]{2,1,0:T(8,128)(2,1)S(1)} async-done(((bf16[64,16,128]{2,1,0:T(8,128)(2,1)}), bf16[64,16,128]{2,1,0:T(8,128)(2,1)S(1)}, u32[]{:S(2)}, u32[]{:S(2)}) %all-to-all-start) | async-done | bytes 262176 | tf_op jit(solution)/shard_map/all_to_all | solution.py:15
  63.5 0.3 broadcast_in_dim.41
  63.8 9.9 %all_to_all.82 = bf16[2,4,16,32,256]{4,3,1,2,0:T(8,128)(2,1)} all-to-all(bf16[2,4,16,32,256]{4,3,1,2,0:T(8,128)(2,1)S(1)} %broadcast_in_dim.41), channel_id=1, replica_groups=mesh['zl'=2,'y'=8,'x'=4,'c'=2,'mp'=4] {'c'}, dimensions={0} | all-to-all | bytes 4194304 | tf_op jit(solution)/shard_map/all_to_all | solution.py:15
  73.7 1.1 broadcast_in_dim.37
  74.8 4.3 %all-to-all-start.1 = ((bf16[4,64,16,128]{3,2,1,0:T(8,128)(2,1)}), bf16[4,64,16,128]{3,2,1,0:T(8,128)(2,1)}, u32[]{:S(2)}, u32[]{:S(2)}) async-start(bf16[4,64,16,128]{3,2,1,0:T(8,128)(2,1)} %broadcast_in_dim.37), calls=%async_computation.1 | async-start | bytes 2097152 | tf_op jit(solution)/shard_map/all_to_all | solution.py:15
  79.1 0.0 copy-done.5
  79.1 0.9 fusion.10.ids_ref
  80.0 1.8 copy.31
  81.8 12.1 %all-to-all-done.1 = bf16[4,64,16,128]{3,2,1,0:T(8,128)(2,1)} async-done(((bf16[4,64,16,128]{3,2,1,0:T(8,128)(2,1)}), bf16[4,64,16,128]{3,2,1,0:T(8,128)(2,1)}, u32[]{:S(2)}, u32[]{:S(2)}) %all-to-all-start.1) | async-done | bytes 1048608 | tf_op jit(solution)/shard_map/all_to_all | solution.py:15
  94.0 1.5 broadcast_in_dim.38
  95.5 6.3 %all_to_all.83 = bf16[2,4,64,16,128]{4,3,2,1,0:T(8,128)(2,1)S(1)} all-to-all(bf16[2,4,64,16,128]{4,3,2,1,0:T(8,128)(2,1)S(1)} %broadcast_in_dim.38), channel_id=1, replica_groups=mesh['zl'=2,'y'=8,'x'=4,'c'=2,'mp'=4] {'c'}, dimensions={0} | all-to-all | bytes 4194304 | tf_op jit(solution)/shard_map/all_to_all | solution.py:15
  101.8 2.3 convert_element_type.43
  104.1 28.8 %fm_forward.1 = (bf16[128,128,128]{2,1,0:T(8,128)(2,1)}, bf16[128,4096]{1,0:T(8,128)(2,1)}, f32[128,128]{1,0:T(8,128)}) custom-call(s32[128,128]{1,0:T(8,128)} %fusion.10.ids_ref, f32[8192,1,128]{2,1,0:T(1,128)} %bitcast.34, bf16[32,128]{1,0:T(8,128)(2,1)} %bitcast.40), custom_call_target="tpu_custom_call" | custom-call | flops 4294967296 | bytes 8388608 | tf_op jit(solution)/shard_map/fm_forward/pallas_call | solution.py:55
  132.9 1.7 fusion.26
  134.6 0.0 copy-done.3
  134.6 0.0 copy-start.1
  134.7 2.1 fusion.grad_ref
  136.8 0.0 copy-done
  136.8 0.8 copy-done.1
  137.6 1.4 fusion.27
  139.0 16.3 %fm_backward.1 = f32[32,128]{1,0:T(8,128)} custom-call(f32[128,4096]{1,0:T(8,128)} %fusion.grad_ref, bf16[128,4096]{1,0:T(8,128)(2,1)} %get-tuple-element.8.normed_ref, f32[128,128]{1,0:T(8,128)} %get-tuple-element.9.inv_ref, bf16[128,128,128]{2,1,0:T(8,128)(2,1)} %get-tuple-element.10.emb_ref), custom_call_target="tpu_custom_call" | custom-call | flops 1610612736 | bytes 7340032 | tf_op jit(solution)/shard_map/fm_backward/pallas_call | solution.py:117
  155.4 1.3 pad_maximum_fusion
  156.7 3.6 %all-to-all-start.12 = ((f32[8,8,128]{2,1,0:T(8,128)}), f32[8,8,128]{2,1,0:T(8,128)S(1)}, u32[]{:S(2)}, u32[]{:S(2)}) async-start(f32[8,8,128]{2,1,0:T(8,128)} %pad_maximum_fusion), calls=%async_computation.12 | async-start | bytes 65536 | tf_op jit(solution)/shard_map/all_to_all | solution.py:15
  160.3 0.0 copy-done.2
  160.3 0.8 convolution_convert_fusion
  161.1 1.5 copy.39
  162.6 2.5 all-to-all-done.12
  165.1 4.5 %all-to-all-start.6 = ((bf16[2,4,16,32,256]{4,3,1,2,0:T(8,128)(2,1)}), bf16[2,4,16,32,256]{4,3,1,2,0:T(8,128)(2,1)S(1)}, u32[]{:S(2)}, u32[]{:S(2)}) async-start(bf16[2,4,16,32,256]{4,3,1,2,0:T(8,128)(2,1)} %bitcast.32), calls=%async_computation.6 | async-start | bytes 4194304 | tf_op jit(solution)/shard_map/all_to_all | solution.py:15
  169.6 2.5 all-to-all-done.6
  172.1 0.6 broadcast_in_dim.45
  172.7 3.5 %all-to-all-start.13 = ((f32[16,8,128]{2,1,0:T(8,128)}), f32[16,8,128]{2,1,0:T(8,128)S(1)}, u32[]{:S(2)}, u32[]{:S(2)}) async-start(f32[16,8,128]{2,1,0:T(8,128)} %broadcast_in_dim.45), calls=%async_computation.13 | async-start | bytes 131072 | tf_op jit(solution)/shard_map/all_to_all | solution.py:15
  176.2 1.7 reduce_sum.60
  177.9 2.3 copy.34
  180.2 3.4 %all-to-all-done.13 = f32[16,8,128]{2,1,0:T(8,128)S(1)} async-done(((f32[16,8,128]{2,1,0:T(8,128)}), f32[16,8,128]{2,1,0:T(8,128)S(1)}, u32[]{:S(2)}, u32[]{:S(2)}) %all-to-all-start.13) | async-done | bytes 65568 | tf_op jit(solution)/shard_map/all_to_all | solution.py:15
  183.6 3.5 %all-to-all-start.7 = ((bf16[4,16,32,256]{3,2,1,0:T(8,128)(2,1)}), bf16[4,16,32,256]{3,2,1,0:T(8,128)(2,1)S(1)}, u32[]{:S(2)}, u32[]{:S(2)}) async-start(bf16[4,16,32,256]{3,2,1,0:T(8,128)(2,1)} %copy.34), calls=%async_computation.7 | async-start | bytes 2097152 | tf_op jit(solution)/shard_map/all_to_all | solution.py:15
  187.2 13.7 %all-to-all-done.7 = bf16[4,16,32,256]{3,2,1,0:T(8,128)(2,1)S(1)} async-done(((bf16[4,16,32,256]{3,2,1,0:T(8,128)(2,1)}), bf16[4,16,32,256]{3,2,1,0:T(8,128)(2,1)S(1)}, u32[]{:S(2)}, u32[]{:S(2)}) %all-to-all-start.7) | async-done | bytes 1048608 | tf_op jit(solution)/shard_map/all_to_all | solution.py:15
  200.8 0.6 broadcast_in_dim.46
  201.4 3.2 %all-to-all-start.14 = ((f32[4,4,128]{2,1,0:T(4,128)}), f32[4,4,128]{2,1,0:T(4,128)S(1)}, u32[]{:S(2)}, u32[]{:S(2)}) async-start(f32[4,4,128]{2,1,0:T(4,128)} %broadcast_in_dim.46), calls=%async_computation.14 | async-start | bytes 16384 | tf_op jit(solution)/shard_map/all_to_all | solution.py:15
  204.7 0.9 reduce_sum.61
  205.6 5.6 %all-to-all-done.14 = f32[4,4,128]{2,1,0:T(4,128)S(1)} async-done(((f32[4,4,128]{2,1,0:T(4,128)}), f32[4,4,128]{2,1,0:T(4,128)S(1)}, u32[]{:S(2)}, u32[]{:S(2)}) %all-to-all-start.14) | async-done | bytes 8224 | tf_op jit(solution)/shard_map/all_to_all | solution.py:15
  211.2 5.0 %all-to-all-start.8 = ((bf16[16,32,256]{2,1,0:T(8,128)(2,1)}), bf16[16,32,256]{2,1,0:T(8,128)(2,1)S(1)}, u32[]{:S(2)}, u32[]{:S(2)}) async-start(bf16[16,32,256]{2,1,0:T(8,128)(2,1)} %reduce_sum.61), calls=%async_computation.8 | async-start | bytes 524288 | tf_op jit(solution)/shard_map/all_to_all | solution.py:15
  216.3 7.8 %all-to-all-done.8 = bf16[16,32,256]{2,1,0:T(8,128)(2,1)S(1)} async-done(((bf16[16,32,256]{2,1,0:T(8,128)(2,1)}), bf16[16,32,256]{2,1,0:T(8,128)(2,1)S(1)}, u32[]{:S(2)}, u32[]{:S(2)}) %all-to-all-start.8) | async-done | bytes 262176 | tf_op jit(solution)/shard_map/all_to_all | solution.py:15
  224.1 0.6 broadcast_in_dim.47
  224.7 7.5 %all-to-all-start.15 = ((f32[8,8,128]{2,1,0:T(8,128)}), f32[8,8,128]{2,1,0:T(8,128)S(1)}, u32[]{:S(2)}, u32[]{:S(2)}) async-start(f32[8,8,128]{2,1,0:T(8,128)} %broadcast_in_dim.47), calls=%async_computation.15 | async-start | bytes 65536 | tf_op jit(solution)/shard_map/all_to_all | solution.py:15
  232.2 0.6 fusion.23
  232.9 4.0 %all-to-all-done.15 = f32[8,8,128]{2,1,0:T(8,128)S(1)} async-done(((f32[8,8,128]{2,1,0:T(8,128)}), f32[8,8,128]{2,1,0:T(8,128)S(1)}, u32[]{:S(2)}, u32[]{:S(2)}) %all-to-all-start.15) | async-done | bytes 32800 | tf_op jit(solution)/shard_map/all_to_all | solution.py:15
  236.9 12.4 %all_to_all.84 = bf16[16,32,256]{2,1,0:T(8,128)(2,1)S(1)} all-to-all(bf16[16,32,256]{2,1,0:T(8,128)(2,1)S(1)} %broadcast_in_dim.42), channel_id=1, replica_groups=mesh['zl'=2,'y'=8,'x'=4,'c'=2,'mp'=4] {'zl','y'}, dimensions={0} | all-to-all | bytes 524288 | tf_op jit(solution)/shard_map/all_to_all | solution.py:15
  249.3 1.1 broadcast_in_dim.43
  250.4 3.5 %all-to-all-start.10 = ((bf16[4,16,32,256]{3,2,1,0:T(8,128)(2,1)}), bf16[4,16,32,256]{3,2,1,0:T(8,128)(2,1)S(1)}, u32[]{:S(2)}, u32[]{:S(2)}) async-start(bf16[4,16,32,256]{3,2,1,0:T(8,128)(2,1)} %broadcast_in_dim.43), calls=%async_computation.10 | async-start | bytes 2097152 | tf_op jit(solution)/shard_map/all_to_all | solution.py:15
  254.0 0.6 fusion.24
  254.6 11.9 %all-to-all-done.10 = bf16[4,16,32,256]{3,2,1,0:T(8,128)(2,1)S(1)} async-done(((bf16[4,16,32,256]{3,2,1,0:T(8,128)(2,1)}), bf16[4,16,32,256]{3,2,1,0:T(8,128)(2,1)S(1)}, u32[]{:S(2)}, u32[]{:S(2)}) %all-to-all-start.10) | async-done | bytes 1048608 | tf_op jit(solution)/shard_map/all_to_all | solution.py:15
  266.5 0.1 copy.35
  266.6 0.3 broadcast_in_dim.44
  266.8 8.5 %all_to_all.85 = bf16[2,4,16,32,256]{4,3,1,2,0:T(8,128)(2,1)S(1)} all-to-all(bf16[2,4,16,32,256]{4,3,1,2,0:T(8,128)(2,1)S(1)} %broadcast_in_dim.44), channel_id=1, replica_groups=mesh['zl'=2,'y'=8,'x'=4,'c'=2,'mp'=4] {'c'}, dimensions={0} | all-to-all | bytes 4194304 | tf_op jit(solution)/shard_map/all_to_all | solution.py:15
  275.4 1.5 copy.36
  (16 shorter events, 0.2 us)
Async XLA Ops:
  0.6 136.2 %copy-start = (bf16[128,32,128]{2,1,0:T(8,128)(2,1)S(1)}, bf16[128,32,128]{2,1,0:T(8,128)(2,1)}, u32[]{:S(2)}) copy-start(bf16[128,32,128]{2,1,0:T(8,128)(2,1)} %param.13) | copy-start | bytes 3145732
  1.5 34.7 %copy-start.7 = (bf16[16,128]{1,0:T(8,128)(2,1)S(1)}, bf16[16,128]{1,0:T(8,128)(2,1)}, u32[]{:S(2)}) copy-start(bf16[16,128]{1,0:T(8,128)(2,1)} %param.8) | copy-start | bytes 12292
  36.9 26.6 %all-to-all-start = ((bf16[64,16,128]{2,1,0:T(8,128)(2,1)}), bf16[64,16,128]{2,1,0:T(8,128)(2,1)S(1)}, u32[]{:S(2)}, u32[]{:S(2)}) async-start(bf16[64,16,128]{2,1,0:T(8,128)(2,1)} %broadcast_in_dim.36), calls=%async_computation | async-start | bytes 524288 | tf_op jit(solution)/shard_map/all_to_all | solution.py:15
  73.7 5.4 %copy-start.5 = (s32[128,128]{1,0:T(8,128)S(1)}, s32[128,128]{1,0:T(8,128)}, u32[]{:S(2)}) copy-start(s32[128,128]{1,0:T(8,128)} %param.7) | copy-start | bytes 196612
  74.8 19.1 %all-to-all-start.1 = ((bf16[4,64,16,128]{3,2,1,0:T(8,128)(2,1)}), bf16[4,64,16,128]{3,2,1,0:T(8,128)(2,1)}, u32[]{:S(2)}, u32[]{:S(2)}) async-start(bf16[4,64,16,128]{3,2,1,0:T(8,128)(2,1)} %broadcast_in_dim.37), calls=%async_computation.1 | async-start | bytes 2097152 | tf_op jit(solution)/shard_map/all_to_all | solution.py:15
  132.9 1.7 copy-start.3
  134.6 2.9 %copy-start.1 = (bf16[128,128,128]{2,1,0:T(8,128)(2,1)S(1)}, bf16[128,128,128]{2,1,0:T(8,128)(2,1)}, u32[]{:S(2)}) copy-start(bf16[128,128,128]{2,1,0:T(8,128)(2,1)} %get-tuple-element.10.emb_ref) | copy-start | bytes 12582916
  139.0 21.3 %copy-start.2 = (bf16[128,4096]{1,0:T(8,128)(2,1)S(1)}, bf16[128,4096]{1,0:T(8,128)(2,1)}, u32[]{:S(2)}) copy-start(bf16[128,4096]{1,0:T(8,128)(2,1)} %get-tuple-element.8.normed_ref) | copy-start | bytes 3145732
  156.7 8.4 %all-to-all-start.12 = ((f32[8,8,128]{2,1,0:T(8,128)}), f32[8,8,128]{2,1,0:T(8,128)S(1)}, u32[]{:S(2)}, u32[]{:S(2)}) async-start(f32[8,8,128]{2,1,0:T(8,128)} %pad_maximum_fusion), calls=%async_computation.12 | async-start | bytes 65536 | tf_op jit(solution)/shard_map/all_to_all | solution.py:15
  165.1 7.0 %all-to-all-start.6 = ((bf16[2,4,16,32,256]{4,3,1,2,0:T(8,128)(2,1)}), bf16[2,4,16,32,256]{4,3,1,2,0:T(8,128)(2,1)S(1)}, u32[]{:S(2)}, u32[]{:S(2)}) async-start(bf16[2,4,16,32,256]{4,3,1,2,0:T(8,128)(2,1)} %bitcast.32), calls=%async_computation.6 | async-start | bytes 4194304 | tf_op jit(solution)/shard_map/all_to_all | solution.py:15
  172.7 10.9 %all-to-all-start.13 = ((f32[16,8,128]{2,1,0:T(8,128)}), f32[16,8,128]{2,1,0:T(8,128)S(1)}, u32[]{:S(2)}, u32[]{:S(2)}) async-start(f32[16,8,128]{2,1,0:T(8,128)} %broadcast_in_dim.45), calls=%async_computation.13 | async-start | bytes 131072 | tf_op jit(solution)/shard_map/all_to_all | solution.py:15
  180.2 52.0 %copy-start.4 = (f32[32,256]{1,0:T(8,128)S(1)}, f32[32,256]{1,0:T(8,128)}, u32[]{:S(2)}) copy-start(f32[32,256]{1,0:T(8,128)} %param.10) | copy-start | bytes 98308
  180.2 52.0 %copy-start.6 = (f32[32,256]{1,0:T(8,128)S(1)}, f32[32,256]{1,0:T(8,128)}, u32[]{:S(2)}) copy-start(f32[32,256]{1,0:T(8,128)} %param.11) | copy-start | bytes 98308
  183.6 17.2 %all-to-all-start.7 = ((bf16[4,16,32,256]{3,2,1,0:T(8,128)(2,1)}), bf16[4,16,32,256]{3,2,1,0:T(8,128)(2,1)S(1)}, u32[]{:S(2)}, u32[]{:S(2)}) async-start(bf16[4,16,32,256]{3,2,1,0:T(8,128)(2,1)} %copy.34), calls=%async_computation.7 | async-start | bytes 2097152 | tf_op jit(solution)/shard_map/all_to_all | solution.py:15
  201.4 9.8 %all-to-all-start.14 = ((f32[4,4,128]{2,1,0:T(4,128)}), f32[4,4,128]{2,1,0:T(4,128)S(1)}, u32[]{:S(2)}, u32[]{:S(2)}) async-start(f32[4,4,128]{2,1,0:T(4,128)} %broadcast_in_dim.46), calls=%async_computation.14 | async-start | bytes 16384 | tf_op jit(solution)/shard_map/all_to_all | solution.py:15
  211.2 12.9 %all-to-all-start.8 = ((bf16[16,32,256]{2,1,0:T(8,128)(2,1)}), bf16[16,32,256]{2,1,0:T(8,128)(2,1)S(1)}, u32[]{:S(2)}, u32[]{:S(2)}) async-start(bf16[16,32,256]{2,1,0:T(8,128)(2,1)} %reduce_sum.61), calls=%async_computation.8 | async-start | bytes 524288 | tf_op jit(solution)/shard_map/all_to_all | solution.py:15
  224.7 12.2 %all-to-all-start.15 = ((f32[8,8,128]{2,1,0:T(8,128)}), f32[8,8,128]{2,1,0:T(8,128)S(1)}, u32[]{:S(2)}, u32[]{:S(2)}) async-start(f32[8,8,128]{2,1,0:T(8,128)} %broadcast_in_dim.47), calls=%async_computation.15 | async-start | bytes 65536 | tf_op jit(solution)/shard_map/all_to_all | solution.py:15
  250.4 16.0 %all-to-all-start.10 = ((bf16[4,16,32,256]{3,2,1,0:T(8,128)(2,1)}), bf16[4,16,32,256]{3,2,1,0:T(8,128)(2,1)S(1)}, u32[]{:S(2)}, u32[]{:S(2)}) async-start(bf16[4,16,32,256]{3,2,1,0:T(8,128)(2,1)} %broadcast_in_dim.43), calls=%async_computation.10 | async-start | bytes 2097152 | tf_op jit(solution)/shard_map/all_to_all | solution.py:15

commit v2 on v1

v2 whole, which is shorter than its diff:
```python
import jax
import jax.numpy as jnp
from jax import lax
from jax.experimental import pallas as pl
from jax.experimental.pallas import tpu as pltpu
from jax.sharding import Mesh
from jax.sharding import PartitionSpec as P


DP = ("zl", "y", "x", "c")
DP_MP = ("zl", "y", "x", "c", "mp")
CX = ("c", "x")
ZY = ("zl", "y")
GROUP = 8
FIRST_SHARE = 0.75


def exchange(tiles, axis):
    return lax.all_to_all(tiles, axis, split_axis=0, concat_axis=0, tiled=True)


def from_everyone(x, axis):
    return exchange(jnp.broadcast_to(x, (lax.axis_size(axis), *x.shape)), axis)


def swapped(x, axis, flip):
    return lax.ppermute(x, axis, [(i, i ^ flip) for i in range(lax.axis_size(axis))])


def doubled(x, axis, flip):
    other = swapped(x, axis, flip)
    high = (lax.axis_index(axis) & flip) != 0
    return jnp.concatenate([jnp.where(high, other, x), jnp.where(high, x, other)], axis=0)


def tied(*values):
    return lax.optimization_barrier(values)


def summed(tiles):
    return tiles.astype(jnp.float32).sum(axis=0)


def forward_kernel(ids_ref, table_ref, proj_ref, emb_ref, normed_ref, inv_ref, even_ref, odd_ref, fm_ref):
    rank, n_emb = proj_ref.shape
    width = table_ref.shape[2]
    proj = proj_ref[...]
    for e in range(0, GROUP, 2):
        rows_ref = (even_ref, odd_ref)[e // 2 % 2]
        for r in range(2 * n_emb):
            rows_ref[pl.ds(r, 1), :] = table_ref[ids_ref[e + r // n_emb, r % n_emb]]
        pair = rows_ref[...].astype(jnp.bfloat16)
        first, second = pair[:n_emb], pair[n_emb:]
        emb_ref[e] = first
        emb_ref[e + 1] = second
        compressed = jnp.dot(
            proj, jnp.concatenate([first, second], axis=1), preferred_element_type=jnp.float32
        ).astype(jnp.bfloat16)
        compressed = jnp.concatenate([compressed[:, :width], compressed[:, width:]], axis=0)
        fm = lax.dot_general(compressed, pair, (((1,), (1,)), ((), ())), preferred_element_type=jnp.float32)
        fm_ref[pl.ds(e * rank, rank), :] = fm[:rank, :n_emb]
        fm_ref[pl.ds((e + 1) * rank, rank), :] = fm[rank:, n_emb:]
    scale = 1.0 / (rank * n_emb)
    parts = [fm_ref[pl.ds(k, GROUP, stride=rank), :] for k in range(rank)]
    mean = jnp.sum(sum(parts), axis=1, keepdims=True) * scale
    parts = [p - mean for p in parts]
    var = jnp.sum(sum(p * p for p in parts), axis=1, keepdims=True) * scale
    inv = 1.0 / jnp.sqrt(var + 1.0)
    per = normed_ref.shape[2] // n_emb
    for k in range(rank):
        at = k % per * n_emb
        normed_ref[k // per, :, at : at + n_emb] = (parts[k] * inv).astype(jnp.bfloat16)
    inv_ref[...] = jnp.broadcast_to(inv, inv_ref.shape)


def forward_features(ids, rows, projection, members, start, examples):
    n_emb = ids.shape[1]
    vocab, _, width = rows.shape
    rank = projection.shape[1]
    columns = rank * n_emb // members
    skip = start // GROUP
    return pl.pallas_call(
        forward_kernel,
        grid=(examples // GROUP,),
        in_specs=[
            pl.BlockSpec((GROUP, n_emb), lambda g: (g + skip, 0), memory_space=pltpu.SMEM),
            pl.BlockSpec((vocab, 1, width), lambda g: (0, 0, 0)),
            pl.BlockSpec((rank, n_emb), lambda g: (0, 0)),
        ],
        out_specs=[
            pl.BlockSpec((GROUP, n_emb, width), lambda g: (g, 0, 0)),
            pl.BlockSpec((members, GROUP, columns), lambda g: (0, g, 0)),
            pl.BlockSpec((GROUP, 128), lambda g: (g, 0)),
        ],
        out_shape=[
            jax.ShapeDtypeStruct((examples, n_emb, width), jnp.bfloat16),
            jax.ShapeDtypeStruct((members, examples, columns), jnp.bfloat16),
            jax.ShapeDtypeStruct((examples, 128), jnp.float32),
        ],
        scratch_shapes=[
            pltpu.VMEM((2 * n_emb, width), jnp.float32),
            pltpu.VMEM((2 * n_emb, width), jnp.float32),
            pltpu.VMEM((GROUP * rank, n_emb), jnp.float32),
        ],
        cost_estimate=pl.CostEstimate(
            flops=100_000_000 * examples,
            bytes_accessed=vocab * width * 4 + examples * n_emb * width * 2,
            transcendentals=0,
        ),
        name="fm_forward",
    )(ids, rows, projection.T)


def backward_kernel(grad_ref, normed_ref, inv_ref, emb_ref, back_ref, fm_grad_ref):
    n_emb = emb_ref.shape[1]
    rank, width = back_ref.shape[1:]
    per = normed_ref.shape[2] // n_emb
    scale = 1.0 / (rank * n_emb)
    grads = [grad_ref[:, k * n_emb : (k + 1) * n_emb] for k in range(rank)]
    normed = [
        normed_ref[k // per, :, k % per * n_emb : (k % per + 1) * n_emb].astype(jnp.float32) for k in range(rank)
    ]
    mean = jnp.sum(sum(grads), axis=1, keepdims=True) * scale
    along = jnp.sum(sum(g * x for g, x in zip(grads, normed)), axis=1, keepdims=True) * scale
    inv = inv_ref[:, :1]
    for k in range(rank):
        fm_grad_ref[pl.ds(k, GROUP, stride=rank), :] = (grads[k] - mean - normed[k] * along) * inv
    for e in range(0, GROUP, 2):
        fm_grad = fm_grad_ref[pl.ds(e * rank, 2 * rank), :].astype(jnp.bfloat16)
        pair = jnp.concatenate([emb_ref[e], emb_ref[e + 1]], axis=1)
        back = jnp.dot(fm_grad, pair, preferred_element_type=jnp.float32).astype(jnp.bfloat16)
        back_ref[e] = back[:rank, :width]
        back_ref[e + 1] = back[rank:, width:]


def backward_features(normed_grad, normed, inv_scale, embedded):
    examples, n_emb, width = embedded.shape
    members, _, columns = normed.shape
    rank = members * columns // n_emb
    return pl.pallas_call(
        backward_kernel,
        grid=(examples // GROUP,),
        in_specs=[
            pl.BlockSpec((GROUP, rank * n_emb), lambda g: (g, 0)),
            pl.BlockSpec((members, GROUP, columns), lambda g: (0, g, 0)),
            pl.BlockSpec((GROUP, 128), lambda g: (g, 0)),
            pl.BlockSpec((GROUP, n_emb, width), lambda g: (g, 0, 0)),
        ],
        out_specs=pl.BlockSpec((GROUP, rank, width), lambda g: (g, 0, 0)),
        out_shape=jax.ShapeDtypeStruct((examples, rank, width), jnp.bfloat16),
        scratch_shapes=[pltpu.VMEM((GROUP * rank, n_emb), jnp.float32)],
        cost_estimate=pl.CostEstimate(
            flops=30_000_000 * examples,
            bytes_accessed=examples * n_emb * (width * 2 + rank * 8),
            transcendentals=0,
        ),
        name="fm_backward",
    )(normed_grad, normed, inv_scale, embedded)


def both_halves(half):
    other = swapped(half, "c", 1)
    high = lax.axis_index("c") == 1
    return jnp.where(high, jnp.stack([other, half]), jnp.stack([half, other])).reshape(-1, *half.shape[1:])


def per_device(feature_ids, emb_table, factor_machine_projection, mlp_weight, momentum, hidden_grad, lcb_grad):
    mp, zl, y, x, c = (lax.axis_size(a) for a in ("mp", "zl", "y", "x", "c"))
    own = emb_table.shape[0]
    rank = factor_machine_projection.shape[1]
    examples, hidden = hidden_grad.shape

    to_worker = []
    for block in range(zl * y * x * c):
        cx, zy = divmod(block, zl * y)
        at_c, at_x = divmod(cx, x)
        to_worker.append((block, (zy * x + at_x) * c + at_c))
    to_owner = [(worker, owner) for owner, worker in to_worker]

    table = from_everyone(emb_table, ("mp", "zl", "y"))
    state = lax.ppermute(jnp.stack([mlp_weight, momentum]), DP, to_worker)
    weight_rows, momentum_rows = state[0], state[1]
    weights = weight_rows.astype(jnp.bfloat16)
    for axis, flip in (("y", 1), ("y", 2), ("y", 4), ("zl", 1)):
        weights = doubled(weights, axis, flip)
    table = from_everyone(table, "x").reshape(-1, emb_table.shape[1])
    weights, table = tied(weights, table)
    table = jnp.concatenate([table, swapped(table, "c", 1)], axis=0)
    rows = table.astype(jnp.float32).reshape(table.shape[0], 1, table.shape[1])
    weights = from_everyone(weights, "x").reshape(-1, hidden)
    owner, row = lax.div(feature_ids, own), lax.rem(feature_ids, own)
    owner, at_mp = lax.div(owner, mp), lax.rem(owner, mp)
    owner, at_c = lax.div(owner, c), lax.rem(owner, c)
    at_zy, at_x = lax.div(owner, x), lax.rem(owner, x)
    ids = ((((at_c ^ lax.axis_index("c")) * x + at_x) * mp + at_mp) * (zl * y) + at_zy) * own + row

    cut = int(examples * FIRST_SHARE)
    shares = ((0, cut), (cut, examples - cut))
    first = forward_features(ids, rows, factor_machine_projection, c * x, *shares[0])
    weights, ids, first_inv = tied(weights, ids, first[2])
    weights = both_halves(weights)
    second = forward_features(ids, rows, factor_machine_projection, c * x, *shares[1])
    features = ((first[0], first[1], first_inv), second)
    columns = [exchange(f[1], CX) for f in features]

    tiled_weights = weights.reshape(c * x, -1, hidden)
    preact = jnp.concatenate(
        [
            jnp.einsum("jbk,jkn->bn", normed, tiled_weights, preferred_element_type=jnp.float32)
            for _, normed, _ in features
        ],
        axis=0,
    )
    sigmoid_pre = jax.nn.sigmoid(preact)
    preact_grad = (
        hidden_grad.astype(jnp.float32) * sigmoid_pre * (1.0 + preact * (1.0 - sigmoid_pre))
    ).astype(jnp.bfloat16)
    group_grad = from_everyone(preact_grad, CX)

    proj_part, lcb_part = 0.0, 0.0
    for (embedded, normed, inv_scale), (start, count) in zip(features, shares):
        normed_part = lax.dot_general(
            preact_grad[start : start + count],
            weights,
            (((1,), (1,)), ((), ())),
            preferred_element_type=jnp.float32,
        )
        back = backward_features(normed_part, normed, inv_scale, embedded)
        proj_part += jnp.einsum("bqh,blh->ql", back, embedded, preferred_element_type=jnp.float32)
        lcb_part += jnp.einsum(
            "bld,bnd->ln", lcb_grad[start : start + count], embedded, preferred_element_type=jnp.float32
        )

    weight_grad = sum(
        lax.dot_general(
            part,
            group_grad[:, start : start + count],
            (((0, 1), (0, 1)), ((), ())),
            preferred_element_type=jnp.float32,
        )
        for part, (start, count) in zip(columns, shares)
    )
    weight_grad = exchange(weight_grad.astype(jnp.bfloat16).reshape(zl * y, -1, hidden), ZY)
    for flip in (1, 3):
        proj_part += swapped(proj_part, "mp", flip)
    both = jnp.concatenate([proj_part, lcb_part], axis=0)
    weight_grad, both = tied(weight_grad, both)
    new_momentum = 0.9 * momentum_rows + summed(weight_grad)
    new_weight = weight_rows - 0.01 * new_momentum
    next_weight = from_everyone(new_weight.astype(jnp.bfloat16), ZY)
    for axis, flip in (("c", 1), ("x", 1), ("x", 3)):
        both += swapped(both, axis, flip)
    next_weight, both = tied(next_weight, both)
    next_weight = from_everyone(next_weight, "x").reshape(-1, hidden)
    state = lax.ppermute(jnp.stack([new_weight, new_momentum]), DP, to_owner)
    for axis, flip in (("zl", 1), ("y", 1), ("y", 3)):
        both += swapped(both, axis, flip)
    next_weight, both, state = tied(next_weight, both, state)
    next_weight = both_halves(next_weight)
    both += swapped(both, "y", 7)
    return (state[0], state[1], next_weight, both[:rank].T, both[rank:].T)


def solution(mesh):
    torus = Mesh(mesh.devices.reshape(2, 8, 4, 2, mesh.shape["mp"]), DP_MP)
    placed = (
        P(DP, None),
        P(DP_MP, None),
        P(),
        P(DP, "mp"),
        P(DP, "mp"),
        P(DP, "mp"),
        P(DP, "mp", None),
    )

    return jax.shard_map(
        per_device,
        mesh=torus,
        in_specs=placed,
        out_specs=(P(DP, "mp"), P(DP, "mp"), P(None, "mp"), P(), P(None, "mp")),
        check_vma=False,
    )
```

time: 279 us -> 301 us (1.079)
  starting transfers between devices: 52.6 us -> 130 us
  blocking collectives: 71.7 us -> 0 us
  waiting for transfers between devices: 76 us -> 33.5 us
  local copies, waits for them, and re-layouts: 15.7 us -> 41.6 us
  other arithmetic: 8.79 us -> 30.8 us
  matrix products: 6.02 us -> 15.4 us
    ppermute x0 -> x18, starting transfers between devices: none -> 71.8 us  [the longest x16 60.5 us: swapped(): lax.ppermute(x, axis, [(i, i ^ flip) for i in range(lax.axis_size(axis))])]
    all_to_all x6 -> x0, blocking collectives: 71.7 us -> none  [exchange(): return lax.all_to_all(tiles, axis, split_axis=0, concat_axis=0, tiled=True)]
    all_to_all x10 -> x9, waiting for transfers between devices: 76 us -> 11.5 us  [exchange(): return lax.all_to_all(tiles, axis, split_axis=0, concat_axis=0, tiled=True)]
    concatenate x0 -> x2, local copies, waits for them, and re-layouts: none -> 33.5 us  [per_device(): table = jnp.concatenate([table, swapped(table, 'c', 1)], axis=0)]
    ppermute x0 -> x18, waiting for transfers between devices: none -> 22 us  [the longest x16 19.3 us: swapped(): lax.ppermute(x, axis, [(i, i ^ flip) for i in range(lax.axis_size(axis))])]
    convert_element_type x3, other arithmetic: 3.81 us -> 25.5 us  [the longest x1 25.5 us: per_device(): rows = table.astype(jnp.float32).reshape(table.shape[0], 1, table.shape[1])]
    dot_general x4 -> x10, matrix products: 6.02 us -> 15.4 us  [the longest x2 4.56 us: per_device(): lax.dot_general(part, group_grad[:, start:start + count], (((0, 1), (0, 1...]
    all_to_all x10 -> x9, starting transfers between devices: 52.6 us -> 58.4 us  [exchange(): return lax.all_to_all(tiles, axis, split_axis=0, concat_axis=0, tiled=True)]
  transfers between devices with their start and end apart: 10 -> 27, of which waited for: 10 -> 13; matrix products, arithmetic and copies ran while one was open for 4% -> 28% of each run, Pallas kernels for 0% -> 15%
where the time goes in v2:
time: 301 us; the launch traced here: 298 us
  starting transfers between devices  130 us (43%)
  Pallas kernels  44.9 us (15%)
  local copies, waits for them, and re-layouts  41.6 us (14%)
  waiting for transfers between devices  33.5 us (11%)
  other arithmetic  30.8 us (10%)
  matrix products  15.4 us (5%)
    ppermute x16, starting transfers between devices, swapped(): lax.ppermute(x, axis, [(i, i ^ flip) for i in range(lax.axis_size(axis))])  60.5 us
    all_to_all x9, starting transfers between devices, exchange(): return lax.all_to_all(tiles, axis, split_axis=0, concat_axis=0, tiled=True)  58.4 us
    concatenate x2, local copies, waits for them, and re-layouts, per_device(): table = jnp.concatenate([table, swapped(table, 'c', 1)], axis=0)  33.5 us
    pallas_call x2, Pallas kernels, forward_features(): pl.pallas_call(forward_kernel, grid=(examples // GROUP,), in_specs=[pl.Bl...  30.7 us
    convert_element_type x1, other arithmetic, per_device(): rows = table.astype(jnp.float32).reshape(table.shape[0], 1, table.shape[1])  25.5 us
    ppermute x16, waiting for transfers between devices, swapped(): lax.ppermute(x, axis, [(i, i ^ flip) for i in range(lax.axis_size(axis))])  19.3 us
    pallas_call x2, Pallas kernels, backward_features(): pl.pallas_call(backward_kernel, grid=(examples // GROUP,), in_specs=[pl.B...  14.2 us
    all_to_all x9, waiting for transfers between devices, exchange(): return lax.all_to_all(tiles, axis, split_axis=0, concat_axis=0, tiled=True)  11.5 us
  transfers between devices with their start and end apart: 27, of which 13 were waited for; matrix products, arithmetic and copies ran while one was open for 28% of the time, Pallas kernels for 15%

profile of v2, /device:TPU:1, one launch (start us, length us, event | category | flops | bytes accessed | tf_op | source)
XLA Modules:
  0.0 297.8 jit_solution(3387977946832407501)
XLA Ops:
  0.6 0.8 pad_maximum_fusion.3
  1.4 4.6 %collective-permute-start = (f32[2,32,256]{2,1,0:T(8,128)S(1)}, f32[2,32,256]{2,1,0:T(8,128)S(1)}, u32[]{:S(2)}, u32[]{:S(2)}) collective-permute-start(f32[2,32,256]{2,1,0:T(8,128)S(1)} %pad_maximum_fusion.3), channel_id=1, source_target_pairs={{0,0},{4,32},{8,64},{12,96},{16,128},{20,160},{24,192},{28,224},{3... | collective-permute-start | bytes 196616 | tf_op jit(solution)/shard_map/ppermute | solution.py:181
  6.0 2.7 collective-permute-done
  8.7 2.6 collective-permute-start.1
  11.3 1.4 broadcast_in_dim.18
  12.8 22.7 %all-to-all-start = ((bf16[64,16,128]{2,1,0:T(8,128)(2,1)}), bf16[64,16,128]{2,1,0:T(8,128)(2,1)S(1)}, u32[]{:S(2)}, u32[]{:S(2)}) async-start(bf16[64,16,128]{2,1,0:T(8,128)(2,1)} %broadcast_in_dim.18), calls=%async_computation | async-start | bytes 524288 | tf_op jit(solution)/shard_map/all_to_all | solution.py:19
  35.5 3.8 %collective-permute-start.2 = (bf16[64,256]{1,0:T(8,128)(2,1)S(1)}, bf16[64,256]{1,0:T(8,128)(2,1)S(1)}, u32[]{:S(2)}, u32[]{:S(2)}) collective-permute-start(bf16[64,256]{1,0:T(8,128)(2,1)S(1)} %pad_maximum_fusion.6), channel_id=1, source_target_pairs={{0,64},{32,96},{64,0},{96,32},{128,192},{160,224},{192,128},{224,1... | collective-permute-start | bytes 98312 | tf_op jit(solution)/shard_map/ppermute | solution.py:27
  39.3 3.9 %collective-permute-done.2 = bf16[64,256]{1,0:T(8,128)(2,1)S(1)} collective-permute-done((bf16[64,256]{1,0:T(8,128)(2,1)S(1)}, bf16[64,256]{1,0:T(8,128)(2,1)S(1)}, u32[]{:S(2)}, u32[]{:S(2)}) %collective-permute-start.2) | collective-permute-done | bytes 32800 | tf_op jit(solution)/shard_map/ppermute | solution.py:27
  43.3 6.9 %collective-permute-start.3 = (bf16[128,256]{1,0:T(8,128)(2,1)S(1)}, bf16[128,256]{1,0:T(8,128)(2,1)S(1)}, u32[]{:S(2)}, u32[]{:S(2)}) collective-permute-start(bf16[128,256]{1,0:T(8,128)(2,1)S(1)} %pad_maximum_fusion.4), channel_id=1, source_target_pairs={{0,128},{32,160},{64,192},{96,224},{128,0},{160,32},{192,64},{224,... | collective-permute-start | bytes 196616 | tf_op jit(solution)/shard_map/ppermute | solution.py:27
  50.2 1.1 broadcast_in_dim.19
  51.3 3.6 %all-to-all-start.1 = ((bf16[4,64,16,128]{3,2,1,0:T(8,128)(2,1)}), bf16[4,64,16,128]{3,2,1,0:T(8,128)(2,1)S(1)}, u32[]{:S(2)}, u32[]{:S(2)}) async-start(bf16[4,64,16,128]{3,2,1,0:T(8,128)(2,1)} %broadcast_in_dim.19), calls=%async_computation.1 | async-start | bytes 2097152 | tf_op jit(solution)/shard_map/all_to_all | solution.py:19
  55.0 2.7 collective-permute-start.4
  57.8 3.3 %collective-permute-done.4 = bf16[256,256]{1,0:T(8,128)(2,1)S(1)} collective-permute-done((bf16[256,256]{1,0:T(8,128)(2,1)S(1)}, bf16[256,256]{1,0:T(8,128)(2,1)S(1)}, u32[]{:S(2)}, u32[]{:S(2)}) %collective-permute-start.4) | collective-permute-done | bytes 131104 | tf_op jit(solution)/shard_map/ppermute | solution.py:27
  61.1 7.0 %all-to-all-done.1 = bf16[4,64,16,128]{3,2,1,0:T(8,128)(2,1)S(1)} async-done(((bf16[4,64,16,128]{3,2,1,0:T(8,128)(2,1)}), bf16[4,64,16,128]{3,2,1,0:T(8,128)(2,1)S(1)}, u32[]{:S(2)}, u32[]{:S(2)}) %all-to-all-start.1) | async-done | bytes 1048608 | tf_op jit(solution)/shard_map/all_to_all | solution.py:19
  68.2 4.7 %collective-permute-start.5 = (bf16[4096,128]{1,0:T(8,128)(2,1)S(1)}, bf16[4096,128]{1,0:T(8,128)(2,1)S(1)}, u32[]{:S(2)}, u32[]{:S(2)}) collective-permute-start(bf16[4096,128]{1,0:T(8,128)(2,1)S(1)} %bitcast.88), channel_id=1, source_target_pairs={{0,4},{4,0},{1,5},{5,1},{2,6},{6,2},{3,7},{7,3},{8,12},{12,8},{9,1... | collective-permute-start | bytes 3145736 | tf_op jit(solution)/shard_map/ppermute | solution.py:27
  72.9 0.7 fusion.17.ids_ref
  73.6 1.0 broadcast_in_dim.20
  74.7 3.5 %all-to-all-start.3 = ((bf16[4,512,256]{2,1,0:T(8,128)(2,1)}), bf16[4,512,256]{2,1,0:T(8,128)(2,1)S(1)}, u32[]{:S(2)}, u32[]{:S(2)}) async-start(bf16[4,512,256]{2,1,0:T(8,128)(2,1)} %broadcast_in_dim.20), calls=%async_computation.3 | async-start | bytes 2097152 | tf_op jit(solution)/shard_map/all_to_all | solution.py:19
  78.2 16.7 %copy.14 = bf16[4096,1,128]{2,1,0:T(2,128)(2,1)S(1)} copy(bf16[4096,1,128]{2,0,1:T(8,128)(2,1)S(1)} %bitcast.89) | data formatting | bytes 2097152 | tf_op jit(solution)/shard_map/concatenate | solution.py:188
  95.0 16.7 %copy.15 = bf16[4096,1,128]{2,1,0:T(2,128)(2,1)S(1)} copy(bf16[4096,1,128]{2,0,1:T(8,128)(2,1)S(1)} %bitcast.94) | data formatting | bytes 2097152 | tf_op jit(solution)/shard_map/concatenate | solution.py:188
  111.7 25.5 %maximum_convert_fusion.table_ref = f32[8192,1,128]{2,1,0:T(1,128)} fusion(bf16[4096,1,128]{2,1,0:T(2,128)(2,1)S(1)} %copy.15, bf16[4096,1,128]{2,1,0:T(2,128)(2,1)S(1)} %copy.14), kind=kLoop, calls=%fused_computation | loop fusion | flops 2097152 | bytes 6291456 | tf_op jit(solution)/shard_map/convert_element_type | solution.py:189
  137.2 21.6 %fm_forward.2 = (bf16[96,128,128]{2,1,0:T(8,128)(2,1)}, bf16[8,96,512]{2,1,0:T(8,128)(2,1)}, f32[96,128]{1,0:T(8,128)}) custom-call(s32[128,128]{1,0:T(8,128)} %fusion.17.ids_ref, f32[8192,1,128]{2,1,0:T(1,128)} %maximum_convert_fusion.table_ref, bf16[32,128]{1,0:T(8,128)(2,1)} %bitcast.98), custom_call_target="tpu_custom_call" | custom-call | flops 9600000000 | bytes 7340032 | tf_op jit(solution)/shard_map/fm_forward/pallas_call | solution.py:82
  158.7 1.9 collective-permute-start.6
  160.7 9.2 %fm_forward.3 = (bf16[32,128,128]{2,1,0:T(8,128)(2,1)}, bf16[8,32,512]{2,1,0:T(8,128)(2,1)}, f32[32,128]{1,0:T(8,128)}) custom-call(s32[128,128]{1,0:T(8,128)} %fusion.17.ids_ref, f32[8192,1,128]{2,1,0:T(1,128)} %maximum_convert_fusion.table_ref, bf16[32,128]{1,0:T(8,128)(2,1)} %bitcast.99), custom_call_target="tpu_custom_call" | custom-call | flops 3200000000 | bytes 5242880 | tf_op jit(solution)/shard_map/fm_forward/pallas_call | solution.py:82
  169.8 4.9 %all-to-all-start.5 = ((bf16[8,32,512]{2,1,0:T(8,128)(2,1)}), bf16[8,32,512]{2,1,0:T(8,128)(2,1)}, u32[]{:S(2)}, u32[]{:S(2)}) async-start(bf16[8,32,512]{2,1,0:T(8,128)(2,1)} %get-tuple-element.29.normed_ref), calls=%async_computation.5 | async-start | bytes 524288 | tf_op jit(solution)/shard_map/all_to_all | solution.py:19
  174.7 1.9 maximum_select_fusion
  177.1 0.6 copy-done.3
  178.3 1.9 fusion.20.grad_ref
  180.2 1.1 all-to-all-done.5
  181.4 0.8 broadcast_in_dim.21
  182.2 4.4 %all-to-all-start.4 = ((bf16[8,128,256]{2,1,0:T(8,128)(2,1)}), bf16[8,128,256]{2,1,0:T(8,128)(2,1)}, u32[]{:S(2)}, u32[]{:S(2)}) async-start(bf16[8,128,256]{2,1,0:T(8,128)(2,1)} %broadcast_in_dim.21), calls=%async_computation.4 | async-start | bytes 1048576 | tf_op jit(solution)/shard_map/all_to_all | solution.py:19
  186.6 1.5 fusion.25.grad_ref
  188.1 4.1 %fm_backward.3 = bf16[32,32,128]{2,1,0:T(8,128)(2,1)} custom-call(f32[32,4096]{1,0:T(8,128)} %fusion.25.grad_ref, bf16[8,32,512]{2,1,0:T(8,128)(2,1)} %get-tuple-element.29.normed_ref, f32[32,128]{1,0:T(8,128)} %get-tuple-element.32.inv_ref, bf16[32,128,128]{2,1,0:T(8,128)(2,1)} %get-tuple-element.33.emb_ref), custom_call_target="tpu_custom_call" | custom-call | flops 960000000 | bytes 2097152 | tf_op jit(solution)/shard_map/fm_backward/pallas_call | solution.py:140
  192.2 10.1 %fm_backward.2 = bf16[96,32,128]{2,1,0:T(8,128)(2,1)} custom-call(f32[96,4096]{1,0:T(8,128)} %fusion.20.grad_ref, bf16[8,96,512]{2,1,0:T(8,128)(2,1)} %get-tuple-element.24.normed_ref, f32[96,128]{1,0:T(8,128)} %get-tuple-element.30.inv_ref, bf16[96,128,128]{2,1,0:T(8,128)(2,1)} %get-tuple-element.31.emb_ref), custom_call_target="tpu_custom_call" | custom-call | flops 2880000000 | bytes 6291456 | tf_op jit(solution)/shard_map/fm_backward/pallas_call | solution.py:140
  202.3 4.8 %all-to-all-start.2 = ((bf16[8,96,512]{2,1,0:T(8,128)(2,1)}), bf16[8,96,512]{2,1,0:T(8,128)(2,1)}, u32[]{:S(2)}, u32[]{:S(2)}) async-start(bf16[8,96,512]{2,1,0:T(8,128)(2,1)} %get-tuple-element.24.normed_ref), calls=%async_computation.2 | async-start | bytes 1572864 | tf_op jit(solution)/shard_map/all_to_all | solution.py:19
  207.1 2.3 convolution_bitcast_fusion.7
  209.9 4.0 %collective-permute-start.7 = (f32[32,128]{1,0:T(8,128)S(1)}, f32[32,128]{1,0:T(8,128)S(1)}, u32[]{:S(2)}, u32[]{:S(2)}) collective-permute-start(f32[32,128]{1,0:T(8,128)S(1)} %fusion.4), channel_id=1, source_target_pairs={{0,1},{1,0},{2,3},{3,2},{4,5},{5,4},{6,7},{7,6},{8,9},{9,8},{10,11... | collective-permute-start | bytes 49160 | tf_op jit(solution)/shard_map/ppermute | solution.py:27
  214.0 2.0 convolution_bitcast_fusion
  216.0 3.3 %all-to-all-done.2 = bf16[8,96,512]{2,1,0:T(8,128)(2,1)} async-done(((bf16[8,96,512]{2,1,0:T(8,128)(2,1)}), bf16[8,96,512]{2,1,0:T(8,128)(2,1)}, u32[]{:S(2)}, u32[]{:S(2)}) %all-to-all-start.2) | async-done | bytes 786464 | tf_op jit(solution)/shard_map/all_to_all | solution.py:19
  219.3 2.5 fusion.1
  221.9 3.5 %all-to-all-start.6 = ((bf16[16,32,256]{2,1,0:T(8,128)(2,1)}), bf16[16,32,256]{2,1,0:T(8,128)(2,1)S(1)}, u32[]{:S(2)}, u32[]{:S(2)}) async-start(bf16[16,32,256]{2,1,0:T(8,128)(2,1)} %bitcast.95), calls=%async_computation.6 | async-start | bytes 524288 | tf_op jit(solution)/shard_map/all_to_all | solution.py:19
  225.4 2.3 convolution_bitcast_fusion.5
  227.8 5.5 %collective-permute-start.8 = (f32[32,128]{1,0:T(8,128)S(1)}, f32[32,128]{1,0:T(8,128)S(1)}, u32[]{:S(2)}, u32[]{:S(2)}) collective-permute-start(f32[32,128]{1,0:T(8,128)S(1)} %add.72), channel_id=1, source_target_pairs={{0,3},{1,2},{2,1},{3,0},{4,7},{5,6},{6,5},{7,4},{8,11},{9,10},{10,... | collective-permute-start | bytes 49160 | tf_op jit(solution)/shard_map/ppermute | solution.py:27
  233.2 1.4 fusion.3
  234.8 0.7 broadcast_in_dim.22
  235.6 7.4 %all-to-all-start.7 = ((bf16[16,32,256]{2,1,0:T(8,128)(2,1)}), bf16[16,32,256]{2,1,0:T(8,128)(2,1)S(1)}, u32[]{:S(2)}, u32[]{:S(2)}) async-start(bf16[16,32,256]{2,1,0:T(8,128)(2,1)} %broadcast_in_dim.22), calls=%async_computation.7 | async-start | bytes 524288 | tf_op jit(solution)/shard_map/all_to_all | solution.py:19
  243.0 3.7 %collective-permute-start.9 = (f32[64,128]{1,0:T(8,128)S(1)}, f32[64,128]{1,0:T(8,128)S(1)}, u32[]{:S(2)}, u32[]{:S(2)}) collective-permute-start(f32[64,128]{1,0:T(8,128)S(1)} %pad_maximum_fusion.7), channel_id=1, source_target_pairs={{0,4},{4,0},{1,5},{5,1},{2,6},{6,2},{3,7},{7,3},{8,12},{12,8},{9,1... | collective-permute-start | bytes 98312 | tf_op jit(solution)/shard_map/ppermute | solution.py:27
  246.7 0.8 collective-permute-done.9
  247.6 2.3 collective-permute-start.10
  249.9 2.6 collective-permute-done.10
  252.5 3.5 %collective-permute-start.11 = (f32[64,128]{1,0:T(8,128)S(1)}, f32[64,128]{1,0:T(8,128)S(1)}, u32[]{:S(2)}, u32[]{:S(2)}) collective-permute-start(f32[64,128]{1,0:T(8,128)S(1)} %add.78), channel_id=1, source_target_pairs={{0,24},{8,16},{16,8},{24,0},{1,25},{9,17},{17,9},{25,1},{2,26},{10... | collective-permute-start | bytes 98312 | tf_op jit(solution)/shard_map/ppermute | solution.py:27
  256.0 2.4 collective-permute-done.11
  258.4 1.1 broadcast_in_dim.23
  259.5 3.5 %all-to-all-start.8 = ((bf16[4,16,32,256]{3,2,1,0:T(8,128)(2,1)}), bf16[4,16,32,256]{3,2,1,0:T(8,128)(2,1)S(1)}, u32[]{:S(2)}, u32[]{:S(2)}) async-start(bf16[4,16,32,256]{3,2,1,0:T(8,128)(2,1)} %broadcast_in_dim.23), calls=%async_computation.8 | async-start | bytes 2097152 | tf_op jit(solution)/shard_map/all_to_all | solution.py:19
  263.0 3.5 %collective-permute-start.12 = (f32[64,128]{1,0:T(8,128)S(1)}, f32[64,128]{1,0:T(8,128)S(1)}, u32[]{:S(2)}, u32[]{:S(2)}) collective-permute-start(f32[64,128]{1,0:T(8,128)S(1)} %add.79), channel_id=1, source_target_pairs={{0,256},{256,0},{1,257},{257,1},{2,258},{258,2},{3,259},{259,3},{4... | collective-permute-start | bytes 98312 | tf_op jit(solution)/shard_map/ppermute | solution.py:27
  266.6 1.3 collective-permute-done.12
  267.9 3.3 %collective-permute-start.13 = (f32[64,128]{1,0:T(8,128)S(1)}, f32[64,128]{1,0:T(8,128)S(1)}, u32[]{:S(2)}, u32[]{:S(2)}) collective-permute-start(f32[64,128]{1,0:T(8,128)S(1)} %add.80), channel_id=1, source_target_pairs={{0,32},{32,0},{64,96},{96,64},{128,160},{160,128},{192,224},{224,1... | collective-permute-start | bytes 98312 | tf_op jit(solution)/shard_map/ppermute | solution.py:27
  271.3 6.8 %collective-permute-start.15 = (f32[2,32,256]{2,1,0:T(8,128)S(1)}, f32[2,32,256]{2,1,0:T(8,128)S(1)}, u32[]{:S(2)}, u32[]{:S(2)}) collective-permute-start(f32[2,32,256]{2,1,0:T(8,128)S(1)} %pad_maximum_fusion.5), channel_id=1, source_target_pairs={{0,0},{32,4},{64,8},{96,12},{128,16},{160,20},{192,24},{224,28},{2... | collective-permute-start | bytes 196616 | tf_op jit(solution)/shard_map/ppermute | solution.py:255
  278.0 2.6 collective-permute-start.14
  280.7 3.9 %collective-permute-done.14 = f32[64,128]{1,0:T(8,128)S(1)} collective-permute-done((f32[64,128]{1,0:T(8,128)S(1)}, f32[64,128]{1,0:T(8,128)S(1)}, u32[]{:S(2)}, u32[]{:S(2)}) %collective-permute-start.14) | collective-permute-done | bytes 32800 | tf_op jit(solution)/shard_map/ppermute | solution.py:27
  284.6 1.9 collective-permute-start.16
  286.6 7.3 %collective-permute-start.17 = (f32[64,128]{1,0:T(8,128)S(1)}, f32[64,128]{1,0:T(8,128)S(1)}, u32[]{:S(2)}, u32[]{:S(2)}) collective-permute-start(f32[64,128]{1,0:T(8,128)S(1)} %add.82), channel_id=1, source_target_pairs={{0,224},{32,192},{64,160},{96,128},{128,96},{160,64},{192,32},{224... | collective-permute-start | bytes 98312 | tf_op jit(solution)/shard_map/ppermute | solution.py:27
  294.5 1.0 collective-permute-done.17
  296.1 1.6 maximum_select_fusion.1
  (59 shorter events, 3.1 us)
Async XLA Ops:
  1.4 7.3 %collective-permute-start = (f32[2,32,256]{2,1,0:T(8,128)S(1)}, f32[2,32,256]{2,1,0:T(8,128)S(1)}, u32[]{:S(2)}, u32[]{:S(2)}) collective-permute-start(f32[2,32,256]{2,1,0:T(8,128)S(1)} %pad_maximum_fusion.3), channel_id=1, source_target_pairs={{0,0},{4,32},{8,64},{12,96},{16,128},{20,160},{24,192},{28,224},{3... | collective-permute-start | bytes 196616 | tf_op jit(solution)/shard_map/ppermute | solution.py:181
  8.7 26.7 %collective-permute-start.1 = (bf16[32,256]{1,0:T(8,128)(2,1)S(1)}, bf16[32,256]{1,0:T(8,128)(2,1)S(1)}, u32[]{:S(2)}, u32[]{:S(2)}) collective-permute-start(bf16[32,256]{1,0:T(8,128)(2,1)S(1)} %bitcast_convert_fusion), channel_id=1, source_target_pairs={{0,32},{32,0},{64,96},{96,64},{128,160},{160,128},{192,224},{224,1... | collective-permute-start | bytes 49160 | tf_op jit(solution)/shard_map/ppermute | solution.py:27
  12.8 37.4 %all-to-all-start = ((bf16[64,16,128]{2,1,0:T(8,128)(2,1)}), bf16[64,16,128]{2,1,0:T(8,128)(2,1)S(1)}, u32[]{:S(2)}, u32[]{:S(2)}) async-start(bf16[64,16,128]{2,1,0:T(8,128)(2,1)} %broadcast_in_dim.18), calls=%async_computation | async-start | bytes 524288 | tf_op jit(solution)/shard_map/all_to_all | solution.py:19
  35.5 7.7 %collective-permute-start.2 = (bf16[64,256]{1,0:T(8,128)(2,1)S(1)}, bf16[64,256]{1,0:T(8,128)(2,1)S(1)}, u32[]{:S(2)}, u32[]{:S(2)}) collective-permute-start(bf16[64,256]{1,0:T(8,128)(2,1)S(1)} %pad_maximum_fusion.6), channel_id=1, source_target_pairs={{0,64},{32,96},{64,0},{96,32},{128,192},{160,224},{192,128},{224,1... | collective-permute-start | bytes 98312 | tf_op jit(solution)/shard_map/ppermute | solution.py:27
  43.3 11.7 %collective-permute-start.3 = (bf16[128,256]{1,0:T(8,128)(2,1)S(1)}, bf16[128,256]{1,0:T(8,128)(2,1)S(1)}, u32[]{:S(2)}, u32[]{:S(2)}) collective-permute-start(bf16[128,256]{1,0:T(8,128)(2,1)S(1)} %pad_maximum_fusion.4), channel_id=1, source_target_pairs={{0,128},{32,160},{64,192},{96,224},{128,0},{160,32},{192,64},{224,... | collective-permute-start | bytes 196616 | tf_op jit(solution)/shard_map/ppermute | solution.py:27
  51.3 21.6 %copy-start.6 = (s32[128,128]{1,0:T(8,128)S(1)}, s32[128,128]{1,0:T(8,128)}, u32[]{:S(2)}) copy-start(s32[128,128]{1,0:T(8,128)} %param.7) | copy-start | bytes 196612
  51.3 16.8 %all-to-all-start.1 = ((bf16[4,64,16,128]{3,2,1,0:T(8,128)(2,1)}), bf16[4,64,16,128]{3,2,1,0:T(8,128)(2,1)S(1)}, u32[]{:S(2)}, u32[]{:S(2)}) async-start(bf16[4,64,16,128]{3,2,1,0:T(8,128)(2,1)} %broadcast_in_dim.19), calls=%async_computation.1 | async-start | bytes 2097152 | tf_op jit(solution)/shard_map/all_to_all | solution.py:19
  55.0 6.0 %collective-permute-start.4 = (bf16[256,256]{1,0:T(8,128)(2,1)S(1)}, bf16[256,256]{1,0:T(8,128)(2,1)S(1)}, u32[]{:S(2)}, u32[]{:S(2)}) collective-permute-start(bf16[256,256]{1,0:T(8,128)(2,1)S(1)} %pad_maximum_fusion.1), channel_id=1, source_target_pairs={{0,256},{256,0},{1,257},{257,1},{2,258},{258,2},{3,259},{259,3},{4... | collective-permute-start | bytes 393224 | tf_op jit(solution)/shard_map/ppermute | solution.py:27
  68.2 26.8 %collective-permute-start.5 = (bf16[4096,128]{1,0:T(8,128)(2,1)S(1)}, bf16[4096,128]{1,0:T(8,128)(2,1)S(1)}, u32[]{:S(2)}, u32[]{:S(2)}) collective-permute-start(bf16[4096,128]{1,0:T(8,128)(2,1)S(1)} %bitcast.88), channel_id=1, source_target_pairs={{0,4},{4,0},{1,5},{5,1},{2,6},{6,2},{3,7},{7,3},{8,12},{12,8},{9,1... | collective-permute-start | bytes 3145736 | tf_op jit(solution)/shard_map/ppermute | solution.py:27
  74.7 84.1 %all-to-all-start.3 = ((bf16[4,512,256]{2,1,0:T(8,128)(2,1)}), bf16[4,512,256]{2,1,0:T(8,128)(2,1)S(1)}, u32[]{:S(2)}, u32[]{:S(2)}) async-start(bf16[4,512,256]{2,1,0:T(8,128)(2,1)} %broadcast_in_dim.20), calls=%async_computation.3 | async-start | bytes 2097152 | tf_op jit(solution)/shard_map/all_to_all | solution.py:19
  158.7 16.0 %collective-permute-start.6 = (bf16[2048,256]{1,0:T(8,128)(2,1)S(1)}, bf16[2048,256]{1,0:T(8,128)(2,1)}, u32[]{:S(2)}, u32[]{:S(2)}) collective-permute-start(bf16[2048,256]{1,0:T(8,128)(2,1)S(1)} %bitcast.90), channel_id=1, source_target_pairs={{0,4},{4,0},{1,5},{5,1},{2,6},{6,2},{3,7},{7,3},{8,12},{12,8},{9,1... | collective-permute-start | bytes 3145736 | tf_op jit(solution)/shard_map/ppermute | solution.py:27
  169.8 11.5 %all-to-all-start.5 = ((bf16[8,32,512]{2,1,0:T(8,128)(2,1)}), bf16[8,32,512]{2,1,0:T(8,128)(2,1)}, u32[]{:S(2)}, u32[]{:S(2)}) async-start(bf16[8,32,512]{2,1,0:T(8,128)(2,1)} %get-tuple-element.29.normed_ref), calls=%async_computation.5 | async-start | bytes 524288 | tf_op jit(solution)/shard_map/all_to_all | solution.py:19
  174.7 1.9 copy-start.4
  176.6 1.1 copy-start.3
  176.7 1.6 copy-start.7
  182.2 20.1 %all-to-all-start.4 = ((bf16[8,128,256]{2,1,0:T(8,128)(2,1)}), bf16[8,128,256]{2,1,0:T(8,128)(2,1)}, u32[]{:S(2)}, u32[]{:S(2)}) async-start(bf16[8,128,256]{2,1,0:T(8,128)(2,1)} %broadcast_in_dim.21), calls=%async_computation.4 | async-start | bytes 1048576 | tf_op jit(solution)/shard_map/all_to_all | solution.py:19
  192.2 14.9 %copy-start = (bf16[96,128,128]{2,1,0:T(8,128)(2,1)S(1)}, bf16[96,128,128]{2,1,0:T(8,128)(2,1)}, u32[]{:S(2)}) copy-start(bf16[96,128,128]{2,1,0:T(8,128)(2,1)} %get-tuple-element.31.emb_ref) | copy-start | bytes 9437188
  202.3 17.0 %all-to-all-start.2 = ((bf16[8,96,512]{2,1,0:T(8,128)(2,1)}), bf16[8,96,512]{2,1,0:T(8,128)(2,1)}, u32[]{:S(2)}, u32[]{:S(2)}) async-start(bf16[8,96,512]{2,1,0:T(8,128)(2,1)} %get-tuple-element.24.normed_ref), calls=%async_computation.2 | async-start | bytes 1572864 | tf_op jit(solution)/shard_map/all_to_all | solution.py:19
  207.1 2.3 copy-start.1
  207.1 2.4 copy-start.5
  209.9 17.8 %collective-permute-start.7 = (f32[32,128]{1,0:T(8,128)S(1)}, f32[32,128]{1,0:T(8,128)S(1)}, u32[]{:S(2)}, u32[]{:S(2)}) collective-permute-start(f32[32,128]{1,0:T(8,128)S(1)} %fusion.4), channel_id=1, source_target_pairs={{0,1},{1,0},{2,3},{3,2},{4,5},{5,4},{6,7},{7,6},{8,9},{9,8},{10,11... | collective-permute-start | bytes 49160 | tf_op jit(solution)/shard_map/ppermute | solution.py:27
  221.9 12.9 %all-to-all-start.6 = ((bf16[16,32,256]{2,1,0:T(8,128)(2,1)}), bf16[16,32,256]{2,1,0:T(8,128)(2,1)S(1)}, u32[]{:S(2)}, u32[]{:S(2)}) async-start(bf16[16,32,256]{2,1,0:T(8,128)(2,1)} %bitcast.95), calls=%async_computation.6 | async-start | bytes 524288 | tf_op jit(solution)/shard_map/all_to_all | solution.py:19
  225.4 7.8 %copy-start.2 = (bf16[32,128,128]{2,1,0:T(8,128)(2,1)S(1)}, bf16[32,128,128]{2,1,0:T(8,128)(2,1)}, u32[]{:S(2)}) copy-start(bf16[32,128,128]{2,1,0:T(8,128)(2,1)} %get-tuple-element.33.emb_ref) | copy-start | bytes 3145732
  227.8 7.0 %collective-permute-start.8 = (f32[32,128]{1,0:T(8,128)S(1)}, f32[32,128]{1,0:T(8,128)S(1)}, u32[]{:S(2)}, u32[]{:S(2)}) collective-permute-start(f32[32,128]{1,0:T(8,128)S(1)} %add.72), channel_id=1, source_target_pairs={{0,3},{1,2},{2,1},{3,0},{4,7},{5,6},{6,5},{7,4},{8,11},{9,10},{10,... | collective-permute-start | bytes 49160 | tf_op jit(solution)/shard_map/ppermute | solution.py:27
  235.6 22.8 %all-to-all-start.7 = ((bf16[16,32,256]{2,1,0:T(8,128)(2,1)}), bf16[16,32,256]{2,1,0:T(8,128)(2,1)S(1)}, u32[]{:S(2)}, u32[]{:S(2)}) async-start(bf16[16,32,256]{2,1,0:T(8,128)(2,1)} %broadcast_in_dim.22), calls=%async_computation.7 | async-start | bytes 524288 | tf_op jit(solution)/shard_map/all_to_all | solution.py:19
  243.0 4.6 %collective-permute-start.9 = (f32[64,128]{1,0:T(8,128)S(1)}, f32[64,128]{1,0:T(8,128)S(1)}, u32[]{:S(2)}, u32[]{:S(2)}) collective-permute-start(f32[64,128]{1,0:T(8,128)S(1)} %pad_maximum_fusion.7), channel_id=1, source_target_pairs={{0,4},{4,0},{1,5},{5,1},{2,6},{6,2},{3,7},{7,3},{8,12},{12,8},{9,1... | collective-permute-start | bytes 98312 | tf_op jit(solution)/shard_map/ppermute | solution.py:27
  247.6 4.9 %collective-permute-start.10 = (f32[64,128]{1,0:T(8,128)S(1)}, f32[64,128]{1,0:T(8,128)S(1)}, u32[]{:S(2)}, u32[]{:S(2)}) collective-permute-start(f32[64,128]{1,0:T(8,128)S(1)} %add.77), channel_id=1, source_target_pairs={{0,8},{8,0},{16,24},{24,16},{1,9},{9,1},{17,25},{25,17},{2,10},{10... | collective-permute-start | bytes 98312 | tf_op jit(solution)/shard_map/ppermute | solution.py:27
  252.5 5.9 %collective-permute-start.11 = (f32[64,128]{1,0:T(8,128)S(1)}, f32[64,128]{1,0:T(8,128)S(1)}, u32[]{:S(2)}, u32[]{:S(2)}) collective-permute-start(f32[64,128]{1,0:T(8,128)S(1)} %add.78), channel_id=1, source_target_pairs={{0,24},{8,16},{16,8},{24,0},{1,25},{9,17},{17,9},{25,1},{2,26},{10... | collective-permute-start | bytes 98312 | tf_op jit(solution)/shard_map/ppermute | solution.py:27
  259.5 25.1 %all-to-all-start.8 = ((bf16[4,16,32,256]{3,2,1,0:T(8,128)(2,1)}), bf16[4,16,32,256]{3,2,1,0:T(8,128)(2,1)S(1)}, u32[]{:S(2)}, u32[]{:S(2)}) async-start(bf16[4,16,32,256]{3,2,1,0:T(8,128)(2,1)} %broadcast_in_dim.23), calls=%async_computation.8 | async-start | bytes 2097152 | tf_op jit(solution)/shard_map/all_to_all | solution.py:19
  263.0 4.8 %collective-permute-start.12 = (f32[64,128]{1,0:T(8,128)S(1)}, f32[64,128]{1,0:T(8,128)S(1)}, u32[]{:S(2)}, u32[]{:S(2)}) collective-permute-start(f32[64,128]{1,0:T(8,128)S(1)} %add.79), channel_id=1, source_target_pairs={{0,256},{256,0},{1,257},{257,1},{2,258},{258,2},{3,259},{259,3},{4... | collective-permute-start | bytes 98312 | tf_op jit(solution)/shard_map/ppermute | solution.py:27
  267.9 10.1 %collective-permute-start.13 = (f32[64,128]{1,0:T(8,128)S(1)}, f32[64,128]{1,0:T(8,128)S(1)}, u32[]{:S(2)}, u32[]{:S(2)}) collective-permute-start(f32[64,128]{1,0:T(8,128)S(1)} %add.80), channel_id=1, source_target_pairs={{0,32},{32,0},{64,96},{96,64},{128,160},{160,128},{192,224},{224,1... | collective-permute-start | bytes 98312 | tf_op jit(solution)/shard_map/ppermute | solution.py:27
  271.3 13.4 %collective-permute-start.15 = (f32[2,32,256]{2,1,0:T(8,128)S(1)}, f32[2,32,256]{2,1,0:T(8,128)S(1)}, u32[]{:S(2)}, u32[]{:S(2)}) collective-permute-start(f32[2,32,256]{2,1,0:T(8,128)S(1)} %pad_maximum_fusion.5), channel_id=1, source_target_pairs={{0,0},{32,4},{64,8},{96,12},{128,16},{160,20},{192,24},{224,28},{2... | collective-permute-start | bytes 196616 | tf_op jit(solution)/shard_map/ppermute | solution.py:255
  278.0 6.6 %collective-permute-start.14 = (f32[64,128]{1,0:T(8,128)S(1)}, f32[64,128]{1,0:T(8,128)S(1)}, u32[]{:S(2)}, u32[]{:S(2)}) collective-permute-start(f32[64,128]{1,0:T(8,128)S(1)} %add.81), channel_id=1, source_target_pairs={{0,96},{32,64},{64,32},{96,0},{128,224},{160,192},{192,160},{224,1... | collective-permute-start | bytes 98312 | tf_op jit(solution)/shard_map/ppermute | solution.py:27
  284.6 11.5 %collective-permute-start.16 = (bf16[2048,256]{1,0:T(8,128)(2,1)S(1)}, bf16[2048,256]{1,0:T(8,128)(2,1)S(1)}, u32[]{:S(2)}, u32[]{:S(2)}) collective-permute-start(bf16[2048,256]{1,0:T(8,128)(2,1)S(1)} %bitcast.86), channel_id=1, source_target_pairs={{0,4},{4,0},{1,5},{5,1},{2,6},{6,2},{3,7},{7,3},{8,12},{12,8},{9,1... | collective-permute-start | bytes 3145736 | tf_op jit(solution)/shard_map/ppermute | solution.py:27
  286.6 8.9 %collective-permute-start.17 = (f32[64,128]{1,0:T(8,128)S(1)}, f32[64,128]{1,0:T(8,128)S(1)}, u32[]{:S(2)}, u32[]{:S(2)}) collective-permute-start(f32[64,128]{1,0:T(8,128)S(1)} %add.82), channel_id=1, source_target_pairs={{0,224},{32,192},{64,160},{96,128},{128,96},{160,64},{192,32},{224... | collective-permute-start | bytes 98312 | tf_op jit(solution)/shard_map/ppermute | solution.py:27

commit v3 on v2

v3 whole, which is shorter than its diff:
```python
import jax
import jax.numpy as jnp
from jax import lax
from jax.experimental import pallas as pl
from jax.experimental.pallas import tpu as pltpu
from jax.sharding import Mesh
from jax.sharding import PartitionSpec as P


DP = ("zl", "y", "x", "c")
DP_MP = ("zl", "y", "x", "c", "mp")
CX = ("c", "x")
ZY = ("zl", "y")
GROUP = 32
ROWS = 8
FIRST_SHARE = 0.75


def exchange(tiles, axis):
    return lax.all_to_all(tiles, axis, split_axis=0, concat_axis=0, tiled=True)


def from_everyone(x, axis):
    return exchange(jnp.broadcast_to(x, (lax.axis_size(axis), *x.shape)), axis)


def swapped(x, axis, flip):
    return lax.ppermute(x, axis, [(i, i ^ flip) for i in range(lax.axis_size(axis))])


def over_four(x, axis):
    near, opposite, far = (
        lax.ppermute(x, axis, [(i, (i + step) % 4) for i in range(4)]) for step in (1, 2, 3)
    )
    return (x + opposite) + (near + far)


def in_parts(x):
    first = lax.reduce_precision(x, 8, 7)
    second = lax.reduce_precision(x - first, 8, 7)
    third = (x - first) - second
    top = jnp.concatenate([first, second], axis=-1)
    return jnp.concatenate([top, jnp.concatenate([third, jnp.zeros_like(third)], axis=-1)], axis=-2).astype(jnp.bfloat16)


def from_parts(parts):
    parts = parts.astype(jnp.float32)
    top, low = parts[..., :4, :], parts[..., 4:, :]
    return (top[..., :128] + top[..., 128:]) + low[..., :128]


def doubled(x, axis, flip):
    other = swapped(x, axis, flip)
    high = (lax.axis_index(axis) & flip) != 0
    return jnp.concatenate([jnp.where(high, other, x), jnp.where(high, x, other)], axis=0)


def tied(*values):
    return lax.optimization_barrier(values)


def summed(tiles):
    return tiles.astype(jnp.float32).sum(axis=0)


def forward_kernel(ids_ref, near_ref, far_ref, proj_ref, *refs):
    emb_ref, normed_ref, inv_ref, table_ref, even_ref, odd_ref, fm_ref = refs[-7:]
    rank, n_emb = proj_ref.shape
    half, width = near_ref.shape

    @pl.when(pl.program_id(0) == 0)
    def _():
        @pl.loop(0, half // 128)
        def _(i):
            at = pl.multiple_of(i * 128, 128)
            table_ref[pl.ds(at, 128), :] = near_ref[pl.ds(at, 128), :].astype(jnp.float32)
            table_ref[pl.ds(half + at, 128), :] = far_ref[pl.ds(at, 128), :].astype(jnp.float32)

    proj = proj_ref[...]
    scale = 1.0 / (rank * n_emb)
    per = normed_ref.shape[2] // n_emb
    for start in range(0, GROUP, ROWS):
        for e in range(0, ROWS, 2):
            rows_ref = (even_ref, odd_ref)[e // 2 % 2]
            for r in range(2 * n_emb):
                row = ids_ref[start + e + r // n_emb, r % n_emb]
                rows_ref[pl.ds(r, 1), :] = table_ref[pl.ds(row, 1), :]
            pair = rows_ref[...].astype(jnp.bfloat16)
            first, second = pair[:n_emb], pair[n_emb:]
            emb_ref[start + e] = first
            emb_ref[start + e + 1] = second
            compressed = jnp.dot(
                proj, jnp.concatenate([first, second], axis=1), preferred_element_type=jnp.float32
            ).astype(jnp.bfloat16)
            compressed = jnp.concatenate([compressed[:, :width], compressed[:, width:]], axis=0)
            fm = lax.dot_general(compressed, pair, (((1,), (1,)), ((), ())), preferred_element_type=jnp.float32)
            fm_ref[pl.ds(e * rank, rank), :] = fm[:rank, :n_emb]
            fm_ref[pl.ds((e + 1) * rank, rank), :] = fm[rank:, n_emb:]
        parts = [fm_ref[pl.ds(k, ROWS, stride=rank), :] for k in range(rank)]
        mean = jnp.sum(sum(parts), axis=1, keepdims=True) * scale
        parts = [p - mean for p in parts]
        var = jnp.sum(sum(p * p for p in parts), axis=1, keepdims=True) * scale
        inv = 1.0 / jnp.sqrt(var + 1.0)
        for k in range(rank):
            at = k % per * n_emb
            normed_ref[k // per, start : start + ROWS, at : at + n_emb] = (parts[k] * inv).astype(jnp.bfloat16)
        inv_ref[start : start + ROWS] = jnp.broadcast_to(inv, (ROWS, inv_ref.shape[1]))


def forward_features(ids, near, far, projection, blocks, start, count, embedded=None):
    examples, n_emb = ids.shape
    half, width = near.shape
    rank = projection.shape[1]
    columns = rank * n_emb // blocks
    skip = start // GROUP
    before = () if embedded is None else (embedded,)
    return pl.pallas_call(
        forward_kernel,
        grid=(count // GROUP,),
        in_specs=[
            pl.BlockSpec((GROUP, n_emb), lambda g: (g + skip, 0), memory_space=pltpu.SMEM),
            pl.BlockSpec((half, width), lambda g: (0, 0)),
            pl.BlockSpec((half, width), lambda g: (0, 0)),
            pl.BlockSpec((rank, n_emb), lambda g: (0, 0)),
            *(pl.BlockSpec(memory_space=pl.ANY) for _ in before),
        ],
        out_specs=[
            pl.BlockSpec((GROUP, n_emb, width), lambda g: (g + skip, 0, 0)),
            pl.BlockSpec((blocks, GROUP, columns), lambda g: (0, g, 0)),
            pl.BlockSpec((GROUP, 128), lambda g: (g, 0)),
        ],
        out_shape=[
            jax.ShapeDtypeStruct((examples, n_emb, width), jnp.bfloat16),
            jax.ShapeDtypeStruct((blocks, count, columns), jnp.bfloat16),
            jax.ShapeDtypeStruct((count, 128), jnp.float32),
        ],
        scratch_shapes=[
            pltpu.VMEM((2 * half, width), jnp.float32),
            pltpu.VMEM((2 * n_emb, width), jnp.float32),
            pltpu.VMEM((2 * n_emb, width), jnp.float32),
            pltpu.VMEM((ROWS * rank, n_emb), jnp.float32),
        ],
        input_output_aliases={4: 0} if before else {},
        cost_estimate=pl.CostEstimate(
            flops=100_000_000 * count,
            bytes_accessed=half * width * 4 + count * n_emb * width * 2,
            transcendentals=0,
        ),
        name="fm_forward",
    )(ids, near, far, projection.T, *before)


def backward_kernel(grad_ref, normed_ref, inv_ref, emb_ref, *refs):
    back_ref, fm_grad_ref = refs[-2:]
    n_emb = emb_ref.shape[1]
    rank, width = back_ref.shape[1:]
    per = normed_ref.shape[2] // n_emb
    scale = 1.0 / (rank * n_emb)
    for start in range(0, GROUP, ROWS):
        rows = slice(start, start + ROWS)
        grads = [grad_ref[rows, k * n_emb : (k + 1) * n_emb] for k in range(rank)]
        normed = [
            normed_ref[k // per, rows, k % per * n_emb : (k % per + 1) * n_emb].astype(jnp.float32)
            for k in range(rank)
        ]
        mean = jnp.sum(sum(grads), axis=1, keepdims=True) * scale
        along = jnp.sum(sum(g * x for g, x in zip(grads, normed)), axis=1, keepdims=True) * scale
        inv = inv_ref[rows, :1]
        for k in range(rank):
            fm_grad_ref[pl.ds(k, ROWS, stride=rank), :] = (grads[k] - mean - normed[k] * along) * inv
        for e in range(0, ROWS, 2):
            fm_grad = fm_grad_ref[pl.ds(e * rank, 2 * rank), :].astype(jnp.bfloat16)
            pair = jnp.concatenate([emb_ref[start + e], emb_ref[start + e + 1]], axis=1)
            back = jnp.dot(fm_grad, pair, preferred_element_type=jnp.float32).astype(jnp.bfloat16)
            back_ref[start + e] = back[:rank, :width]
            back_ref[start + e + 1] = back[rank:, width:]


def backward_features(normed_grad, normed, inv_scale, embedded, start, back=None):
    examples, n_emb, width = embedded.shape
    blocks, count, columns = normed.shape
    rank = blocks * columns // n_emb
    skip = start // GROUP
    before = () if back is None else (back,)
    return pl.pallas_call(
        backward_kernel,
        grid=(count // GROUP,),
        in_specs=[
            pl.BlockSpec((GROUP, rank * n_emb), lambda g: (g + skip, 0)),
            pl.BlockSpec((blocks, GROUP, columns), lambda g: (0, g, 0)),
            pl.BlockSpec((GROUP, 128), lambda g: (g, 0)),
            pl.BlockSpec((GROUP, n_emb, width), lambda g: (g + skip, 0, 0)),
            *(pl.BlockSpec(memory_space=pl.ANY) for _ in before),
        ],
        out_specs=pl.BlockSpec((GROUP, rank, width), lambda g: (g + skip, 0, 0)),
        out_shape=jax.ShapeDtypeStruct((examples, rank, width), jnp.bfloat16),
        scratch_shapes=[pltpu.VMEM((ROWS * rank, n_emb), jnp.float32)],
        input_output_aliases={4: 0} if before else {},
        cost_estimate=pl.CostEstimate(
            flops=30_000_000 * count,
            bytes_accessed=count * n_emb * (width * 2 + rank * 8),
            transcendentals=0,
        ),
        name="fm_backward",
    )(normed_grad, normed, inv_scale, embedded, *before)


def both_halves(half):
    other = swapped(half, "c", 1)
    high = lax.axis_index("c") == 1
    return jnp.where(high, jnp.stack([other, half]), jnp.stack([half, other])).reshape(-1, *half.shape[1:])


def per_device(feature_ids, emb_table, factor_machine_projection, mlp_weight, momentum, hidden_grad, lcb_grad):
    mp, zl, y, x, c = (lax.axis_size(a) for a in ("mp", "zl", "y", "x", "c"))
    own = emb_table.shape[0]
    rank = factor_machine_projection.shape[1]
    examples, hidden = hidden_grad.shape

    to_worker = []
    for block in range(zl * y * x * c):
        cx, zy = divmod(block, zl * y)
        at_c, at_x = divmod(cx, x)
        to_worker.append((block, (zy * x + at_x) * c + at_c))
    to_owner = [(worker, owner) for owner, worker in to_worker]

    width = emb_table.shape[1]
    table = from_everyone(emb_table, ("mp", "zl")).reshape(-1, width)
    state = lax.ppermute(jnp.stack([mlp_weight, momentum]), DP, to_worker)
    weight_rows, momentum_rows = state[0], state[1]
    weights = weight_rows.astype(jnp.bfloat16)
    near_rows = table.shape[0]
    table = from_everyone(jnp.concatenate([table, weights[:, :width], weights[:, width:]], axis=0), "y")
    weights = table[:, near_rows:].reshape(y, hidden // width, -1, width)
    weights = jnp.swapaxes(weights, 1, 2).reshape(-1, hidden)
    weights = doubled(weights, "zl", 1)
    table = from_everyone(table[:, :near_rows], "x").reshape(-1, width)
    weights, table = tied(weights, table)
    table_far = swapped(table, "c", 1)
    weights = from_everyone(weights, "x").reshape(-1, hidden)
    owner, row = lax.div(feature_ids, own), lax.rem(feature_ids, own)
    owner, at_mp = lax.div(owner, mp), lax.rem(owner, mp)
    owner, at_c = lax.div(owner, c), lax.rem(owner, c)
    owner, at_x = lax.div(owner, x), lax.rem(owner, x)
    at_zl, at_y = lax.div(owner, y), lax.rem(owner, y)
    ids = (((((at_c ^ lax.axis_index("c")) * x + at_x) * y + at_y) * mp + at_mp) * zl + at_zl) * own + row

    blocks = 2 * c * x
    cut = int(examples * FIRST_SHARE)
    shares = ((0, cut), (cut, examples - cut))
    embedded, normed_a, inv_a = forward_features(ids, table, table_far, factor_machine_projection, blocks, *shares[0])
    weights = both_halves(weights)
    embedded, normed_b, inv_b = forward_features(
        ids, table, table_far, factor_machine_projection, blocks, *shares[1], embedded
    )
    columns_a = exchange(normed_a.reshape(c * x, 2 * cut, -1), CX)

    tiled_weights = weights.reshape(blocks, -1, hidden)
    preact = jnp.concatenate(
        [
            jnp.einsum("jbk,jkn->bn", normed, tiled_weights, preferred_element_type=jnp.float32)
            for normed in (normed_a, normed_b)
        ],
        axis=0,
    )
    sigmoid_pre = jax.nn.sigmoid(preact)
    preact_grad = (
        hidden_grad.astype(jnp.float32) * sigmoid_pre * (1.0 + preact * (1.0 - sigmoid_pre))
    ).astype(jnp.bfloat16)
    group_grad = exchange(
        jnp.concatenate(
            [
                jnp.broadcast_to(preact_grad, (c * x, examples, hidden)),
                normed_b.reshape(c * x, -1, hidden),
            ],
            axis=1,
        ),
        CX,
    )

    normed_part = lax.dot_general(preact_grad, weights, (((1,), (1,)), ((), ())), preferred_element_type=jnp.float32)
    back = backward_features(normed_part, normed_a, inv_a, embedded, 0)
    back = backward_features(normed_part, normed_b, inv_b, embedded, cut, back)
    proj_part = jnp.einsum("bqh,blh->ql", back, embedded, preferred_element_type=jnp.float32)
    lcb_part = jnp.einsum("bld,bnd->ln", lcb_grad, embedded, preferred_element_type=jnp.float32)
    both = jnp.concatenate([proj_part, lcb_part], axis=0)

    weight_grad = 0.0
    columns_b = group_grad[:, examples:]
    for part, (start, count) in zip((columns_a, columns_b), shares):
        weight_grad += jnp.einsum(
            "shbk,sbn->hkn",
            part.reshape(c * x, 2, count, -1),
            group_grad[:, start : start + count],
            preferred_element_type=jnp.float32,
        )
    arrived = exchange(
        jnp.concatenate(
            [
                weight_grad.astype(jnp.bfloat16).reshape(zl * y, -1, hidden),
                in_parts(both.reshape(zl * y, -1, both.shape[1])),
            ],
            axis=1,
        ),
        ZY,
    )
    own_rows = weight_rows.shape[0]
    both = from_parts(summed(arrived[:, own_rows:]))
    new_momentum = 0.9 * momentum_rows + summed(arrived[:, :own_rows])
    new_weight = weight_rows - 0.01 * new_momentum
    arrived = from_everyone(jnp.concatenate([new_weight.astype(jnp.bfloat16), in_parts(both)], axis=0), ZY)
    next_weight = from_everyone(arrived[:, :own_rows], "x").reshape(-1, hidden)
    both = from_parts(arrived[:, own_rows:]).reshape(-1, both.shape[1])
    state = lax.ppermute(jnp.stack([new_weight, new_momentum]), DP, to_owner)
    proj_sum = over_four(both[:rank], "mp")
    both = over_four(jnp.concatenate([proj_sum, both[rank:]], axis=0), "x")
    next_weight, both, state = tied(next_weight, both, state)
    next_weight = both_halves(next_weight)
    both += swapped(both, "c", 1)
    return (state[0], state[1], next_weight, both[:rank].T, both[rank:].T)


def solution(mesh):
    torus = Mesh(mesh.devices.reshape(2, 8, 4, 2, mesh.shape["mp"]), DP_MP)
    placed = (
        P(DP, None),
        P(DP_MP, None),
        P(),
        P(DP, "mp"),
        P(DP, "mp"),
        P(DP, "mp"),
        P(DP, "mp", None),
    )

    return jax.shard_map(
        per_device,
        mesh=torus,
        in_specs=placed,
        out_specs=(P(DP, "mp"), P(DP, "mp"), P(None, "mp"), P(), P(None, "mp")),
        check_vma=False,
    )
```

time: 301 us -> 239 us (0.79)
  the two profiles are of different devices: /device:TPU:1 before, /device:TPU:5 now
where the time goes in v3:
time: 239 us; the launch traced here: 238 us
  starting transfers between devices  99.6 us (42%)
  blocking collectives  42.8 us (18%)
  waiting for transfers between devices  33.2 us (14%)
  Pallas kernels  31.9 us (13%)
  matrix products  14.4 us (6%)
  local copies, waits for them, and re-layouts  8.21 us (3%)
  other arithmetic  6.52 us (3%)
    all_to_all x6, starting transfers between devices, exchange(): return lax.all_to_all(tiles, axis, split_axis=0, concat_axis=0, tiled=True)  43.1 us
    all_to_all x3, blocking collectives, exchange(): return lax.all_to_all(tiles, axis, split_axis=0, concat_axis=0, tiled=True)  42.8 us
    all_to_all x6, waiting for transfers between devices, exchange(): return lax.all_to_all(tiles, axis, split_axis=0, concat_axis=0, tiled=True)  26.6 us
    pallas_call x2, Pallas kernels, forward_features(): pl.pallas_call(forward_kernel, grid=(count // GROUP,), in_specs=[pl.Block...  23.6 us
    ppermute x6, starting transfers between devices, over_four(): lax.ppermute(x, axis, [(i, (i + step) % 4) for i in range(4)])  19.9 us
    ppermute x5, starting transfers between devices, swapped(): lax.ppermute(x, axis, [(i, i ^ flip) for i in range(lax.axis_size(axis))])  19.7 us
    ppermute x1, starting transfers between devices, per_device(): state = lax.ppermute(jnp.stack([new_weight, new_momentum]), DP, to_owner)  9.73 us
    pallas_call x2, Pallas kernels, backward_features(): pl.pallas_call(backward_kernel, grid=(count // GROUP,), in_specs=[pl.Bloc...  8.26 us
  transfers between devices with their start and end apart: 19, of which 7 were waited for; matrix products, arithmetic and copies ran while one was open for 7% of the time, Pallas kernels for 13%

profile of v3, /device:TPU:5, one launch (start us, length us, event | category | flops | bytes accessed | tf_op | source)
XLA Modules:
  0.0 237.7 jit_solution(15483237633503558227)
XLA Ops:
  0.6 0.0 copy-start
  0.6 0.9 pad_maximum_fusion.3
  1.5 7.2 %collective-permute-start = (f32[2,32,256]{2,1,0:T(8,128)S(1)}, f32[2,32,256]{2,1,0:T(8,128)S(1)}, u32[]{:S(2)}, u32[]{:S(2)}) collective-permute-start(f32[2,32,256]{2,1,0:T(8,128)S(1)} %pad_maximum_fusion.3), channel_id=1, source_target_pairs={{0,0},{4,32},{8,64},{12,96},{16,128},{20,160},{24,192},{28,224},{3... | collective-permute-start | bytes 196616 | tf_op jit(solution)/shard_map/ppermute | solution.py:229
  8.7 1.3 broadcast_in_dim.23
  10.0 10.0 %all-to-all-start = ((bf16[8,16,128]{2,1,0:T(8,128)(2,1)}), bf16[8,16,128]{2,1,0:T(8,128)(2,1)S(1)}, u32[]{:S(2)}, u32[]{:S(2)}) async-start(bf16[8,16,128]{2,1,0:T(8,128)(2,1)} %broadcast_in_dim.23), calls=%async_computation | async-start | bytes 65536 | tf_op jit(solution)/shard_map/all_to_all | solution.py:20
  20.0 0.0 collective-permute-done
  20.0 6.8 %all-to-all-done = bf16[8,16,128]{2,1,0:T(8,128)(2,1)S(1)} async-done(((bf16[8,16,128]{2,1,0:T(8,128)(2,1)}), bf16[8,16,128]{2,1,0:T(8,128)(2,1)S(1)}, u32[]{:S(2)}, u32[]{:S(2)}) %all-to-all-start) | async-done | bytes 32800 | tf_op jit(solution)/shard_map/all_to_all | solution.py:20
  26.9 0.1 broadcast_in_dim.24
  27.0 14.8 %all_to_all.45 = bf16[8,192,128]{2,1,0:T(8,128)(2,1)S(1)} all-to-all(bf16[8,192,128]{2,1,0:T(8,128)(2,1)S(1)} %broadcast_in_dim.24), channel_id=1, replica_groups=mesh['zl'=2,'y'=8,'x'=4,'c'=2,'mp'=4] {'y'}, dimensions={0} | all-to-all | bytes 786432 | tf_op jit(solution)/shard_map/all_to_all | solution.py:20
  41.7 1.2 broadcast_in_dim.25
  42.9 8.7 %all-to-all-start.2 = ((bf16[4,8,128,128]{3,2,1,0:T(8,128)(2,1)}), bf16[4,8,128,128]{3,2,1,0:T(8,128)(2,1)}, u32[]{:S(2)}, u32[]{:S(2)}) async-start(bf16[4,8,128,128]{3,2,1,0:T(8,128)(2,1)} %broadcast_in_dim.25), calls=%async_computation.2 | async-start | bytes 2097152 | tf_op jit(solution)/shard_map/all_to_all | solution.py:20
  51.6 0.1 copy.17
  51.8 2.2 collective-permute-start.1
  54.0 3.9 %collective-permute-done.1 = bf16[256,256]{1,0:T(8,128)(2,1)S(1)} collective-permute-done((bf16[256,256]{1,0:T(8,128)(2,1)S(1)}, bf16[256,256]{1,0:T(8,128)(2,1)S(1)}, u32[]{:S(2)}, u32[]{:S(2)}) %collective-permute-start.1) | collective-permute-done | bytes 131104 | tf_op jit(solution)/shard_map/ppermute | solution.py:28
  57.9 0.0 copy-start.5
  57.9 4.2 %all-to-all-done.2 = bf16[4,8,128,128]{3,2,1,0:T(8,128)(2,1)} async-done(((bf16[4,8,128,128]{3,2,1,0:T(8,128)(2,1)}), bf16[4,8,128,128]{3,2,1,0:T(8,128)(2,1)}, u32[]{:S(2)}, u32[]{:S(2)}) %all-to-all-start.2) | async-done | bytes 1048608 | tf_op jit(solution)/shard_map/all_to_all | solution.py:20
  62.2 4.8 %collective-permute-start.2 = (bf16[4096,128]{1,0:T(8,128)(2,1)}, bf16[4096,128]{1,0:T(8,128)(2,1)}, u32[]{:S(2)}, u32[]{:S(2)}) collective-permute-start(bf16[4096,128]{1,0:T(8,128)(2,1)} %bitcast.7.near_ref), channel_id=1, source_target_pairs={{0,4},{4,0},{1,5},{5,1},{2,6},{6,2},{3,7},{7,3},{8,12},{12,8},{9,1... | collective-permute-start | bytes 3145736 | tf_op jit(solution)/shard_map/ppermute | solution.py:28
  67.0 1.0 broadcast_in_dim.26
  68.0 6.2 %all-to-all-start.4 = ((bf16[4,512,256]{2,1,0:T(8,128)(2,1)}), bf16[4,512,256]{2,1,0:T(8,128)(2,1)S(1)}, u32[]{:S(2)}, u32[]{:S(2)}) async-start(bf16[4,512,256]{2,1,0:T(8,128)(2,1)} %broadcast_in_dim.26), calls=%async_computation.4 | async-start | bytes 2097152 | tf_op jit(solution)/shard_map/all_to_all | solution.py:20
  74.2 0.8 fusion.14.ids_ref
  75.0 11.8 %all-to-all-done.4 = bf16[4,512,256]{2,1,0:T(8,128)(2,1)S(1)} async-done(((bf16[4,512,256]{2,1,0:T(8,128)(2,1)}), bf16[4,512,256]{2,1,0:T(8,128)(2,1)S(1)}, u32[]{:S(2)}, u32[]{:S(2)}) %all-to-all-start.4) | async-done | bytes 1048608 | tf_op jit(solution)/shard_map/all_to_all | solution.py:20
  86.7 2.7 %collective-permute-start.3 = (bf16[2048,256]{1,0:T(8,128)(2,1)S(1)}, bf16[2048,256]{1,0:T(8,128)(2,1)S(1)}, u32[]{:S(2)}, u32[]{:S(2)}) collective-permute-start(bf16[2048,256]{1,0:T(8,128)(2,1)S(1)} %bitcast.101), channel_id=1, source_target_pairs={{0,4},{4,0},{1,5},{5,1},{2,6},{6,2},{3,7},{7,3},{8,12},{12,8},{9,1... | collective-permute-start | bytes 3145736 | tf_op jit(solution)/shard_map/ppermute | solution.py:28
  89.5 17.3 %fm_forward.2 = (bf16[128,128,128]{2,1,0:T(8,128)(2,1)}, bf16[16,96,256]{2,1,0:T(8,128)(2,1)}, f32[96,128]{1,0:T(8,128)}) custom-call(s32[128,128]{1,0:T(8,128)} %fusion.14.ids_ref, bf16[4096,128]{1,0:T(8,128)(2,1)} %bitcast.7.near_ref, bf16[4096,128]{1,0:T(8,128)(2,1)} %collective-permute-done.2.far_ref, bf16[32,128]{1,0:T(8,128)(2,1)} %bitcast.124), custom_call_target="tpu_custom_call" | custom-call | flops 9600000000 | bytes 5242880 | tf_op jit(solution)/shard_map/fm_forward/pallas_call | solution.py:117
  106.7 6.4 %fm_forward.3 = (bf16[128,128,128]{2,1,0:T(8,128)(2,1)}, bf16[16,32,256]{2,1,0:T(8,128)(2,1)}, f32[32,128]{1,0:T(8,128)}) custom-call(s32[128,128]{1,0:T(8,128)} %fusion.14.ids_ref, bf16[4096,128]{1,0:T(8,128)(2,1)} %bitcast.7.near_ref, bf16[4096,128]{1,0:T(8,128)(2,1)} %collective-permute-done.2.far_ref, ...), custom_call_target="tpu_custom_call", output_to_operand_aliasing={{0}: (4, {})} | custom-call | flops 3200000000 | bytes 3145728 | tf_op jit(solution)/shard_map/fm_forward/pallas_call | solution.py:117
  113.1 3.7 %convolution_bitcast_fusion.4 = f32[32,128]{1,0:T(8,128)S(1)} fusion(bf16[128,128,128]{2,1,0:T(8,128)(2,1)} %get-tuple-element.22.emb_ref, bf16[128,32,128]{2,1,0:T(8,128)(2,1)S(1)} %copy-done), kind=kOutput, calls=%fused_computation.8 | convolution fusion | flops 134217728 | bytes 5259264 | tf_op jit(solution)/shard_map/bld,bnd->ln/dot_general | solution.py:285
  116.8 0.0 collective-permute-done.3
  116.9 1.0 copy-done.4
  117.9 1.9 maximum_select_fusion
  119.8 0.0 copy-start.6
  119.8 0.5 convolution_bitcast_fusion.3
  120.2 1.6 convolution_bitcast_fusion.2
  121.9 0.1 multiply_convert_fusion
  122.0 1.0 pad_maximum_fusion
  123.0 6.7 %all-to-all-start.5 = ((bf16[8,192,256]{2,1,0:T(8,128)(2,1)}), bf16[8,192,256]{2,1,0:T(8,128)(2,1)}, u32[]{:S(2)}, u32[]{:S(2)}) async-start(bf16[8,192,256]{2,1,0:T(8,128)(2,1)} %pad_maximum_fusion), calls=%async_computation.5 | async-start | bytes 1572864 | tf_op jit(solution)/shard_map/all_to_all | solution.py:20
  129.7 2.1 fusion.26.grad_ref
  131.8 5.3 %fm_backward.2.refs_0_ = bf16[128,32,128]{2,1,0:T(8,128)(2,1)} custom-call(f32[128,4096]{1,0:T(8,128)} %fusion.26.grad_ref, bf16[16,96,256]{2,1,0:T(8,128)(2,1)} %get-tuple-element.17.normed_ref, f32[96,128]{1,0:T(8,128)} %get-tuple-element.23.inv_ref, bf16[128,128,128]{2,1,0:T(8,128)(2,1)} %get-tuple-element.22.emb_ref), custom_call_target="tpu_custom_call" | custom-call | flops 2880000000 | bytes 6291456 | tf_op jit(solution)/shard_map/fm_backward/pallas_call | solution.py:185
  137.1 2.9 %fm_backward.3 = bf16[128,32,128]{2,1,0:T(8,128)(2,1)} custom-call(f32[128,4096]{1,0:T(8,128)} %fusion.26.grad_ref, bf16[16,32,256]{2,1,0:T(8,128)(2,1)} %get-tuple-element.20.normed_ref, f32[32,128]{1,0:T(8,128)} %get-tuple-element.21.inv_ref, bf16[128,128,128]{2,1,0:T(8,128)(2,1)} %get-tuple-element.22.emb_ref, ...), custom_call_target="tpu_custom_call", output_to_operand_aliasing={{}: (4, {})} | custom-call | flops 960000000 | bytes 2097152 | tf_op jit(solution)/shard_map/fm_backward/pallas_call | solution.py:185
  140.1 0.0 all-to-all-done.5
  140.1 5.6 %all-to-all-start.3 = ((bf16[8,192,256]{2,1,0:T(8,128)(2,1)}), bf16[8,192,256]{2,1,0:T(8,128)(2,1)S(1)}, u32[]{:S(2)}, u32[]{:S(2)}) async-start(bf16[8,192,256]{2,1,0:T(8,128)(2,1)} %bitcast.9), calls=%async_computation.3 | async-start | bytes 1572864 | tf_op jit(solution)/shard_map/all_to_all | solution.py:20
  145.7 3.9 %convolution_bitcast_fusion.5 = f32[32,128]{1,0:T(8,128)S(1)} fusion(bf16[128,32,128]{2,1,0:T(8,128)(2,1)} %fm_backward.3, bf16[128,128,128]{2,1,0:T(8,128)(2,1)} %get-tuple-element.22.emb_ref), kind=kOutput, calls=%fused_computation.9 | convolution fusion | flops 134217728 | bytes 5259264 | tf_op jit(solution)/shard_map/bqh,blh->ql/dot_general | solution.py:284
  149.7 1.0 slice.125
  150.7 1.2 convolution_bitcast_fusion
  151.9 3.8 %all-to-all-done.3 = bf16[8,192,256]{2,1,0:T(8,128)(2,1)S(1)} async-done(((bf16[8,192,256]{2,1,0:T(8,128)(2,1)}), bf16[8,192,256]{2,1,0:T(8,128)(2,1)S(1)}, u32[]{:S(2)}, u32[]{:S(2)}) %all-to-all-start.3) | async-done | bytes 786464 | tf_op jit(solution)/shard_map/all_to_all | solution.py:20
  155.7 1.4 fusion.1
  157.1 12.7 %all_to_all.46 = bf16[16,40,256]{2,1,0:T(8,128)(2,1)S(1)} all-to-all(bf16[16,40,256]{2,1,0:T(8,128)(2,1)S(1)} %fusion.3), channel_id=1, replica_groups=mesh['zl'=2,'y'=8,'x'=4,'c'=2,'mp'=4] {'zl','y'}, dimensions={0} | all-to-all | bytes 655360 | tf_op jit(solution)/shard_map/all_to_all | solution.py:20
  170.0 15.3 %all_to_all.47 = bf16[16,40,256]{2,1,0:T(8,128)(2,1)S(1)} all-to-all(bf16[16,40,256]{2,1,0:T(8,128)(2,1)S(1)} %broadcast_in_dim.28), channel_id=1, replica_groups=mesh['zl'=2,'y'=8,'x'=4,'c'=2,'mp'=4] {'zl','y'}, dimensions={0} | all-to-all | bytes 655360 | tf_op jit(solution)/shard_map/all_to_all | solution.py:20
  185.3 2.0 collective-permute-start.5
  187.4 5.3 %collective-permute-start.6 = (f32[32,128]{1,0:T(8,128)S(1)}, f32[32,128]{1,0:T(8,128)S(1)}, u32[]{:S(2)}, u32[]{:S(2)}) collective-permute-start(f32[32,128]{1,0:T(8,128)S(1)} %bitcast.119), channel_id=1, source_target_pairs={{0,3},{1,0},{2,1},{3,2},{4,7},{5,4},{6,5},{7,6},{8,11},{9,8},{10,9... | collective-permute-start | bytes 49160 | tf_op jit(solution)/shard_map/ppermute | solution.py:33
  192.8 3.1 %collective-permute-start.4 = (f32[32,128]{1,0:T(8,128)S(1)}, f32[32,128]{1,0:T(8,128)S(1)}, u32[]{:S(2)}, u32[]{:S(2)}) collective-permute-start(f32[32,128]{1,0:T(8,128)S(1)} %bitcast.120), channel_id=1, source_target_pairs={{0,2},{1,3},{2,0},{3,1},{4,6},{5,7},{6,4},{7,5},{8,10},{9,11},{10,... | collective-permute-start | bytes 49160 | tf_op jit(solution)/shard_map/ppermute | solution.py:33
  195.9 1.1 broadcast_in_dim.29
  197.0 5.9 %all-to-all-start.8 = ((bf16[4,16,32,256]{3,2,1,0:T(8,128)(2,1)}), bf16[4,16,32,256]{3,2,1,0:T(8,128)(2,1)S(1)}, u32[]{:S(2)}, u32[]{:S(2)}) async-start(bf16[4,16,32,256]{3,2,1,0:T(8,128)(2,1)} %broadcast_in_dim.29), calls=%async_computation.8 | async-start | bytes 2097152 | tf_op jit(solution)/shard_map/all_to_all | solution.py:20
  202.9 0.0 collective-permute-done.4
  202.9 2.8 %collective-permute-start.8 = (f32[64,128]{1,0:T(8,128)S(1)}, f32[64,128]{1,0:T(8,128)S(1)}, u32[]{:S(2)}, u32[]{:S(2)}) collective-permute-start(f32[64,128]{1,0:T(8,128)S(1)} %pad_maximum_fusion.7), channel_id=1, source_target_pairs={{0,8},{8,16},{16,24},{24,0},{1,9},{9,17},{17,25},{25,1},{2,10},{10... | collective-permute-start | bytes 98312 | tf_op jit(solution)/shard_map/ppermute | solution.py:33
  205.7 2.5 %collective-permute-start.9 = (f32[64,128]{1,0:T(8,128)S(1)}, f32[64,128]{1,0:T(8,128)S(1)}, u32[]{:S(2)}, u32[]{:S(2)}) collective-permute-start(f32[64,128]{1,0:T(8,128)S(1)} %pad_maximum_fusion.7), channel_id=1, source_target_pairs={{0,24},{8,0},{16,8},{24,16},{1,25},{9,1},{17,9},{25,17},{2,26},{10... | collective-permute-start | bytes 98312 | tf_op jit(solution)/shard_map/ppermute | solution.py:33
  208.2 4.2 %collective-permute-start.7 = (f32[64,128]{1,0:T(8,128)S(1)}, f32[64,128]{1,0:T(8,128)S(1)}, u32[]{:S(2)}, u32[]{:S(2)}) collective-permute-start(f32[64,128]{1,0:T(8,128)S(1)} %pad_maximum_fusion.7), channel_id=1, source_target_pairs={{0,16},{8,24},{16,0},{24,8},{1,17},{9,25},{17,1},{25,9},{2,18},{10... | collective-permute-start | bytes 98312 | tf_op jit(solution)/shard_map/ppermute | solution.py:33
  212.4 9.7 %collective-permute-start.10 = (f32[2,32,256]{2,1,0:T(8,128)S(1)}, f32[2,32,256]{2,1,0:T(8,128)S(1)}, u32[]{:S(2)}, u32[]{:S(2)}) collective-permute-start(f32[2,32,256]{2,1,0:T(8,128)S(1)} %pad_maximum_fusion.4), channel_id=1, source_target_pairs={{0,0},{32,4},{64,8},{96,12},{128,16},{160,20},{192,24},{224,28},{2... | collective-permute-start | bytes 196616 | tf_op jit(solution)/shard_map/ppermute | solution.py:314
  222.2 0.0 collective-permute-done.8
  222.2 2.1 collective-permute-done.10
  224.3 8.0 %collective-permute-start.11 = (bf16[2048,256]{1,0:T(8,128)(2,1)S(1)}, bf16[2048,256]{1,0:T(8,128)(2,1)S(1)}, u32[]{:S(2)}, u32[]{:S(2)}) collective-permute-start(bf16[2048,256]{1,0:T(8,128)(2,1)S(1)} %bitcast.99), channel_id=1, source_target_pairs={{0,4},{4,0},{1,5},{5,1},{2,6},{6,2},{3,7},{7,3},{8,12},{12,8},{9,1... | collective-permute-start | bytes 3145736 | tf_op jit(solution)/shard_map/ppermute | solution.py:28
  232.3 1.9 collective-permute-start.12
  234.3 0.6 slice_bitcast_fusion.4
  234.9 0.5 collective-permute-done.12
  235.4 0.6 slice_bitcast_fusion.6
  236.1 1.6 maximum_select_fusion.1
  (46 shorter events, 0.5 us)
Async XLA Ops:
  0.6 112.5 %copy-start = (bf16[128,32,128]{2,1,0:T(8,128)(2,1)S(1)}, bf16[128,32,128]{2,1,0:T(8,128)(2,1)}, u32[]{:S(2)}) copy-start(bf16[128,32,128]{2,1,0:T(8,128)(2,1)} %param.13) | copy-start | bytes 3145732
  1.5 18.5 %collective-permute-start = (f32[2,32,256]{2,1,0:T(8,128)S(1)}, f32[2,32,256]{2,1,0:T(8,128)S(1)}, u32[]{:S(2)}, u32[]{:S(2)}) collective-permute-start(f32[2,32,256]{2,1,0:T(8,128)S(1)} %pad_maximum_fusion.3), channel_id=1, source_target_pairs={{0,0},{4,32},{8,64},{12,96},{16,128},{20,160},{24,192},{28,224},{3... | collective-permute-start | bytes 196616 | tf_op jit(solution)/shard_map/ppermute | solution.py:229
  10.0 16.9 %all-to-all-start = ((bf16[8,16,128]{2,1,0:T(8,128)(2,1)}), bf16[8,16,128]{2,1,0:T(8,128)(2,1)S(1)}, u32[]{:S(2)}, u32[]{:S(2)}) async-start(bf16[8,16,128]{2,1,0:T(8,128)(2,1)} %broadcast_in_dim.23), calls=%async_computation | async-start | bytes 65536 | tf_op jit(solution)/shard_map/all_to_all | solution.py:20
  42.9 19.2 %all-to-all-start.2 = ((bf16[4,8,128,128]{3,2,1,0:T(8,128)(2,1)}), bf16[4,8,128,128]{3,2,1,0:T(8,128)(2,1)}, u32[]{:S(2)}, u32[]{:S(2)}) async-start(bf16[4,8,128,128]{3,2,1,0:T(8,128)(2,1)} %broadcast_in_dim.25), calls=%async_computation.2 | async-start | bytes 2097152 | tf_op jit(solution)/shard_map/all_to_all | solution.py:20
  51.8 6.1 %collective-permute-start.1 = (bf16[256,256]{1,0:T(8,128)(2,1)S(1)}, bf16[256,256]{1,0:T(8,128)(2,1)S(1)}, u32[]{:S(2)}, u32[]{:S(2)}) collective-permute-start(bf16[256,256]{1,0:T(8,128)(2,1)S(1)} %bitcast.116), channel_id=1, source_target_pairs={{0,256},{256,0},{1,257},{257,1},{2,258},{258,2},{3,259},{259,3},{4... | collective-permute-start | bytes 393224 | tf_op jit(solution)/shard_map/ppermute | solution.py:28
  57.9 16.3 %copy-start.5 = (s32[128,128]{1,0:T(8,128)S(1)}, s32[128,128]{1,0:T(8,128)}, u32[]{:S(2)}) copy-start(s32[128,128]{1,0:T(8,128)} %param.7) | copy-start | bytes 196612
  62.2 27.3 %collective-permute-start.2 = (bf16[4096,128]{1,0:T(8,128)(2,1)}, bf16[4096,128]{1,0:T(8,128)(2,1)}, u32[]{:S(2)}, u32[]{:S(2)}) collective-permute-start(bf16[4096,128]{1,0:T(8,128)(2,1)} %bitcast.7.near_ref), channel_id=1, source_target_pairs={{0,4},{4,0},{1,5},{5,1},{2,6},{6,2},{3,7},{7,3},{8,12},{12,8},{9,1... | collective-permute-start | bytes 3145736 | tf_op jit(solution)/shard_map/ppermute | solution.py:28
  68.0 18.7 %all-to-all-start.4 = ((bf16[4,512,256]{2,1,0:T(8,128)(2,1)}), bf16[4,512,256]{2,1,0:T(8,128)(2,1)S(1)}, u32[]{:S(2)}, u32[]{:S(2)}) async-start(bf16[4,512,256]{2,1,0:T(8,128)(2,1)} %broadcast_in_dim.26), calls=%async_computation.4 | async-start | bytes 2097152 | tf_op jit(solution)/shard_map/all_to_all | solution.py:20
  86.7 20.0 %copy-start.1 = (bf16[4,512,256]{2,1,0:T(8,128)(2,1)}, bf16[4,512,256]{2,1,0:T(8,128)(2,1)S(1)}, u32[]{:S(2)}) copy-start(bf16[4,512,256]{2,1,0:T(8,128)(2,1)S(1)} %all-to-all-done.4) | copy-start | bytes 3145732
  86.7 30.1 %collective-permute-start.3 = (bf16[2048,256]{1,0:T(8,128)(2,1)S(1)}, bf16[2048,256]{1,0:T(8,128)(2,1)S(1)}, u32[]{:S(2)}, u32[]{:S(2)}) collective-permute-start(bf16[2048,256]{1,0:T(8,128)(2,1)S(1)} %bitcast.101), channel_id=1, source_target_pairs={{0,4},{4,0},{1,5},{5,1},{2,6},{6,2},{3,7},{7,3},{8,12},{12,8},{9,1... | collective-permute-start | bytes 3145736 | tf_op jit(solution)/shard_map/ppermute | solution.py:28
  113.1 4.7 %copy-start.2 = (bf16[4,512,256]{2,1,0:T(8,128)(2,1)S(1)}, bf16[4,512,256]{2,1,0:T(8,128)(2,1)}, u32[]{:S(2)}) copy-start(bf16[4,512,256]{2,1,0:T(8,128)(2,1)} %copy-done.1) | copy-start | bytes 3145732
  116.8 1.0 copy-start.4
  117.8 1.9 copy-start.3
  119.8 2.1 copy-start.6
  123.0 17.1 %all-to-all-start.5 = ((bf16[8,192,256]{2,1,0:T(8,128)(2,1)}), bf16[8,192,256]{2,1,0:T(8,128)(2,1)}, u32[]{:S(2)}, u32[]{:S(2)}) async-start(bf16[8,192,256]{2,1,0:T(8,128)(2,1)} %pad_maximum_fusion), calls=%async_computation.5 | async-start | bytes 1572864 | tf_op jit(solution)/shard_map/all_to_all | solution.py:20
  140.1 15.6 %all-to-all-start.3 = ((bf16[8,192,256]{2,1,0:T(8,128)(2,1)}), bf16[8,192,256]{2,1,0:T(8,128)(2,1)S(1)}, u32[]{:S(2)}, u32[]{:S(2)}) async-start(bf16[8,192,256]{2,1,0:T(8,128)(2,1)} %bitcast.9), calls=%async_computation.3 | async-start | bytes 1572864 | tf_op jit(solution)/shard_map/all_to_all | solution.py:20
  185.3 17.5 %collective-permute-start.5 = (f32[32,128]{1,0:T(8,128)S(1)}, f32[32,128]{1,0:T(8,128)S(1)}, u32[]{:S(2)}, u32[]{:S(2)}) collective-permute-start(f32[32,128]{1,0:T(8,128)S(1)} %bitcast.118), channel_id=1, source_target_pairs={{0,1},{1,2},{2,3},{3,0},{4,5},{5,6},{6,7},{7,4},{8,9},{9,10},{10,1... | collective-permute-start | bytes 49160 | tf_op jit(solution)/shard_map/ppermute | solution.py:33
  187.4 15.5 %collective-permute-start.6 = (f32[32,128]{1,0:T(8,128)S(1)}, f32[32,128]{1,0:T(8,128)S(1)}, u32[]{:S(2)}, u32[]{:S(2)}) collective-permute-start(f32[32,128]{1,0:T(8,128)S(1)} %bitcast.119), channel_id=1, source_target_pairs={{0,3},{1,0},{2,1},{3,2},{4,7},{5,4},{6,5},{7,6},{8,11},{9,8},{10,9... | collective-permute-start | bytes 49160 | tf_op jit(solution)/shard_map/ppermute | solution.py:33
  192.8 10.1 %collective-permute-start.4 = (f32[32,128]{1,0:T(8,128)S(1)}, f32[32,128]{1,0:T(8,128)S(1)}, u32[]{:S(2)}, u32[]{:S(2)}) collective-permute-start(f32[32,128]{1,0:T(8,128)S(1)} %bitcast.120), channel_id=1, source_target_pairs={{0,2},{1,3},{2,0},{3,1},{4,6},{5,7},{6,4},{7,5},{8,10},{9,11},{10,... | collective-permute-start | bytes 49160 | tf_op jit(solution)/shard_map/ppermute | solution.py:33
  197.0 27.3 %all-to-all-start.8 = ((bf16[4,16,32,256]{3,2,1,0:T(8,128)(2,1)}), bf16[4,16,32,256]{3,2,1,0:T(8,128)(2,1)S(1)}, u32[]{:S(2)}, u32[]{:S(2)}) async-start(bf16[4,16,32,256]{3,2,1,0:T(8,128)(2,1)} %broadcast_in_dim.29), calls=%async_computation.8 | async-start | bytes 2097152 | tf_op jit(solution)/shard_map/all_to_all | solution.py:20
  202.9 19.2 %collective-permute-start.8 = (f32[64,128]{1,0:T(8,128)S(1)}, f32[64,128]{1,0:T(8,128)S(1)}, u32[]{:S(2)}, u32[]{:S(2)}) collective-permute-start(f32[64,128]{1,0:T(8,128)S(1)} %pad_maximum_fusion.7), channel_id=1, source_target_pairs={{0,8},{8,16},{16,24},{24,0},{1,9},{9,17},{17,25},{25,1},{2,10},{10... | collective-permute-start | bytes 98312 | tf_op jit(solution)/shard_map/ppermute | solution.py:33
  205.7 16.4 %collective-permute-start.9 = (f32[64,128]{1,0:T(8,128)S(1)}, f32[64,128]{1,0:T(8,128)S(1)}, u32[]{:S(2)}, u32[]{:S(2)}) collective-permute-start(f32[64,128]{1,0:T(8,128)S(1)} %pad_maximum_fusion.7), channel_id=1, source_target_pairs={{0,24},{8,0},{16,8},{24,16},{1,25},{9,1},{17,9},{25,17},{2,26},{10... | collective-permute-start | bytes 98312 | tf_op jit(solution)/shard_map/ppermute | solution.py:33
  208.2 14.0 %collective-permute-start.7 = (f32[64,128]{1,0:T(8,128)S(1)}, f32[64,128]{1,0:T(8,128)S(1)}, u32[]{:S(2)}, u32[]{:S(2)}) collective-permute-start(f32[64,128]{1,0:T(8,128)S(1)} %pad_maximum_fusion.7), channel_id=1, source_target_pairs={{0,16},{8,24},{16,0},{24,8},{1,17},{9,25},{17,1},{25,9},{2,18},{10... | collective-permute-start | bytes 98312 | tf_op jit(solution)/shard_map/ppermute | solution.py:33
  212.4 11.9 %collective-permute-start.10 = (f32[2,32,256]{2,1,0:T(8,128)S(1)}, f32[2,32,256]{2,1,0:T(8,128)S(1)}, u32[]{:S(2)}, u32[]{:S(2)}) collective-permute-start(f32[2,32,256]{2,1,0:T(8,128)S(1)} %pad_maximum_fusion.4), channel_id=1, source_target_pairs={{0,0},{32,4},{64,8},{96,12},{128,16},{160,20},{192,24},{224,28},{2... | collective-permute-start | bytes 196616 | tf_op jit(solution)/shard_map/ppermute | solution.py:314
  224.3 11.8 %collective-permute-start.11 = (bf16[2048,256]{1,0:T(8,128)(2,1)S(1)}, bf16[2048,256]{1,0:T(8,128)(2,1)S(1)}, u32[]{:S(2)}, u32[]{:S(2)}) collective-permute-start(bf16[2048,256]{1,0:T(8,128)(2,1)S(1)} %bitcast.99), channel_id=1, source_target_pairs={{0,4},{4,0},{1,5},{5,1},{2,6},{6,2},{3,7},{7,3},{8,12},{12,8},{9,1... | collective-permute-start | bytes 3145736 | tf_op jit(solution)/shard_map/ppermute | solution.py:28
  232.3 3.1 %collective-permute-start.12 = (f32[64,128]{1,0:T(8,128)S(1)}, f32[64,128]{1,0:T(8,128)S(1)}, u32[]{:S(2)}, u32[]{:S(2)}) collective-permute-start(f32[64,128]{1,0:T(8,128)S(1)} %add_add_fusion), channel_id=1, source_target_pairs={{0,4},{4,0},{1,5},{5,1},{2,6},{6,2},{3,7},{7,3},{8,12},{12,8},{9,1... | collective-permute-start | bytes 98312 | tf_op jit(solution)/shard_map/ppermute | solution.py:28

commit v4 on v3

--- a/solution.py
+++ b/solution.py
@@ -28,13 +28,6 @@
     return lax.ppermute(x, axis, [(i, i ^ flip) for i in range(lax.axis_size(axis))])
 
 
-def over_four(x, axis):
-    near, opposite, far = (
-        lax.ppermute(x, axis, [(i, (i + step) % 4) for i in range(4)]) for step in (1, 2, 3)
-    )
-    return (x + opposite) + (near + far)
-
-
 def in_parts(x):
     first = lax.reduce_precision(x, 8, 7)
     second = lax.reduce_precision(x - first, 8, 7)
@@ -63,13 +56,15 @@
     return tiles.astype(jnp.float32).sum(axis=0)
 
 
-def forward_kernel(ids_ref, near_ref, far_ref, proj_ref, *refs):
-    emb_ref, normed_ref, inv_ref, table_ref, even_ref, odd_ref, fm_ref = refs[-7:]
+def forward_kernel(ids_ref, near_ref, far_ref, proj_ref, lcb_ref, *refs):
+    emb_ref, normed_ref, inv_ref, lcb_sum_ref, table_ref, even_ref, odd_ref, fm_ref = refs[-8:]
     rank, n_emb = proj_ref.shape
     half, width = near_ref.shape
 
     @pl.when(pl.program_id(0) == 0)
     def _():
+        lcb_sum_ref[...] = jnp.zeros_like(lcb_sum_ref)
+
         @pl.loop(0, half // 128)
         def _(i):
             at = pl.multiple_of(i * 128, 128)
@@ -79,6 +74,8 @@
     proj = proj_ref[...]
     scale = 1.0 / (rank * n_emb)
     per = normed_ref.shape[2] // n_emb
+    outputs = lcb_ref.shape[1]
+    lcb_sum = jnp.zeros(lcb_sum_ref.shape, jnp.float32)
     for start in range(0, GROUP, ROWS):
         for e in range(0, ROWS, 2):
             rows_ref = (even_ref, odd_ref)[e // 2 % 2]
@@ -92,10 +89,13 @@
             compressed = jnp.dot(
                 proj, jnp.concatenate([first, second], axis=1), preferred_element_type=jnp.float32
             ).astype(jnp.bfloat16)
-            compressed = jnp.concatenate([compressed[:, :width], compressed[:, width:]], axis=0)
-            fm = lax.dot_general(compressed, pair, (((1,), (1,)), ((), ())), preferred_element_type=jnp.float32)
+            left = jnp.concatenate(
+                [compressed[:, :width], compressed[:, width:], lcb_ref[start + e], lcb_ref[start + e + 1]], axis=0
+            )
+            fm = lax.dot_general(left, pair, (((1,), (1,)), ((), ())), preferred_element_type=jnp.float32)
             fm_ref[pl.ds(e * rank, rank), :] = fm[:rank, :n_emb]
-            fm_ref[pl.ds((e + 1) * rank, rank), :] = fm[rank:, n_emb:]
+            fm_ref[pl.ds((e + 1) * rank, rank), :] = fm[rank : 2 * rank, n_emb:]
+            lcb_sum += fm[2 * rank : 2 * rank + outputs, :n_emb] + fm[2 * rank + outputs :, n_emb:]
         parts = [fm_ref[pl.ds(k, ROWS, stride=rank), :] for k in range(rank)]
         mean = jnp.sum(sum(parts), axis=1, keepdims=True) * scale
         parts = [p - mean for p in parts]
@@ -105,15 +105,16 @@
             at = k % per * n_emb
             normed_ref[k // per, start : start + ROWS, at : at + n_emb] = (parts[k] * inv).astype(jnp.bfloat16)
         inv_ref[start : start + ROWS] = jnp.broadcast_to(inv, (ROWS, inv_ref.shape[1]))
-
-
-def forward_features(ids, near, far, projection, blocks, start, count, embedded=None):
+    lcb_sum_ref[...] += lcb_sum
+
+
+def forward_features(ids, near, far, projection, lcb_grad, blocks, start, count, before=()):
     examples, n_emb = ids.shape
     half, width = near.shape
     rank = projection.shape[1]
     columns = rank * n_emb // blocks
     skip = start // GROUP
-    before = () if embedded is None else (embedded,)
+    outputs = lcb_grad.shape[1]
     return pl.pallas_call(
         forward_kernel,
         grid=(count // GROUP,),
@@ -122,17 +123,20 @@
             pl.BlockSpec((half, width), lambda g: (0, 0)),
             pl.BlockSpec((half, width), lambda g: (0, 0)),
             pl.BlockSpec((rank, n_emb), lambda g: (0, 0)),
+            pl.BlockSpec((GROUP, outputs, width), lambda g: (g + skip, 0, 0)),
             *(pl.BlockSpec(memory_space=pl.ANY) for _ in before),
         ],
         out_specs=[
             pl.BlockSpec((GROUP, n_emb, width), lambda g: (g + skip, 0, 0)),
             pl.BlockSpec((blocks, GROUP, columns), lambda g: (0, g, 0)),
-            pl.BlockSpec((GROUP, 128), lambda g: (g, 0)),
+            pl.BlockSpec((GROUP, 128), lambda g: (g + skip, 0)),
+            pl.BlockSpec((outputs, n_emb), lambda g: (0, 0)),
         ],
         out_shape=[
             jax.ShapeDtypeStruct((examples, n_emb, width), jnp.bfloat16),
             jax.ShapeDtypeStruct((blocks, count, columns), jnp.bfloat16),
-            jax.ShapeDtypeStruct((count, 128), jnp.float32),
+            jax.ShapeDtypeStruct((examples, 128), jnp.float32),
+            jax.ShapeDtypeStruct((outputs, n_emb), jnp.float32),
         ],
         scratch_shapes=[
             pltpu.VMEM((2 * half, width), jnp.float32),
@@ -140,28 +144,34 @@
             pltpu.VMEM((2 * n_emb, width), jnp.float32),
             pltpu.VMEM((ROWS * rank, n_emb), jnp.float32),
         ],
-        input_output_aliases={4: 0} if before else {},
+        input_output_aliases={5: 0, 6: 2} if before else {},
         cost_estimate=pl.CostEstimate(
             flops=100_000_000 * count,
             bytes_accessed=half * width * 4 + count * n_emb * width * 2,
             transcendentals=0,
         ),
         name="fm_forward",
-    )(ids, near, far, projection.T, *before)
-
-
-def backward_kernel(grad_ref, normed_ref, inv_ref, emb_ref, *refs):
-    back_ref, fm_grad_ref = refs[-2:]
-    n_emb = emb_ref.shape[1]
-    rank, width = back_ref.shape[1:]
-    per = normed_ref.shape[2] // n_emb
+    )(ids, near, far, projection.T, lcb_grad, *before)
+
+
+def backward_kernel(grad_ref, first_ref, last_ref, inv_ref, emb_ref, proj_ref, fm_grad_ref):
+    n_emb, rank = proj_ref.shape
+    width = emb_ref.shape[2]
+    per = last_ref.shape[2] // n_emb
     scale = 1.0 / (rank * n_emb)
+    at_last = pl.program_id(0) == pl.num_programs(0) - 1
+
+    @pl.when(pl.program_id(0) == 0)
+    def _():
+        proj_ref[...] = jnp.zeros_like(proj_ref)
+
+    proj = jnp.zeros(proj_ref.shape, jnp.float32)
     for start in range(0, GROUP, ROWS):
         rows = slice(start, start + ROWS)
         grads = [grad_ref[rows, k * n_emb : (k + 1) * n_emb] for k in range(rank)]
+        cuts = [(k // per, rows, slice(k % per * n_emb, (k % per + 1) * n_emb)) for k in range(rank)]
         normed = [
-            normed_ref[k // per, rows, k % per * n_emb : (k % per + 1) * n_emb].astype(jnp.float32)
-            for k in range(rank)
+            jnp.where(at_last, last_ref[cut].astype(jnp.float32), first_ref[cut].astype(jnp.float32)) for cut in cuts
         ]
         mean = jnp.sum(sum(grads), axis=1, keepdims=True) * scale
         along = jnp.sum(sum(g * x for g, x in zip(grads, normed)), axis=1, keepdims=True) * scale
@@ -172,43 +182,48 @@
             fm_grad = fm_grad_ref[pl.ds(e * rank, 2 * rank), :].astype(jnp.bfloat16)
             pair = jnp.concatenate([emb_ref[start + e], emb_ref[start + e + 1]], axis=1)
             back = jnp.dot(fm_grad, pair, preferred_element_type=jnp.float32).astype(jnp.bfloat16)
-            back_ref[start + e] = back[:rank, :width]
-            back_ref[start + e + 1] = back[rank:, width:]
-
-
-def backward_features(normed_grad, normed, inv_scale, embedded, start, back=None):
+            back = jnp.concatenate([back[:rank, :width], back[rank:, width:]], axis=1)
+            proj += lax.dot_general(pair, back, (((1,), (1,)), ((), ())), preferred_element_type=jnp.float32)
+    proj_ref[...] += proj
+
+
+def backward_features(normed_grad, normed_first, normed_last, inv_scale, embedded):
     examples, n_emb, width = embedded.shape
-    blocks, count, columns = normed.shape
+    blocks, count, columns = normed_first.shape
     rank = blocks * columns // n_emb
-    skip = start // GROUP
-    before = () if back is None else (back,)
+    firsts = count // GROUP
+    assert normed_last.shape[1] == GROUP and count + GROUP == examples
     return pl.pallas_call(
         backward_kernel,
-        grid=(count // GROUP,),
+        grid=(firsts + 1,),
         in_specs=[
-            pl.BlockSpec((GROUP, rank * n_emb), lambda g: (g + skip, 0)),
-            pl.BlockSpec((blocks, GROUP, columns), lambda g: (0, g, 0)),
+            pl.BlockSpec((GROUP, rank * n_emb), lambda g: (g, 0)),
+            pl.BlockSpec((blocks, GROUP, columns), lambda g: (0, jnp.minimum(g, firsts - 1), 0)),
+            pl.BlockSpec((blocks, GROUP, columns), lambda g: (0, 0, 0)),
             pl.BlockSpec((GROUP, 128), lambda g: (g, 0)),
-            pl.BlockSpec((GROUP, n_emb, width), lambda g: (g + skip, 0, 0)),
-            *(pl.BlockSpec(memory_space=pl.ANY) for _ in before),
-        ],
-        out_specs=pl.BlockSpec((GROUP, rank, width), lambda g: (g + skip, 0, 0)),
-        out_shape=jax.ShapeDtypeStruct((examples, rank, width), jnp.bfloat16),
+            pl.BlockSpec((GROUP, n_emb, width), lambda g: (g, 0, 0)),
+        ],
+        out_specs=pl.BlockSpec((n_emb, rank), lambda g: (0, 0)),
+        out_shape=jax.ShapeDtypeStruct((n_emb, rank), jnp.float32),
         scratch_shapes=[pltpu.VMEM((ROWS * rank, n_emb), jnp.float32)],
-        input_output_aliases={4: 0} if before else {},
         cost_estimate=pl.CostEstimate(
-            flops=30_000_000 * count,
-            bytes_accessed=count * n_emb * (width * 2 + rank * 8),
+            flops=40_000_000 * examples,
+            bytes_accessed=examples * n_emb * (width * 2 + rank * 6),
             transcendentals=0,
         ),
         name="fm_backward",
-    )(normed_grad, normed, inv_scale, embedded, *before)
-
-
-def both_halves(half):
+    )(normed_grad, normed_first, normed_last, inv_scale, embedded)
+
+
+def both_halves(half, order=None):
     other = swapped(half, "c", 1)
     high = lax.axis_index("c") == 1
-    return jnp.where(high, jnp.stack([other, half]), jnp.stack([half, other])).reshape(-1, *half.shape[1:])
+    if order is None:
+        return jnp.where(high, jnp.stack([other, half]), jnp.stack([half, other])).reshape(-1, *half.shape[1:])
+    dims, axes = order
+    both = [h.reshape(*dims, *half.shape[1:]) for h in (half, other)]
+    both = jnp.where(high, jnp.stack(both[::-1]), jnp.stack(both))
+    return jnp.transpose(both, axes).reshape(-1, *half.shape[1:])
 
 
 def per_device(feature_ids, emb_table, factor_machine_projection, mlp_weight, momentum, hidden_grad, lcb_grad):
@@ -228,7 +243,7 @@
     table = from_everyone(emb_table, ("mp", "zl")).reshape(-1, width)
     state = lax.ppermute(jnp.stack([mlp_weight, momentum]), DP, to_worker)
     weight_rows, momentum_rows = state[0], state[1]
-    weights = weight_rows.astype(jnp.bfloat16)
+    weights = mlp_weight.astype(jnp.bfloat16)
     near_rows = table.shape[0]
     table = from_everyone(jnp.concatenate([table, weights[:, :width], weights[:, width:]], axis=0), "y")
     weights = table[:, near_rows:].reshape(y, hidden // width, -1, width)
@@ -248,10 +263,11 @@
     blocks = 2 * c * x
     cut = int(examples * FIRST_SHARE)
     shares = ((0, cut), (cut, examples - cut))
-    embedded, normed_a, inv_a = forward_features(ids, table, table_far, factor_machine_projection, blocks, *shares[0])
-    weights = both_halves(weights)
-    embedded, normed_b, inv_b = forward_features(
-        ids, table, table_far, factor_machine_projection, blocks, *shares[1], embedded
+    inputs = (ids, table, table_far, factor_machine_projection, lcb_grad)
+    embedded, normed_a, inv_scale, lcb_a = forward_features(*inputs, blocks, *shares[0])
+    weights = both_halves(weights, ((x, zl, y, mlp_weight.shape[0]), (2, 3, 1, 0, 4, 5)))
+    embedded, normed_b, inv_scale, lcb_b = forward_features(
+        *inputs, blocks, *shares[1], (embedded, inv_scale)
     )
     columns_a = exchange(normed_a.reshape(c * x, 2 * cut, -1), CX)
 
@@ -279,21 +295,26 @@
     )
 
     normed_part = lax.dot_general(preact_grad, weights, (((1,), (1,)), ((), ())), preferred_element_type=jnp.float32)
-    back = backward_features(normed_part, normed_a, inv_a, embedded, 0)
-    back = backward_features(normed_part, normed_b, inv_b, embedded, cut, back)
-    proj_part = jnp.einsum("bqh,blh->ql", back, embedded, preferred_element_type=jnp.float32)
-    lcb_part = jnp.einsum("bld,bnd->ln", lcb_grad, embedded, preferred_element_type=jnp.float32)
-    both = jnp.concatenate([proj_part, lcb_part], axis=0)
-
-    weight_grad = 0.0
-    columns_b = group_grad[:, examples:]
-    for part, (start, count) in zip((columns_a, columns_b), shares):
-        weight_grad += jnp.einsum(
-            "shbk,sbn->hkn",
-            part.reshape(c * x, 2, count, -1),
-            group_grad[:, start : start + count],
-            preferred_element_type=jnp.float32,
-        )
+    proj_part = backward_features(normed_part, normed_a, normed_b, inv_scale, embedded)
+    both = jnp.concatenate([proj_part.T, lcb_a + lcb_b], axis=0)
+
+    (start_a, count_a), (start_b, count_b) = shares
+    weight_grad = jnp.einsum(
+        "shbk,sbn->hkn",
+        columns_a.reshape(c * x, 2, count_a, -1),
+        group_grad[:, :count_a],
+        preferred_element_type=jnp.float32,
+    ) + jnp.stack(
+        [
+            jnp.einsum(
+                "sbk,sbn->kn",
+                group_grad[:, at : at + count_b],
+                group_grad[:, start_b:examples],
+                preferred_element_type=jnp.float32,
+            )
+            for at in (examples, examples + count_b)
+        ]
+    )
     arrived = exchange(
         jnp.concatenate(
             [
@@ -308,15 +329,19 @@
     both = from_parts(summed(arrived[:, own_rows:]))
     new_momentum = 0.9 * momentum_rows + summed(arrived[:, :own_rows])
     new_weight = weight_rows - 0.01 * new_momentum
-    arrived = from_everyone(jnp.concatenate([new_weight.astype(jnp.bfloat16), in_parts(both)], axis=0), ZY)
-    next_weight = from_everyone(arrived[:, :own_rows], "x").reshape(-1, hidden)
-    both = from_parts(arrived[:, own_rows:]).reshape(-1, both.shape[1])
+    next_weight = from_everyone(new_weight.astype(jnp.bfloat16), ZY)
+    over_mp = both + swapped(both, "mp", 1)
+    over_mp += swapped(over_mp, "mp", 3)
+    both = jnp.where(lax.axis_index("zl") == 0, over_mp, both)
+    both += swapped(both, "c", 1)
+    next_weight, both = tied(next_weight, both)
+    next_weight = from_everyone(next_weight, "x").reshape(-1, hidden)
     state = lax.ppermute(jnp.stack([new_weight, new_momentum]), DP, to_owner)
-    proj_sum = over_four(both[:rank], "mp")
-    both = over_four(jnp.concatenate([proj_sum, both[rank:]], axis=0), "x")
+    both += swapped(both, "x", 1)
+    both += swapped(both, "x", 3)
     next_weight, both, state = tied(next_weight, both, state)
     next_weight = both_halves(next_weight)
-    both += swapped(both, "c", 1)
+    both = from_everyone(both, ZY).reshape(2 * rank, -1)
     return (state[0], state[1], next_weight, both[:rank].T, both[rank:].T)
 
 

time: 239 us -> 239 us (level)
  the two profiles are of different devices: /device:TPU:5 before, /device:TPU:1 now
where the time goes in v4:
time: 239 us; the launch traced here: 237 us
  starting transfers between devices  94.6 us (40%)
  waiting for transfers between devices  69.2 us (29%)
  Pallas kernels  33.2 us (14%)
  blocking collectives  18.2 us (8%)
  local copies, waits for them, and re-layouts  8.62 us (4%)
  other arithmetic  7.13 us (3%)
  matrix products  5.06 us (2%)
    all_to_all x9, starting transfers between devices, exchange(): return lax.all_to_all(tiles, axis, split_axis=0, concat_axis=0, tiled=True)  52 us
    all_to_all x9, waiting for transfers between devices, exchange(): return lax.all_to_all(tiles, axis, split_axis=0, concat_axis=0, tiled=True)  49.9 us
    ppermute x9, starting transfers between devices, swapped(): lax.ppermute(x, axis, [(i, i ^ flip) for i in range(lax.axis_size(axis))])  35.1 us
    pallas_call x2, Pallas kernels, forward_features(): pl.pallas_call(forward_kernel, grid=(count // GROUP,), in_specs=[pl.Block...  23.3 us
    ppermute x9, waiting for transfers between devices, swapped(): lax.ppermute(x, axis, [(i, i ^ flip) for i in range(lax.axis_size(axis))])  19.4 us
    all_to_all x1, blocking collectives, exchange(): return lax.all_to_all(tiles, axis, split_axis=0, concat_axis=0, tiled=True)  18.2 us
    pallas_call x1, Pallas kernels, backward_features(): pl.pallas_call(backward_kernel, grid=(firsts + 1,), in_specs=[pl.BlockSpe...  9.86 us
    broadcast_in_dim x7, local copies, waits for them, and re-layouts, from_everyone(): return exchange(jnp.broadcast_to(x, (lax.axis_size(axis), *x.shape)), axis)  6.06 us
  transfers between devices with their start and end apart: 20, of which 12 were waited for; matrix products, arithmetic and copies ran while one was open for 4% of the time, Pallas kernels for 14%

profile of v4, /device:TPU:1, one launch (start us, length us, event | category | flops | bytes accessed | tf_op | source)
XLA Modules:
  0.0 237.1 jit_solution(6446527184562784617)
XLA Ops:
  0.6 1.3 broadcast_in_dim.25
  1.9 10.9 %all-to-all-start = ((bf16[8,16,128]{2,1,0:T(8,128)(2,1)}), bf16[8,16,128]{2,1,0:T(8,128)(2,1)S(1)}, u32[]{:S(2)}, u32[]{:S(2)}) async-start(bf16[8,16,128]{2,1,0:T(8,128)(2,1)} %broadcast_in_dim.25), calls=%async_computation | async-start | bytes 65536 | tf_op jit(solution)/shard_map/all_to_all | solution.py:20
  12.8 0.8 convert_element_type.22
  13.6 6.1 %all-to-all-done = bf16[8,16,128]{2,1,0:T(8,128)(2,1)S(1)} async-done(((bf16[8,16,128]{2,1,0:T(8,128)(2,1)}), bf16[8,16,128]{2,1,0:T(8,128)(2,1)S(1)}, u32[]{:S(2)}, u32[]{:S(2)}) %all-to-all-start) | async-done | bytes 32800 | tf_op jit(solution)/shard_map/all_to_all | solution.py:20
  19.7 18.2 %all_to_all.50 = bf16[8,192,128]{2,1,0:T(8,128)(2,1)S(1)} all-to-all(bf16[8,192,128]{2,1,0:T(8,128)(2,1)S(1)} %broadcast_in_dim.26), channel_id=1, replica_groups=mesh['zl'=2,'y'=8,'x'=4,'c'=2,'mp'=4] {'y'}, dimensions={0} | all-to-all | bytes 786432 | tf_op jit(solution)/shard_map/all_to_all | solution.py:20
  38.0 1.2 broadcast_in_dim.27
  39.2 4.0 %all-to-all-start.2 = ((bf16[4,8,128,128]{3,2,1,0:T(8,128)(2,1)}), bf16[4,8,128,128]{3,2,1,0:T(8,128)(2,1)S(1)}, u32[]{:S(2)}, u32[]{:S(2)}) async-start(bf16[4,8,128,128]{3,2,1,0:T(8,128)(2,1)} %broadcast_in_dim.27), calls=%async_computation.2 | async-start | bytes 2097152 | tf_op jit(solution)/shard_map/all_to_all | solution.py:20
  43.2 0.1 copy.28
  43.3 2.2 collective-permute-start.1
  45.6 3.5 %collective-permute-done.1 = bf16[256,256]{1,0:T(8,128)(2,1)S(1)} collective-permute-done((bf16[256,256]{1,0:T(8,128)(2,1)S(1)}, bf16[256,256]{1,0:T(8,128)(2,1)S(1)}, u32[]{:S(2)}, u32[]{:S(2)}) %collective-permute-start.1) | collective-permute-done | bytes 131104 | tf_op jit(solution)/shard_map/ppermute | solution.py:28
  49.1 4.6 %all-to-all-done.2 = bf16[4,8,128,128]{3,2,1,0:T(8,128)(2,1)S(1)} async-done(((bf16[4,8,128,128]{3,2,1,0:T(8,128)(2,1)}), bf16[4,8,128,128]{3,2,1,0:T(8,128)(2,1)S(1)}, u32[]{:S(2)}, u32[]{:S(2)}) %all-to-all-start.2) | async-done | bytes 1048608 | tf_op jit(solution)/shard_map/all_to_all | solution.py:20
  53.8 7.4 %collective-permute-start.2 = (bf16[4096,128]{1,0:T(8,128)(2,1)S(1)}, bf16[4096,128]{1,0:T(8,128)(2,1)}, u32[]{:S(2)}, u32[]{:S(2)}) collective-permute-start(bf16[4096,128]{1,0:T(8,128)(2,1)S(1)} %bitcast.97), channel_id=1, source_target_pairs={{0,4},{4,0},{1,5},{5,1},{2,6},{6,2},{3,7},{7,3},{8,12},{12,8},{9,1... | collective-permute-start | bytes 3145736 | tf_op jit(solution)/shard_map/ppermute | solution.py:28
  61.2 1.0 broadcast_in_dim.28
  62.2 3.5 %all-to-all-start.4 = ((bf16[4,512,256]{2,1,0:T(8,128)(2,1)}), bf16[4,512,256]{2,1,0:T(8,128)(2,1)S(1)}, u32[]{:S(2)}, u32[]{:S(2)}) async-start(bf16[4,512,256]{2,1,0:T(8,128)(2,1)} %broadcast_in_dim.28), calls=%async_computation.4 | async-start | bytes 2097152 | tf_op jit(solution)/shard_map/all_to_all | solution.py:20
  65.7 0.8 fusion.19.ids_ref
  66.5 14.4 %all-to-all-done.4 = bf16[4,512,256]{2,1,0:T(8,128)(2,1)S(1)} async-done(((bf16[4,512,256]{2,1,0:T(8,128)(2,1)}), bf16[4,512,256]{2,1,0:T(8,128)(2,1)S(1)}, u32[]{:S(2)}, u32[]{:S(2)}) %all-to-all-start.4) | async-done | bytes 1048608 | tf_op jit(solution)/shard_map/all_to_all | solution.py:20
  80.9 2.8 %collective-permute-start.3 = (bf16[2048,256]{1,0:T(8,128)(2,1)S(1)}, bf16[2048,256]{1,0:T(8,128)(2,1)S(1)}, u32[]{:S(2)}, u32[]{:S(2)}) collective-permute-start(bf16[2048,256]{1,0:T(8,128)(2,1)S(1)} %bitcast.90), channel_id=1, source_target_pairs={{0,4},{4,0},{1,5},{5,1},{2,6},{6,2},{3,7},{7,3},{8,12},{12,8},{9,1... | collective-permute-start | bytes 3145736 | tf_op jit(solution)/shard_map/ppermute | solution.py:28
  83.7 16.9 %fm_forward.2 = (bf16[128,128,128]{2,1,0:T(8,128)(2,1)}, bf16[16,96,256]{2,1,0:T(8,128)(2,1)}, f32[128,128]{1,0:T(8,128)}, f32[32,128]{1,0:T(8,128)}) custom-call(s32[128,128]{1,0:T(8,128)} %fusion.19.ids_ref, bf16[4096,128]{1,0:T(8,128)(2,1)} %bitcast.98, bf16[4096,128]{1,0:T(8,128)(2,1)} %collective-permute-done.2.far_ref, bf16[32,128]{1,0:T(8,128)(2,1)} %bitcast.112, ...), custom_call_target="tpu_custom_call" | custom-call | flops 9600000000 | bytes 5242880 | tf_op jit(solution)/shard_map/fm_forward/pallas_call | solution.py:118
  100.6 6.4 %fm_forward.3 = (bf16[128,128,128]{2,1,0:T(8,128)(2,1)}, bf16[16,32,256]{2,1,0:T(8,128)(2,1)}, f32[128,128]{1,0:T(8,128)}, f32[32,128]{1,0:T(8,128)}) custom-call(s32[128,128]{1,0:T(8,128)} %fusion.19.ids_ref, bf16[4096,128]{1,0:T(8,128)(2,1)} %bitcast.99, ...), custom_call_target="tpu_custom_call", output_to_operand_aliasing={{0}: (5, {}), {2}: (6, {})} | custom-call | flops 3200000000 | bytes 3145728 | tf_op jit(solution)/shard_map/fm_forward/pallas_call | solution.py:118
  107.0 0.7 add.65
  107.7 0.1 copy.31
  107.8 0.3 fusion
  108.2 0.2 copy.29
  108.4 0.7 copy-done.1
  109.1 0.5 convolution_bitcast_fusion.4
  109.6 1.6 convolution_bitcast_fusion.3
  111.2 0.1 multiply_convert_fusion
  111.3 1.0 pad_maximum_fusion
  112.3 3.5 %all-to-all-start.5 = ((bf16[8,192,256]{2,1,0:T(8,128)(2,1)}), bf16[8,192,256]{2,1,0:T(8,128)(2,1)S(1)}, u32[]{:S(2)}, u32[]{:S(2)}) async-start(bf16[8,192,256]{2,1,0:T(8,128)(2,1)} %pad_maximum_fusion), calls=%async_computation.5 | async-start | bytes 1572864 | tf_op jit(solution)/shard_map/all_to_all | solution.py:20
  115.8 2.1 fusion.28.grad_ref
  117.9 9.9 %fm_backward.1 = f32[128,32]{1,0:T(8,128)} custom-call(f32[128,4096]{1,0:T(8,128)} %fusion.28.grad_ref, bf16[16,96,256]{2,1,0:T(8,128)(2,1)} %get-tuple-element.21.first_ref, bf16[16,32,256]{2,1,0:T(8,128)(2,1)} %get-tuple-element.25.last_ref, f32[128,128]{1,0:T(8,128)} %get-tuple-element.26.inv_ref, bf16[128,128,128]{2,1,0:T(8,128)(2,1)} %get-tuple-element.27.emb_ref), custom_call_target="tpu_custom_call" | custom-call | flops 5120000000 | bytes 7340032 | tf_op jit(solution)/shard_map/fm_backward/pallas_call | solution.py:196
  127.8 0.9 pad_maximum_fusion.4
  128.7 0.1 copy.32
  128.8 4.8 %all-to-all-start.3 = ((bf16[8,192,256]{2,1,0:T(8,128)(2,1)}), bf16[8,192,256]{2,1,0:T(8,128)(2,1)S(1)}, u32[]{:S(2)}, u32[]{:S(2)}) async-start(bf16[8,192,256]{2,1,0:T(8,128)(2,1)} %bitcast.9), calls=%async_computation.3 | async-start | bytes 1572864 | tf_op jit(solution)/shard_map/all_to_all | solution.py:20
  133.6 0.2 convolution_bitcast_fusion.1
  133.8 0.2 convolution_bitcast_fusion.2
  134.1 11.6 %all-to-all-done.3 = bf16[8,192,256]{2,1,0:T(8,128)(2,1)S(1)} async-done(((bf16[8,192,256]{2,1,0:T(8,128)(2,1)}), bf16[8,192,256]{2,1,0:T(8,128)(2,1)S(1)}, u32[]{:S(2)}, u32[]{:S(2)}) %all-to-all-start.3) | async-done | bytes 786464 | tf_op jit(solution)/shard_map/all_to_all | solution.py:20
  145.7 0.4 fusion.2
  146.2 0.8 fusion.4
  146.9 3.5 %all-to-all-start.6 = ((bf16[16,40,256]{2,1,0:T(8,128)(2,1)}), bf16[16,40,256]{2,1,0:T(8,128)(2,1)S(1)}, u32[]{:S(2)}, u32[]{:S(2)}) async-start(bf16[16,40,256]{2,1,0:T(8,128)(2,1)} %fusion.4), calls=%async_computation.6 | async-start | bytes 655360 | tf_op jit(solution)/shard_map/all_to_all | solution.py:20
  150.5 3.8 %collective-permute-start = (f32[2,32,256]{2,1,0:T(8,128)S(1)}, f32[2,32,256]{2,1,0:T(8,128)S(1)}, u32[]{:S(2)}, u32[]{:S(2)}) collective-permute-start(f32[2,32,256]{2,1,0:T(8,128)S(1)} %pad_maximum_fusion.3), channel_id=1, source_target_pairs={{0,0},{4,32},{8,64},{12,96},{16,128},{20,160},{24,192},{28,224},{3... | collective-permute-start | bytes 196616 | tf_op jit(solution)/shard_map/ppermute | solution.py:244
  154.3 6.4 %all-to-all-done.6 = bf16[16,40,256]{2,1,0:T(8,128)(2,1)S(1)} async-done(((bf16[16,40,256]{2,1,0:T(8,128)(2,1)}), bf16[16,40,256]{2,1,0:T(8,128)(2,1)S(1)}, u32[]{:S(2)}, u32[]{:S(2)}) %all-to-all-start.6) | async-done | bytes 327712 | tf_op jit(solution)/shard_map/all_to_all | solution.py:20
  160.7 0.7 broadcast_in_dim.30
  161.5 9.8 %all-to-all-start.7 = ((bf16[16,32,256]{2,1,0:T(8,128)(2,1)}), bf16[16,32,256]{2,1,0:T(8,128)(2,1)S(1)}, u32[]{:S(2)}, u32[]{:S(2)}) async-start(bf16[16,32,256]{2,1,0:T(8,128)(2,1)} %broadcast_in_dim.30), calls=%async_computation.7 | async-start | bytes 524288 | tf_op jit(solution)/shard_map/all_to_all | solution.py:20
  171.4 2.2 collective-permute-start.4
  173.5 3.1 %collective-permute-done.4 = f32[4,128]{1,0:T(4,128)S(1)} collective-permute-done((f32[4,128]{1,0:T(4,128)S(1)}, f32[4,128]{1,0:T(4,128)S(1)}, u32[]{:S(2)}, u32[]{:S(2)}) %collective-permute-start.4) | collective-permute-done | bytes 2080 | tf_op jit(solution)/shard_map/ppermute | solution.py:28
  176.6 3.0 %collective-permute-start.5 = (f32[4,128]{1,0:T(4,128)S(1)}, f32[4,128]{1,0:T(4,128)S(1)}, u32[]{:S(2)}, u32[]{:S(2)}) collective-permute-start(f32[4,128]{1,0:T(4,128)S(1)} %fusion.36), channel_id=1, source_target_pairs={{0,3},{1,2},{2,1},{3,0},{4,7},{5,6},{6,5},{7,4},{8,11},{9,10},{10,... | collective-permute-start | bytes 6152 | tf_op jit(solution)/shard_map/ppermute | solution.py:28
  179.6 3.4 %collective-permute-done.5 = f32[4,128]{1,0:T(4,128)S(1)} collective-permute-done((f32[4,128]{1,0:T(4,128)S(1)}, f32[4,128]{1,0:T(4,128)S(1)}, u32[]{:S(2)}, u32[]{:S(2)}) %collective-permute-start.5) | collective-permute-done | bytes 2080 | tf_op jit(solution)/shard_map/ppermute | solution.py:28
  183.0 5.8 %collective-permute-start.6 = (f32[4,128]{1,0:T(4,128)S(1)}, f32[4,128]{1,0:T(4,128)S(1)}, u32[]{:S(2)}, u32[]{:S(2)}) collective-permute-start(f32[4,128]{1,0:T(4,128)S(1)} %add_select_fusion), channel_id=1, source_target_pairs={{0,4},{4,0},{1,5},{5,1},{2,6},{6,2},{3,7},{7,3},{8,12},{12,8},{9,1... | collective-permute-start | bytes 6152 | tf_op jit(solution)/shard_map/ppermute | solution.py:28
  188.8 0.8 collective-permute-done.6
  189.6 1.1 broadcast_in_dim.31
  190.7 3.5 %all-to-all-start.8 = ((bf16[4,16,32,256]{3,2,1,0:T(8,128)(2,1)}), bf16[4,16,32,256]{3,2,1,0:T(8,128)(2,1)S(1)}, u32[]{:S(2)}, u32[]{:S(2)}) async-start(bf16[4,16,32,256]{3,2,1,0:T(8,128)(2,1)} %broadcast_in_dim.31), calls=%async_computation.8 | async-start | bytes 2097152 | tf_op jit(solution)/shard_map/all_to_all | solution.py:20
  194.3 3.8 %collective-permute-start.9 = (f32[2,32,256]{2,1,0:T(8,128)S(1)}, f32[2,32,256]{2,1,0:T(8,128)S(1)}, u32[]{:S(2)}, u32[]{:S(2)}) collective-permute-start(f32[2,32,256]{2,1,0:T(8,128)S(1)} %pad_maximum_fusion.5), channel_id=1, source_target_pairs={{0,0},{32,4},{64,8},{96,12},{128,16},{160,20},{192,24},{224,28},{2... | collective-permute-start | bytes 196616 | tf_op jit(solution)/shard_map/ppermute | solution.py:339
  198.1 4.9 %collective-permute-start.7 = (f32[4,128]{1,0:T(4,128)S(1)}, f32[4,128]{1,0:T(4,128)S(1)}, u32[]{:S(2)}, u32[]{:S(2)}) collective-permute-start(f32[4,128]{1,0:T(4,128)S(1)} %add.71), channel_id=1, source_target_pairs={{0,8},{8,0},{16,24},{24,16},{1,9},{9,1},{17,25},{25,17},{2,10},{10... | collective-permute-start | bytes 6152 | tf_op jit(solution)/shard_map/ppermute | solution.py:28
  203.0 5.7 %collective-permute-done.7 = f32[4,128]{1,0:T(4,128)S(1)} collective-permute-done((f32[4,128]{1,0:T(4,128)S(1)}, f32[4,128]{1,0:T(4,128)S(1)}, u32[]{:S(2)}, u32[]{:S(2)}) %collective-permute-start.7) | collective-permute-done | bytes 2080 | tf_op jit(solution)/shard_map/ppermute | solution.py:28
  208.7 2.6 %collective-permute-start.8 = (f32[4,128]{1,0:T(4,128)S(1)}, f32[4,128]{1,0:T(4,128)S(1)}, u32[]{:S(2)}, u32[]{:S(2)}) collective-permute-start(f32[4,128]{1,0:T(4,128)S(1)} %add.72), channel_id=1, source_target_pairs={{0,24},{8,16},{16,8},{24,0},{1,25},{9,17},{17,9},{25,1},{2,26},{10... | collective-permute-start | bytes 6152 | tf_op jit(solution)/shard_map/ppermute | solution.py:28
  211.3 2.9 %collective-permute-done.8 = f32[4,128]{1,0:T(4,128)S(1)} collective-permute-done((f32[4,128]{1,0:T(4,128)S(1)}, f32[4,128]{1,0:T(4,128)S(1)}, u32[]{:S(2)}, u32[]{:S(2)}) %collective-permute-start.8) | collective-permute-done | bytes 2080 | tf_op jit(solution)/shard_map/ppermute | solution.py:28
  214.2 4.3 %collective-permute-start.10 = (bf16[2048,256]{1,0:T(8,128)(2,1)S(1)}, bf16[2048,256]{1,0:T(8,128)(2,1)S(1)}, u32[]{:S(2)}, u32[]{:S(2)}) collective-permute-start(bf16[2048,256]{1,0:T(8,128)(2,1)S(1)} %bitcast.88), channel_id=1, source_target_pairs={{0,4},{4,0},{1,5},{5,1},{2,6},{6,2},{3,7},{7,3},{8,12},{12,8},{9,1... | collective-permute-start | bytes 3145736 | tf_op jit(solution)/shard_map/ppermute | solution.py:28
  218.5 0.6 broadcast_in_dim.32
  219.1 8.4 %all-to-all-start.9 = ((f32[16,4,128]{2,1,0:T(4,128)}), f32[16,4,128]{2,1,0:T(4,128)S(1)}, u32[]{:S(2)}, u32[]{:S(2)}) async-start(f32[16,4,128]{2,1,0:T(4,128)} %broadcast_in_dim.32), calls=%async_computation.9 | async-start | bytes 65536 | tf_op jit(solution)/shard_map/all_to_all | solution.py:20
  227.5 0.6 slice_bitcast_fusion.2
  228.2 6.7 %all-to-all-done.9 = f32[16,4,128]{2,1,0:T(4,128)S(1)} async-done(((f32[16,4,128]{2,1,0:T(4,128)}), f32[16,4,128]{2,1,0:T(4,128)S(1)}, u32[]{:S(2)}, u32[]{:S(2)}) %all-to-all-start.9) | async-done | bytes 32800 | tf_op jit(solution)/shard_map/all_to_all | solution.py:20
  234.9 0.6 fusion.26
  235.5 1.6 maximum_select_fusion.1
  (43 shorter events, 0.4 us)
Async XLA Ops:
  1.9 17.7 %all-to-all-start = ((bf16[8,16,128]{2,1,0:T(8,128)(2,1)}), bf16[8,16,128]{2,1,0:T(8,128)(2,1)S(1)}, u32[]{:S(2)}, u32[]{:S(2)}) async-start(bf16[8,16,128]{2,1,0:T(8,128)(2,1)} %broadcast_in_dim.25), calls=%async_computation | async-start | bytes 65536 | tf_op jit(solution)/shard_map/all_to_all | solution.py:20
  39.2 14.6 %all-to-all-start.2 = ((bf16[4,8,128,128]{3,2,1,0:T(8,128)(2,1)}), bf16[4,8,128,128]{3,2,1,0:T(8,128)(2,1)S(1)}, u32[]{:S(2)}, u32[]{:S(2)}) async-start(bf16[4,8,128,128]{3,2,1,0:T(8,128)(2,1)} %broadcast_in_dim.27), calls=%async_computation.2 | async-start | bytes 2097152 | tf_op jit(solution)/shard_map/all_to_all | solution.py:20
  43.3 5.7 %collective-permute-start.1 = (bf16[256,256]{1,0:T(8,128)(2,1)S(1)}, bf16[256,256]{1,0:T(8,128)(2,1)S(1)}, u32[]{:S(2)}, u32[]{:S(2)}) collective-permute-start(bf16[256,256]{1,0:T(8,128)(2,1)S(1)} %bitcast.106), channel_id=1, source_target_pairs={{0,256},{256,0},{1,257},{257,1},{2,258},{258,2},{3,259},{259,3},{4... | collective-permute-start | bytes 393224 | tf_op jit(solution)/shard_map/ppermute | solution.py:28
  49.1 16.6 %copy-start.3 = (s32[128,128]{1,0:T(8,128)S(1)}, s32[128,128]{1,0:T(8,128)}, u32[]{:S(2)}) copy-start(s32[128,128]{1,0:T(8,128)} %param.7) | copy-start | bytes 196612
  53.8 29.9 %copy-start = (bf16[4,8,128,128]{3,2,1,0:T(8,128)(2,1)}, bf16[4,8,128,128]{3,2,1,0:T(8,128)(2,1)S(1)}, u32[]{:S(2)}) copy-start(bf16[4,8,128,128]{3,2,1,0:T(8,128)(2,1)S(1)} %all-to-all-done.2) | copy-start | bytes 3145732
  53.8 29.9 %collective-permute-start.2 = (bf16[4096,128]{1,0:T(8,128)(2,1)S(1)}, bf16[4096,128]{1,0:T(8,128)(2,1)}, u32[]{:S(2)}, u32[]{:S(2)}) collective-permute-start(bf16[4096,128]{1,0:T(8,128)(2,1)S(1)} %bitcast.97), channel_id=1, source_target_pairs={{0,4},{4,0},{1,5},{5,1},{2,6},{6,2},{3,7},{7,3},{8,12},{12,8},{9,1... | collective-permute-start | bytes 3145736 | tf_op jit(solution)/shard_map/ppermute | solution.py:28
  62.2 18.7 %all-to-all-start.4 = ((bf16[4,512,256]{2,1,0:T(8,128)(2,1)}), bf16[4,512,256]{2,1,0:T(8,128)(2,1)S(1)}, u32[]{:S(2)}, u32[]{:S(2)}) async-start(bf16[4,512,256]{2,1,0:T(8,128)(2,1)} %broadcast_in_dim.28), calls=%async_computation.4 | async-start | bytes 2097152 | tf_op jit(solution)/shard_map/all_to_all | solution.py:20
  80.9 27.0 %collective-permute-start.3 = (bf16[2048,256]{1,0:T(8,128)(2,1)S(1)}, bf16[2048,256]{1,0:T(8,128)(2,1)S(1)}, u32[]{:S(2)}, u32[]{:S(2)}) collective-permute-start(bf16[2048,256]{1,0:T(8,128)(2,1)S(1)} %bitcast.90), channel_id=1, source_target_pairs={{0,4},{4,0},{1,5},{5,1},{2,6},{6,2},{3,7},{7,3},{8,12},{12,8},{9,1... | collective-permute-start | bytes 3145736 | tf_op jit(solution)/shard_map/ppermute | solution.py:28
  100.6 6.4 %copy-start.6 = (f32[32,128]{1,0:T(8,128)S(1)}, f32[32,128]{1,0:T(8,128)}, u32[]{:S(2)}) copy-start(f32[32,128]{1,0:T(8,128)} %get-tuple-element.28) | copy-start | bytes 49156
  108.2 1.0 copy-start.1
  109.1 2.1 copy-start.4
  112.3 16.5 %all-to-all-start.5 = ((bf16[8,192,256]{2,1,0:T(8,128)(2,1)}), bf16[8,192,256]{2,1,0:T(8,128)(2,1)S(1)}, u32[]{:S(2)}, u32[]{:S(2)}) async-start(bf16[8,192,256]{2,1,0:T(8,128)(2,1)} %pad_maximum_fusion), calls=%async_computation.5 | async-start | bytes 1572864 | tf_op jit(solution)/shard_map/all_to_all | solution.py:20
  128.8 16.9 %all-to-all-start.3 = ((bf16[8,192,256]{2,1,0:T(8,128)(2,1)}), bf16[8,192,256]{2,1,0:T(8,128)(2,1)S(1)}, u32[]{:S(2)}, u32[]{:S(2)}) async-start(bf16[8,192,256]{2,1,0:T(8,128)(2,1)} %bitcast.9), calls=%async_computation.3 | async-start | bytes 1572864 | tf_op jit(solution)/shard_map/all_to_all | solution.py:20
  134.1 16.4 %copy-start.2 = (f32[32,256]{1,0:T(8,128)S(1)}, f32[32,256]{1,0:T(8,128)}, u32[]{:S(2)}) copy-start(f32[32,256]{1,0:T(8,128)} %param.10) | copy-start | bytes 98308
  134.1 16.4 %copy-start.5 = (f32[32,256]{1,0:T(8,128)S(1)}, f32[32,256]{1,0:T(8,128)}, u32[]{:S(2)}) copy-start(f32[32,256]{1,0:T(8,128)} %param.11) | copy-start | bytes 98308
  146.9 13.7 %all-to-all-start.6 = ((bf16[16,40,256]{2,1,0:T(8,128)(2,1)}), bf16[16,40,256]{2,1,0:T(8,128)(2,1)S(1)}, u32[]{:S(2)}, u32[]{:S(2)}) async-start(bf16[16,40,256]{2,1,0:T(8,128)(2,1)} %fusion.4), calls=%async_computation.6 | async-start | bytes 655360 | tf_op jit(solution)/shard_map/all_to_all | solution.py:20
  150.5 10.2 %collective-permute-start = (f32[2,32,256]{2,1,0:T(8,128)S(1)}, f32[2,32,256]{2,1,0:T(8,128)S(1)}, u32[]{:S(2)}, u32[]{:S(2)}) collective-permute-start(f32[2,32,256]{2,1,0:T(8,128)S(1)} %pad_maximum_fusion.3), channel_id=1, source_target_pairs={{0,0},{4,32},{8,64},{12,96},{16,128},{20,160},{24,192},{28,224},{3... | collective-permute-start | bytes 196616 | tf_op jit(solution)/shard_map/ppermute | solution.py:244
  161.5 28.1 %all-to-all-start.7 = ((bf16[16,32,256]{2,1,0:T(8,128)(2,1)}), bf16[16,32,256]{2,1,0:T(8,128)(2,1)S(1)}, u32[]{:S(2)}, u32[]{:S(2)}) async-start(bf16[16,32,256]{2,1,0:T(8,128)(2,1)} %broadcast_in_dim.30), calls=%async_computation.7 | async-start | bytes 524288 | tf_op jit(solution)/shard_map/all_to_all | solution.py:20
  171.4 5.2 %collective-permute-start.4 = (f32[4,128]{1,0:T(4,128)S(1)}, f32[4,128]{1,0:T(4,128)S(1)}, u32[]{:S(2)}, u32[]{:S(2)}) collective-permute-start(f32[4,128]{1,0:T(4,128)S(1)} %slice_add_fusion), channel_id=1, source_target_pairs={{0,1},{1,0},{2,3},{3,2},{4,5},{5,4},{6,7},{7,6},{8,9},{9,8},{10,11... | collective-permute-start | bytes 6152 | tf_op jit(solution)/shard_map/ppermute | solution.py:28
  176.6 6.4 %collective-permute-start.5 = (f32[4,128]{1,0:T(4,128)S(1)}, f32[4,128]{1,0:T(4,128)S(1)}, u32[]{:S(2)}, u32[]{:S(2)}) collective-permute-start(f32[4,128]{1,0:T(4,128)S(1)} %fusion.36), channel_id=1, source_target_pairs={{0,3},{1,2},{2,1},{3,0},{4,7},{5,6},{6,5},{7,4},{8,11},{9,10},{10,... | collective-permute-start | bytes 6152 | tf_op jit(solution)/shard_map/ppermute | solution.py:28
  183.0 6.6 %collective-permute-start.6 = (f32[4,128]{1,0:T(4,128)S(1)}, f32[4,128]{1,0:T(4,128)S(1)}, u32[]{:S(2)}, u32[]{:S(2)}) collective-permute-start(f32[4,128]{1,0:T(4,128)S(1)} %add_select_fusion), channel_id=1, source_target_pairs={{0,4},{4,0},{1,5},{5,1},{2,6},{6,2},{3,7},{7,3},{8,12},{12,8},{9,1... | collective-permute-start | bytes 6152 | tf_op jit(solution)/shard_map/ppermute | solution.py:28
  190.7 23.5 %all-to-all-start.8 = ((bf16[4,16,32,256]{3,2,1,0:T(8,128)(2,1)}), bf16[4,16,32,256]{3,2,1,0:T(8,128)(2,1)S(1)}, u32[]{:S(2)}, u32[]{:S(2)}) async-start(bf16[4,16,32,256]{3,2,1,0:T(8,128)(2,1)} %broadcast_in_dim.31), calls=%async_computation.8 | async-start | bytes 2097152 | tf_op jit(solution)/shard_map/all_to_all | solution.py:20
  194.3 19.9 %collective-permute-start.9 = (f32[2,32,256]{2,1,0:T(8,128)S(1)}, f32[2,32,256]{2,1,0:T(8,128)S(1)}, u32[]{:S(2)}, u32[]{:S(2)}) collective-permute-start(f32[2,32,256]{2,1,0:T(8,128)S(1)} %pad_maximum_fusion.5), channel_id=1, source_target_pairs={{0,0},{32,4},{64,8},{96,12},{128,16},{160,20},{192,24},{224,28},{2... | collective-permute-start | bytes 196616 | tf_op jit(solution)/shard_map/ppermute | solution.py:339
  198.1 10.6 %collective-permute-start.7 = (f32[4,128]{1,0:T(4,128)S(1)}, f32[4,128]{1,0:T(4,128)S(1)}, u32[]{:S(2)}, u32[]{:S(2)}) collective-permute-start(f32[4,128]{1,0:T(4,128)S(1)} %add.71), channel_id=1, source_target_pairs={{0,8},{8,0},{16,24},{24,16},{1,9},{9,1},{17,25},{25,17},{2,10},{10... | collective-permute-start | bytes 6152 | tf_op jit(solution)/shard_map/ppermute | solution.py:28
  208.7 5.5 %collective-permute-start.8 = (f32[4,128]{1,0:T(4,128)S(1)}, f32[4,128]{1,0:T(4,128)S(1)}, u32[]{:S(2)}, u32[]{:S(2)}) collective-permute-start(f32[4,128]{1,0:T(4,128)S(1)} %add.72), channel_id=1, source_target_pairs={{0,24},{8,16},{16,8},{24,0},{1,25},{9,17},{17,9},{25,1},{2,26},{10... | collective-permute-start | bytes 6152 | tf_op jit(solution)/shard_map/ppermute | solution.py:28
  214.2 21.3 %collective-permute-start.10 = (bf16[2048,256]{1,0:T(8,128)(2,1)S(1)}, bf16[2048,256]{1,0:T(8,128)(2,1)S(1)}, u32[]{:S(2)}, u32[]{:S(2)}) collective-permute-start(bf16[2048,256]{1,0:T(8,128)(2,1)S(1)} %bitcast.88), channel_id=1, source_target_pairs={{0,4},{4,0},{1,5},{5,1},{2,6},{6,2},{3,7},{7,3},{8,12},{12,8},{9,1... | collective-permute-start | bytes 3145736 | tf_op jit(solution)/shard_map/ppermute | solution.py:28
  219.1 15.8 %all-to-all-start.9 = ((f32[16,4,128]{2,1,0:T(4,128)}), f32[16,4,128]{2,1,0:T(4,128)S(1)}, u32[]{:S(2)}, u32[]{:S(2)}) async-start(f32[16,4,128]{2,1,0:T(4,128)} %broadcast_in_dim.32), calls=%async_computation.9 | async-start | bytes 65536 | tf_op jit(solution)/shard_map/all_to_all | solution.py:20

commit v5 on v4

--- a/solution.py
+++ b/solution.py
@@ -28,18 +28,9 @@
     return lax.ppermute(x, axis, [(i, i ^ flip) for i in range(lax.axis_size(axis))])
 
 
-def in_parts(x):
+def in_two_parts(x):
     first = lax.reduce_precision(x, 8, 7)
-    second = lax.reduce_precision(x - first, 8, 7)
-    third = (x - first) - second
-    top = jnp.concatenate([first, second], axis=-1)
-    return jnp.concatenate([top, jnp.concatenate([third, jnp.zeros_like(third)], axis=-1)], axis=-2).astype(jnp.bfloat16)
-
-
-def from_parts(parts):
-    parts = parts.astype(jnp.float32)
-    top, low = parts[..., :4, :], parts[..., 4:, :]
-    return (top[..., :128] + top[..., 128:]) + low[..., :128]
+    return jnp.concatenate([first, x - first], axis=0).astype(jnp.bfloat16)
 
 
 def doubled(x, axis, flip):
@@ -215,12 +206,9 @@
     )(normed_grad, normed_first, normed_last, inv_scale, embedded)
 
 
-def both_halves(half, order=None):
+def both_cores(half, dims, axes):
     other = swapped(half, "c", 1)
     high = lax.axis_index("c") == 1
-    if order is None:
-        return jnp.where(high, jnp.stack([other, half]), jnp.stack([half, other])).reshape(-1, *half.shape[1:])
-    dims, axes = order
     both = [h.reshape(*dims, *half.shape[1:]) for h in (half, other)]
     both = jnp.where(high, jnp.stack(both[::-1]), jnp.stack(both))
     return jnp.transpose(both, axes).reshape(-1, *half.shape[1:])
@@ -229,7 +217,6 @@
 def per_device(feature_ids, emb_table, factor_machine_projection, mlp_weight, momentum, hidden_grad, lcb_grad):
     mp, zl, y, x, c = (lax.axis_size(a) for a in ("mp", "zl", "y", "x", "c"))
     own = emb_table.shape[0]
-    rank = factor_machine_projection.shape[1]
     examples, hidden = hidden_grad.shape
 
     to_worker = []
@@ -249,23 +236,24 @@
     weights = table[:, near_rows:].reshape(y, hidden // width, -1, width)
     weights = jnp.swapaxes(weights, 1, 2).reshape(-1, hidden)
     weights = doubled(weights, "zl", 1)
-    table = from_everyone(table[:, :near_rows], "x").reshape(-1, width)
-    weights, table = tied(weights, table)
-    table_far = swapped(table, "c", 1)
-    weights = from_everyone(weights, "x").reshape(-1, hidden)
+    weights = jnp.broadcast_to(weights, (x, *weights.shape))
     owner, row = lax.div(feature_ids, own), lax.rem(feature_ids, own)
     owner, at_mp = lax.div(owner, mp), lax.rem(owner, mp)
     owner, at_c = lax.div(owner, c), lax.rem(owner, c)
     owner, at_x = lax.div(owner, x), lax.rem(owner, x)
     at_zl, at_y = lax.div(owner, y), lax.rem(owner, y)
     ids = (((((at_c ^ lax.axis_index("c")) * x + at_x) * y + at_y) * mp + at_mp) * zl + at_zl) * own + row
+    table = from_everyone(table[:, :near_rows], "x").reshape(-1, width)
+    weights, table = tied(weights, table)
+    table_far = swapped(table, "c", 1)
+    weights = exchange(weights, "x").reshape(-1, hidden)
 
     blocks = 2 * c * x
     cut = int(examples * FIRST_SHARE)
     shares = ((0, cut), (cut, examples - cut))
     inputs = (ids, table, table_far, factor_machine_projection, lcb_grad)
     embedded, normed_a, inv_scale, lcb_a = forward_features(*inputs, blocks, *shares[0])
-    weights = both_halves(weights, ((x, zl, y, mlp_weight.shape[0]), (2, 3, 1, 0, 4, 5)))
+    weights = both_cores(weights, (x, zl, y, mlp_weight.shape[0]), (2, 3, 1, 0, 4, 5))
     embedded, normed_b, inv_scale, lcb_b = forward_features(
         *inputs, blocks, *shares[1], (embedded, inv_scale)
     )
@@ -296,8 +284,6 @@
 
     normed_part = lax.dot_general(preact_grad, weights, (((1,), (1,)), ((), ())), preferred_element_type=jnp.float32)
     proj_part = backward_features(normed_part, normed_a, normed_b, inv_scale, embedded)
-    both = jnp.concatenate([proj_part.T, lcb_a + lcb_b], axis=0)
-
     (start_a, count_a), (start_b, count_b) = shares
     weight_grad = jnp.einsum(
         "shbk,sbn->hkn",
@@ -315,34 +301,30 @@
             for at in (examples, examples + count_b)
         ]
     )
-    arrived = exchange(
-        jnp.concatenate(
-            [
-                weight_grad.astype(jnp.bfloat16).reshape(zl * y, -1, hidden),
-                in_parts(both.reshape(zl * y, -1, both.shape[1])),
-            ],
-            axis=1,
-        ),
-        ZY,
-    )
-    own_rows = weight_rows.shape[0]
-    both = from_parts(summed(arrived[:, own_rows:]))
-    new_momentum = 0.9 * momentum_rows + summed(arrived[:, :own_rows])
+    arrived = exchange(weight_grad.astype(jnp.bfloat16).reshape(zl * y, -1, hidden), ZY)
+    small = proj_part.T
+    small += swapped(small, "mp", 1)
+    small += swapped(small, "mp", 3)
+    small = jnp.concatenate([small, lcb_a + lcb_b], axis=1)
+    arrived, small = tied(arrived, small)
+    new_momentum = 0.9 * momentum_rows + summed(arrived)
     new_weight = weight_rows - 0.01 * new_momentum
-    next_weight = from_everyone(new_weight.astype(jnp.bfloat16), ZY)
-    over_mp = both + swapped(both, "mp", 1)
-    over_mp += swapped(over_mp, "mp", 3)
-    both = jnp.where(lax.axis_index("zl") == 0, over_mp, both)
-    both += swapped(both, "c", 1)
-    next_weight, both = tied(next_weight, both)
-    next_weight = from_everyone(next_weight, "x").reshape(-1, hidden)
+    own_rows = new_weight.shape[0]
+    arrived = from_everyone(jnp.concatenate([new_weight, small], axis=0).astype(jnp.bfloat16), ZY)
+    next_weight = arrived[:, :own_rows].reshape(-1, hidden)
+    small = in_two_parts(summed(arrived[:, own_rows:]))
+    column_rows = next_weight.shape[0]
+    arrived = from_everyone(jnp.concatenate([next_weight, small], axis=0), "x")
     state = lax.ppermute(jnp.stack([new_weight, new_momentum]), DP, to_owner)
-    both += swapped(both, "x", 1)
-    both += swapped(both, "x", 3)
-    next_weight, both, state = tied(next_weight, both, state)
-    next_weight = both_halves(next_weight)
-    both = from_everyone(both, ZY).reshape(2 * rank, -1)
-    return (state[0], state[1], next_weight, both[:rank].T, both[rank:].T)
+    arrived, state = tied(arrived, state)
+    other = swapped(arrived, "c", 1)
+    high = lax.axis_index("c") == 1
+    halves = [h[:, :column_rows] for h in (arrived, other)]
+    next_weight = jnp.where(high, jnp.stack(halves[::-1]), jnp.stack(halves)).reshape(-1, hidden)
+    small = [summed(h[:, column_rows:].reshape(2 * x, -1, hidden)) for h in (arrived, other)]
+    small = small[0] + small[1]
+    n_emb = small.shape[1] // 2
+    return (state[0], state[1], next_weight, small[:, :n_emb].T, small[:, n_emb:].T)
 
 
 def solution(mesh):

time: 239 us -> 232 us (0.971)
  blocking collectives: 18.2 us -> 57.4 us
  starting transfers between devices: 94.6 us -> 66 us
  waiting for transfers between devices: 69.2 us -> 52.3 us
    all_to_all x1 -> x3, blocking collectives: 18.2 us -> 57.4 us  [exchange(): return lax.all_to_all(tiles, axis, split_axis=0, concat_axis=0, tiled=True)]
    all_to_all x9 -> x6, starting transfers between devices: 52 us -> 30.1 us  [exchange(): return lax.all_to_all(tiles, axis, split_axis=0, concat_axis=0, tiled=True)]
    all_to_all x9 -> x6, waiting for transfers between devices: 49.9 us -> 38 us  [exchange(): return lax.all_to_all(tiles, axis, split_axis=0, concat_axis=0, tiled=True)]
    ppermute x9 -> x6, starting transfers between devices: 35.1 us -> 24 us  [swapped(): lax.ppermute(x, axis, [(i, i ^ flip) for i in range(lax.axis_size(axis))])]
    ppermute x9 -> x6, waiting for transfers between devices: 19.4 us -> 9.29 us  [swapped(): lax.ppermute(x, axis, [(i, i ^ flip) for i in range(lax.axis_size(axis))])]
    ppermute x1, starting transfers between devices: 3.79 us -> 6.5 us  [per_device(): state = lax.ppermute(jnp.stack([new_weight, new_momentum]), DP, to_owner)]
    ppermute x1, waiting for transfers between devices: 0.01 us -> 2.7 us  [per_device(): state = lax.ppermute(jnp.stack([new_weight, new_momentum]), DP, to_owner)]
    broadcast_in_dim x7 -> x5, local copies, waits for them, and re-layouts: 6.06 us -> 3.71 us  [from_everyone(): return exchange(jnp.broadcast_to(x, (lax.axis_size(axis), *x.shape)), axis)]
  transfers between devices with their start and end apart: 20 -> 14, of which waited for: 12 -> 10; matrix products, arithmetic and copies ran while one was open for 4% -> 3% of each run, Pallas kernels for 14% -> 14%
where the time goes in v5:
time: 232 us; the launch traced here: 229 us
  starting transfers between devices  66 us (28%)
  blocking collectives  57.4 us (25%)
  waiting for transfers between devices  52.3 us (23%)
  Pallas kernels  33.2 us (14%)
  local copies, waits for them, and re-layouts  7.49 us (3%)
  matrix products  6.9 us (3%)
  other arithmetic  4.76 us (2%)
    all_to_all x3, blocking collectives, exchange(): return lax.all_to_all(tiles, axis, split_axis=0, concat_axis=0, tiled=True)  57.4 us
    all_to_all x6, waiting for transfers between devices, exchange(): return lax.all_to_all(tiles, axis, split_axis=0, concat_axis=0, tiled=True)  38 us
    all_to_all x6, starting transfers between devices, exchange(): return lax.all_to_all(tiles, axis, split_axis=0, concat_axis=0, tiled=True)  30.1 us
    ppermute x6, starting transfers between devices, swapped(): lax.ppermute(x, axis, [(i, i ^ flip) for i in range(lax.axis_size(axis))])  24 us
    pallas_call x2, Pallas kernels, forward_features(): pl.pallas_call(forward_kernel, grid=(count // GROUP,), in_specs=[pl.Block...  23.3 us
    pallas_call x1, Pallas kernels, backward_features(): pl.pallas_call(backward_kernel, grid=(firsts + 1,), in_specs=[pl.BlockSpe...  9.87 us
    ppermute x6, waiting for transfers between devices, swapped(): lax.ppermute(x, axis, [(i, i ^ flip) for i in range(lax.axis_size(axis))])  9.29 us
    ppermute x1, starting transfers between devices, per_device(): state = lax.ppermute(jnp.stack([new_weight, new_momentum]), DP, to_owner)  6.5 us
  transfers between devices with their start and end apart: 14, of which 10 were waited for; matrix products, arithmetic and copies ran while one was open for 3% of the time, Pallas kernels for 14%

profile of v5, /device:TPU:1, one launch (start us, length us, event | category | flops | bytes accessed | tf_op | source)
XLA Modules:
  0.0 229.2 jit_solution(3998891366008417724)
XLA Ops:
  0.6 1.3 broadcast_in_dim.21
  1.9 10.9 %all-to-all-start = ((bf16[8,16,128]{2,1,0:T(8,128)(2,1)}), bf16[8,16,128]{2,1,0:T(8,128)(2,1)S(1)}, u32[]{:S(2)}, u32[]{:S(2)}) async-start(bf16[8,16,128]{2,1,0:T(8,128)(2,1)} %broadcast_in_dim.21), calls=%async_computation | async-start | bytes 65536 | tf_op jit(solution)/shard_map/all_to_all | solution.py:20
  12.8 0.8 convert_element_type.32
  13.6 6.1 %all-to-all-done = bf16[8,16,128]{2,1,0:T(8,128)(2,1)S(1)} async-done(((bf16[8,16,128]{2,1,0:T(8,128)(2,1)}), bf16[8,16,128]{2,1,0:T(8,128)(2,1)S(1)}, u32[]{:S(2)}, u32[]{:S(2)}) %all-to-all-start) | async-done | bytes 32800 | tf_op jit(solution)/shard_map/all_to_all | solution.py:20
  19.7 0.1 broadcast_in_dim.22
  19.7 18.2 %all_to_all.45 = bf16[8,192,128]{2,1,0:T(8,128)(2,1)S(1)} all-to-all(bf16[8,192,128]{2,1,0:T(8,128)(2,1)S(1)} %broadcast_in_dim.22), channel_id=1, replica_groups=mesh['zl'=2,'y'=8,'x'=4,'c'=2,'mp'=4] {'y'}, dimensions={0} | all-to-all | bytes 786432 | tf_op jit(solution)/shard_map/all_to_all | solution.py:20
  38.0 1.2 broadcast_in_dim.24
  39.2 4.0 %all-to-all-start.2 = ((bf16[4,8,128,128]{3,2,1,0:T(8,128)(2,1)}), bf16[4,8,128,128]{3,2,1,0:T(8,128)(2,1)S(1)}, u32[]{:S(2)}, u32[]{:S(2)}) async-start(bf16[4,8,128,128]{3,2,1,0:T(8,128)(2,1)} %broadcast_in_dim.24), calls=%async_computation.2 | async-start | bytes 2097152 | tf_op jit(solution)/shard_map/all_to_all | solution.py:20
  43.2 0.1 copy.39
  43.3 2.2 collective-permute-start.1
  45.6 3.5 %collective-permute-done.1 = bf16[256,256]{1,0:T(8,128)(2,1)S(1)} collective-permute-done((bf16[256,256]{1,0:T(8,128)(2,1)S(1)}, bf16[256,256]{1,0:T(8,128)(2,1)S(1)}, u32[]{:S(2)}, u32[]{:S(2)}) %collective-permute-start.1) | collective-permute-done | bytes 131104 | tf_op jit(solution)/shard_map/ppermute | solution.py:28
  49.1 0.0 copy-start.3
  49.1 4.6 %all-to-all-done.2 = bf16[4,8,128,128]{3,2,1,0:T(8,128)(2,1)S(1)} async-done(((bf16[4,8,128,128]{3,2,1,0:T(8,128)(2,1)}), bf16[4,8,128,128]{3,2,1,0:T(8,128)(2,1)S(1)}, u32[]{:S(2)}, u32[]{:S(2)}) %all-to-all-start.2) | async-done | bytes 1048608 | tf_op jit(solution)/shard_map/all_to_all | solution.py:20
  53.8 1.1 broadcast_in_dim.23
  54.9 7.4 %collective-permute-start.2 = (bf16[4096,128]{1,0:T(8,128)(2,1)S(1)}, bf16[4096,128]{1,0:T(8,128)(2,1)}, u32[]{:S(2)}, u32[]{:S(2)}) collective-permute-start(bf16[4096,128]{1,0:T(8,128)(2,1)S(1)} %bitcast.98), channel_id=1, source_target_pairs={{0,4},{4,0},{1,5},{5,1},{2,6},{6,2},{3,7},{7,3},{8,12},{12,8},{9,1... | collective-permute-start | bytes 3145736 | tf_op jit(solution)/shard_map/ppermute | solution.py:28
  62.3 3.5 %all-to-all-start.4 = ((bf16[4,512,256]{2,1,0:T(8,128)(2,1)}), bf16[4,512,256]{2,1,0:T(8,128)(2,1)S(1)}, u32[]{:S(2)}, u32[]{:S(2)}) async-start(bf16[4,512,256]{2,1,0:T(8,128)(2,1)} %broadcast_in_dim.23), calls=%async_computation.4 | async-start | bytes 2097152 | tf_op jit(solution)/shard_map/all_to_all | solution.py:20
  65.8 0.8 fusion.17.ids_ref
  66.6 14.4 %all-to-all-done.4 = bf16[4,512,256]{2,1,0:T(8,128)(2,1)S(1)} async-done(((bf16[4,512,256]{2,1,0:T(8,128)(2,1)}), bf16[4,512,256]{2,1,0:T(8,128)(2,1)S(1)}, u32[]{:S(2)}, u32[]{:S(2)}) %all-to-all-start.4) | async-done | bytes 1048608 | tf_op jit(solution)/shard_map/all_to_all | solution.py:20
  81.0 2.8 %collective-permute-start.3 = (bf16[2048,256]{1,0:T(8,128)(2,1)S(1)}, bf16[2048,256]{1,0:T(8,128)(2,1)S(1)}, u32[]{:S(2)}, u32[]{:S(2)}) collective-permute-start(bf16[2048,256]{1,0:T(8,128)(2,1)S(1)} %bitcast.92), channel_id=1, source_target_pairs={{0,4},{4,0},{1,5},{5,1},{2,6},{6,2},{3,7},{7,3},{8,12},{12,8},{9,1... | collective-permute-start | bytes 3145736 | tf_op jit(solution)/shard_map/ppermute | solution.py:28
  83.7 0.0 collective-permute-done.2.far_ref
  83.8 16.9 %fm_forward.2 = (bf16[128,128,128]{2,1,0:T(8,128)(2,1)}, bf16[16,96,256]{2,1,0:T(8,128)(2,1)}, f32[128,128]{1,0:T(8,128)}, f32[32,128]{1,0:T(8,128)}) custom-call(s32[128,128]{1,0:T(8,128)} %fusion.17.ids_ref, bf16[4096,128]{1,0:T(8,128)(2,1)} %bitcast.99, bf16[4096,128]{1,0:T(8,128)(2,1)} %collective-permute-done.2.far_ref, bf16[32,128]{1,0:T(8,128)(2,1)} %bitcast.111, ...), custom_call_target="tpu_custom_call" | custom-call | flops 9600000000 | bytes 5242880 | tf_op jit(solution)/shard_map/fm_forward/pallas_call | solution.py:109
  100.7 6.4 %fm_forward.3 = (bf16[128,128,128]{2,1,0:T(8,128)(2,1)}, bf16[16,32,256]{2,1,0:T(8,128)(2,1)}, f32[128,128]{1,0:T(8,128)}, f32[32,128]{1,0:T(8,128)}) custom-call(s32[128,128]{1,0:T(8,128)} %fusion.17.ids_ref, bf16[4096,128]{1,0:T(8,128)(2,1)} %bitcast.100, ...), custom_call_target="tpu_custom_call", output_to_operand_aliasing={{0}: (5, {}), {2}: (6, {})} | custom-call | flops 3200000000 | bytes 3145728 | tf_op jit(solution)/shard_map/fm_forward/pallas_call | solution.py:109
  107.1 0.0 collective-permute-done.3
  107.1 0.3 fusion
  107.4 0.2 copy.40
  107.7 0.7 copy-done.1
  108.4 0.5 convolution_bitcast_fusion.4
  108.8 1.6 convolution_bitcast_fusion.3
  110.5 0.1 multiply_convert_fusion
  110.6 0.1 pad_maximum_fusion
  110.6 14.6 %all_to_all.46 = bf16[8,192,256]{2,1,0:T(8,128)(2,1)S(1)} all-to-all(bf16[8,192,256]{2,1,0:T(8,128)(2,1)S(1)} %pad_maximum_fusion), channel_id=1, replica_groups=mesh['zl'=2,'y'=8,'x'=4,'c'=2,'mp'=4] {'c','x'}, dimensions={0} | all-to-all | bytes 1572864 | tf_op jit(solution)/shard_map/all_to_all | solution.py:20
  125.2 4.4 %all-to-all-start.3 = ((bf16[8,192,256]{2,1,0:T(8,128)(2,1)}), bf16[8,192,256]{2,1,0:T(8,128)(2,1)}, u32[]{:S(2)}, u32[]{:S(2)}) async-start(bf16[8,192,256]{2,1,0:T(8,128)(2,1)} %bitcast.9), calls=%async_computation.3 | async-start | bytes 1572864 | tf_op jit(solution)/shard_map/all_to_all | solution.py:20
  129.7 2.1 fusion.25.grad_ref
  131.8 0.2 convolution_bitcast_fusion.1
  132.0 0.2 convolution_bitcast_fusion.2
  132.2 9.7 %all-to-all-done.3 = bf16[8,192,256]{2,1,0:T(8,128)(2,1)} async-done(((bf16[8,192,256]{2,1,0:T(8,128)(2,1)}), bf16[8,192,256]{2,1,0:T(8,128)(2,1)}, u32[]{:S(2)}, u32[]{:S(2)}) %all-to-all-start.3) | async-done | bytes 786464 | tf_op jit(solution)/shard_map/all_to_all | solution.py:20
  141.9 2.3 fusion.2
  144.2 3.7 %all-to-all-start.6 = ((bf16[16,32,256]{2,1,0:T(8,128)(2,1)}), bf16[16,32,256]{2,1,0:T(8,128)(2,1)S(1)}, u32[]{:S(2)}, u32[]{:S(2)}) async-start(bf16[16,32,256]{2,1,0:T(8,128)(2,1)} %bitcast.26), calls=%async_computation.6 | async-start | bytes 524288 | tf_op jit(solution)/shard_map/all_to_all | solution.py:20
  147.9 0.0 copy-start.2
  147.9 0.0 copy-start.5
  148.0 0.0 copy-start.6
  148.0 0.0 copy-start.7
  148.0 9.9 %fm_backward.1 = f32[128,32]{1,0:T(8,128)} custom-call(f32[128,4096]{1,0:T(8,128)} %fusion.25.grad_ref, bf16[16,96,256]{2,1,0:T(8,128)(2,1)} %get-tuple-element.20.first_ref, bf16[16,32,256]{2,1,0:T(8,128)(2,1)} %get-tuple-element.24.last_ref, f32[128,128]{1,0:T(8,128)} %get-tuple-element.25.inv_ref, bf16[128,128,128]{2,1,0:T(8,128)(2,1)} %get-tuple-element.26.emb_ref), custom_call_target="tpu_custom_call" | custom-call | flops 5120000000 | bytes 7340032 | tf_op jit(solution)/shard_map/fm_backward/pallas_call | solution.py:187
  157.8 2.1 collective-permute-start.4
  159.9 4.0 %collective-permute-done.4 = f32[32,128]{0,1:T(8,128)S(1)} collective-permute-done((f32[32,128]{0,1:T(8,128)}, f32[32,128]{0,1:T(8,128)S(1)}, u32[]{:S(2)}, u32[]{:S(2)}) %collective-permute-start.4) | collective-permute-done | bytes 16416 | tf_op jit(solution)/shard_map/ppermute | solution.py:28
  164.0 0.9 bitcast_add_fusion.2
  164.8 2.7 %collective-permute-start.5 = (f32[32,128]{0,1:T(8,128)S(1)}, f32[32,128]{0,1:T(8,128)S(1)}, u32[]{:S(2)}, u32[]{:S(2)}) collective-permute-start(f32[32,128]{0,1:T(8,128)S(1)} %bitcast_add_fusion.2), channel_id=1, source_target_pairs={{0,3},{1,2},{2,1},{3,0},{4,7},{5,6},{6,5},{7,4},{8,11},{9,10},{10,... | collective-permute-start | bytes 49160 | tf_op jit(solution)/shard_map/ppermute | solution.py:28
  167.5 5.5 %collective-permute-start = (f32[2,32,256]{2,1,0:T(8,128)S(1)}, f32[2,32,256]{2,1,0:T(8,128)S(1)}, u32[]{:S(2)}, u32[]{:S(2)}) collective-permute-start(f32[2,32,256]{2,1,0:T(8,128)S(1)} %pad_maximum_fusion.4), channel_id=1, source_target_pairs={{0,0},{4,32},{8,64},{12,96},{16,128},{20,160},{24,192},{28,224},{3... | collective-permute-start | bytes 196616 | tf_op jit(solution)/shard_map/ppermute | solution.py:231
  173.1 0.0 collective-permute-done.5
  173.1 0.1 copy.42
  173.2 2.3 %collective-permute-done = f32[2,32,256]{2,1,0:T(8,128)S(1)} collective-permute-done((f32[2,32,256]{2,1,0:T(8,128)S(1)}, f32[2,32,256]{2,1,0:T(8,128)S(1)}, u32[]{:S(2)}, u32[]{:S(2)}) %collective-permute-start) | collective-permute-done | bytes 65568 | tf_op jit(solution)/shard_map/ppermute | solution.py:231
  175.6 24.6 %all_to_all.47 = bf16[16,64,256]{2,1,0:T(8,128)(2,1)S(1)} all-to-all(bf16[16,64,256]{2,1,0:T(8,128)(2,1)S(1)} %broadcast_in_dim.26), channel_id=1, replica_groups=mesh['zl'=2,'y'=8,'x'=4,'c'=2,'mp'=4] {'zl','y'}, dimensions={0} | all-to-all | bytes 1048576 | tf_op jit(solution)/shard_map/all_to_all | solution.py:20
  200.4 1.1 broadcast_in_dim.27
  201.5 3.5 %all-to-all-start.8 = ((bf16[4,576,256]{2,1,0:T(8,128)(2,1)}), bf16[4,576,256]{2,1,0:T(8,128)(2,1)S(1)}, u32[]{:S(2)}, u32[]{:S(2)}) async-start(bf16[4,576,256]{2,1,0:T(8,128)(2,1)} %broadcast_in_dim.27), calls=%async_computation.8 | async-start | bytes 2359296 | tf_op jit(solution)/shard_map/all_to_all | solution.py:20
  205.0 6.5 %collective-permute-start.6 = (f32[2,32,256]{2,1,0:T(8,128)S(1)}, f32[2,32,256]{2,1,0:T(8,128)S(1)}, u32[]{:S(2)}, u32[]{:S(2)}) collective-permute-start(f32[2,32,256]{2,1,0:T(8,128)S(1)} %pad_maximum_fusion.5), channel_id=1, source_target_pairs={{0,0},{32,4},{64,8},{96,12},{128,16},{160,20},{192,24},{224,28},{2... | collective-permute-start | bytes 196616 | tf_op jit(solution)/shard_map/ppermute | solution.py:318
  211.6 2.7 %collective-permute-done.6 = f32[2,32,256]{2,1,0:T(8,128)S(1)} collective-permute-done((f32[2,32,256]{2,1,0:T(8,128)S(1)}, f32[2,32,256]{2,1,0:T(8,128)S(1)}, u32[]{:S(2)}, u32[]{:S(2)}) %collective-permute-start.6) | collective-permute-done | bytes 65568 | tf_op jit(solution)/shard_map/ppermute | solution.py:318
  214.3 3.2 %all-to-all-done.8 = bf16[4,576,256]{2,1,0:T(8,128)(2,1)S(1)} async-done(((bf16[4,576,256]{2,1,0:T(8,128)(2,1)}), bf16[4,576,256]{2,1,0:T(8,128)(2,1)S(1)}, u32[]{:S(2)}, u32[]{:S(2)}) %all-to-all-start.8) | async-done | bytes 1179680 | tf_op jit(solution)/shard_map/all_to_all | solution.py:20
  217.4 6.9 %collective-permute-start.7 = (bf16[4,576,256]{2,1,0:T(8,128)(2,1)S(1)}, bf16[4,576,256]{2,1,0:T(8,128)(2,1)S(1)}, u32[]{:S(2)}, u32[]{:S(2)}) collective-permute-start(bf16[4,576,256]{2,1,0:T(8,128)(2,1)S(1)} %all-to-all-done.8), channel_id=1, source_target_pairs={{0,4},{4,0},{1,5},{5,1},{2,6},{6,2},{3,7},{7,3},{8,12},{12,8},{9,1... | collective-permute-start | bytes 3538952 | tf_op jit(solution)/shard_map/ppermute | solution.py:28
  224.4 0.6 slice_bitcast_fusion.4
  225.0 0.1 slice_bitcast_fusion.1
  225.1 1.7 collective-permute-done.7
  226.9 0.6 slice_bitcast_fusion.6
  227.5 0.1 slice_bitcast_fusion
  227.5 1.6 maximum_select_fusion.1
  (37 shorter events, 0.5 us)
Async XLA Ops:
  1.9 17.7 %all-to-all-start = ((bf16[8,16,128]{2,1,0:T(8,128)(2,1)}), bf16[8,16,128]{2,1,0:T(8,128)(2,1)S(1)}, u32[]{:S(2)}, u32[]{:S(2)}) async-start(bf16[8,16,128]{2,1,0:T(8,128)(2,1)} %broadcast_in_dim.21), calls=%async_computation | async-start | bytes 65536 | tf_op jit(solution)/shard_map/all_to_all | solution.py:20
  39.2 14.6 %all-to-all-start.2 = ((bf16[4,8,128,128]{3,2,1,0:T(8,128)(2,1)}), bf16[4,8,128,128]{3,2,1,0:T(8,128)(2,1)S(1)}, u32[]{:S(2)}, u32[]{:S(2)}) async-start(bf16[4,8,128,128]{3,2,1,0:T(8,128)(2,1)} %broadcast_in_dim.24), calls=%async_computation.2 | async-start | bytes 2097152 | tf_op jit(solution)/shard_map/all_to_all | solution.py:20
  43.3 5.7 %collective-permute-start.1 = (bf16[256,256]{1,0:T(8,128)(2,1)S(1)}, bf16[256,256]{1,0:T(8,128)(2,1)S(1)}, u32[]{:S(2)}, u32[]{:S(2)}) collective-permute-start(bf16[256,256]{1,0:T(8,128)(2,1)S(1)} %bitcast.107), channel_id=1, source_target_pairs={{0,256},{256,0},{1,257},{257,1},{2,258},{258,2},{3,259},{259,3},{4... | collective-permute-start | bytes 393224 | tf_op jit(solution)/shard_map/ppermute | solution.py:28
  49.1 16.7 %copy-start.3 = (s32[128,128]{1,0:T(8,128)S(1)}, s32[128,128]{1,0:T(8,128)}, u32[]{:S(2)}) copy-start(s32[128,128]{1,0:T(8,128)} %param.7) | copy-start | bytes 196612
  53.8 30.0 %copy-start = (bf16[4,8,128,128]{3,2,1,0:T(8,128)(2,1)}, bf16[4,8,128,128]{3,2,1,0:T(8,128)(2,1)S(1)}, u32[]{:S(2)}) copy-start(bf16[4,8,128,128]{3,2,1,0:T(8,128)(2,1)S(1)} %all-to-all-done.2) | copy-start | bytes 3145732
  54.9 28.8 %collective-permute-start.2 = (bf16[4096,128]{1,0:T(8,128)(2,1)S(1)}, bf16[4096,128]{1,0:T(8,128)(2,1)}, u32[]{:S(2)}, u32[]{:S(2)}) collective-permute-start(bf16[4096,128]{1,0:T(8,128)(2,1)S(1)} %bitcast.98), channel_id=1, source_target_pairs={{0,4},{4,0},{1,5},{5,1},{2,6},{6,2},{3,7},{7,3},{8,12},{12,8},{9,1... | collective-permute-start | bytes 3145736 | tf_op jit(solution)/shard_map/ppermute | solution.py:28
  62.3 18.7 %all-to-all-start.4 = ((bf16[4,512,256]{2,1,0:T(8,128)(2,1)}), bf16[4,512,256]{2,1,0:T(8,128)(2,1)S(1)}, u32[]{:S(2)}, u32[]{:S(2)}) async-start(bf16[4,512,256]{2,1,0:T(8,128)(2,1)} %broadcast_in_dim.23), calls=%async_computation.4 | async-start | bytes 2097152 | tf_op jit(solution)/shard_map/all_to_all | solution.py:20
  81.0 26.1 %collective-permute-start.3 = (bf16[2048,256]{1,0:T(8,128)(2,1)S(1)}, bf16[2048,256]{1,0:T(8,128)(2,1)S(1)}, u32[]{:S(2)}, u32[]{:S(2)}) collective-permute-start(bf16[2048,256]{1,0:T(8,128)(2,1)S(1)} %bitcast.92), channel_id=1, source_target_pairs={{0,4},{4,0},{1,5},{5,1},{2,6},{6,2},{3,7},{7,3},{8,12},{12,8},{9,1... | collective-permute-start | bytes 3145736 | tf_op jit(solution)/shard_map/ppermute | solution.py:28
  107.4 1.0 copy-start.1
  108.4 2.1 copy-start.4
  125.2 16.7 %all-to-all-start.3 = ((bf16[8,192,256]{2,1,0:T(8,128)(2,1)}), bf16[8,192,256]{2,1,0:T(8,128)(2,1)}, u32[]{:S(2)}, u32[]{:S(2)}) async-start(bf16[8,192,256]{2,1,0:T(8,128)(2,1)} %bitcast.9), calls=%async_computation.3 | async-start | bytes 1572864 | tf_op jit(solution)/shard_map/all_to_all | solution.py:20
  144.2 29.0 %all-to-all-start.6 = ((bf16[16,32,256]{2,1,0:T(8,128)(2,1)}), bf16[16,32,256]{2,1,0:T(8,128)(2,1)S(1)}, u32[]{:S(2)}, u32[]{:S(2)}) async-start(bf16[16,32,256]{2,1,0:T(8,128)(2,1)} %bitcast.26), calls=%async_computation.6 | async-start | bytes 524288 | tf_op jit(solution)/shard_map/all_to_all | solution.py:20
  147.9 19.6 %copy-start.2 = (f32[32,256]{1,0:T(8,128)S(1)}, f32[32,256]{1,0:T(8,128)}, u32[]{:S(2)}) copy-start(f32[32,256]{1,0:T(8,128)} %param.10) | copy-start | bytes 98308
  147.9 19.6 %copy-start.5 = (f32[32,256]{1,0:T(8,128)S(1)}, f32[32,256]{1,0:T(8,128)}, u32[]{:S(2)}) copy-start(f32[32,256]{1,0:T(8,128)} %param.11) | copy-start | bytes 98308
  148.0 25.1 %copy-start.6 = (f32[32,128]{1,0:T(8,128)S(1)}, f32[32,128]{1,0:T(8,128)}, u32[]{:S(2)}) copy-start(f32[32,128]{1,0:T(8,128)} %get-tuple-element.27) | copy-start | bytes 49156
  148.0 25.1 %copy-start.7 = (f32[32,128]{1,0:T(8,128)S(1)}, f32[32,128]{1,0:T(8,128)}, u32[]{:S(2)}) copy-start(f32[32,128]{1,0:T(8,128)} %get-tuple-element.28) | copy-start | bytes 49156
  157.8 6.1 %collective-permute-start.4 = (f32[32,128]{0,1:T(8,128)}, f32[32,128]{0,1:T(8,128)S(1)}, u32[]{:S(2)}, u32[]{:S(2)}) collective-permute-start(f32[32,128]{0,1:T(8,128)} %bitcast.109), channel_id=1, source_target_pairs={{0,1},{1,0},{2,3},{3,2},{4,5},{5,4},{6,7},{7,6},{8,9},{9,8},{10,11... | collective-permute-start | bytes 49160 | tf_op jit(solution)/shard_map/ppermute | solution.py:28
  164.8 8.3 %collective-permute-start.5 = (f32[32,128]{0,1:T(8,128)S(1)}, f32[32,128]{0,1:T(8,128)S(1)}, u32[]{:S(2)}, u32[]{:S(2)}) collective-permute-start(f32[32,128]{0,1:T(8,128)S(1)} %bitcast_add_fusion.2), channel_id=1, source_target_pairs={{0,3},{1,2},{2,1},{3,0},{4,7},{5,6},{6,5},{7,4},{8,11},{9,10},{10,... | collective-permute-start | bytes 49160 | tf_op jit(solution)/shard_map/ppermute | solution.py:28
  167.5 8.0 %collective-permute-start = (f32[2,32,256]{2,1,0:T(8,128)S(1)}, f32[2,32,256]{2,1,0:T(8,128)S(1)}, u32[]{:S(2)}, u32[]{:S(2)}) collective-permute-start(f32[2,32,256]{2,1,0:T(8,128)S(1)} %pad_maximum_fusion.4), channel_id=1, source_target_pairs={{0,0},{4,32},{8,64},{12,96},{16,128},{20,160},{24,192},{28,224},{3... | collective-permute-start | bytes 196616 | tf_op jit(solution)/shard_map/ppermute | solution.py:231
  201.5 16.0 %all-to-all-start.8 = ((bf16[4,576,256]{2,1,0:T(8,128)(2,1)}), bf16[4,576,256]{2,1,0:T(8,128)(2,1)S(1)}, u32[]{:S(2)}, u32[]{:S(2)}) async-start(bf16[4,576,256]{2,1,0:T(8,128)(2,1)} %broadcast_in_dim.27), calls=%async_computation.8 | async-start | bytes 2359296 | tf_op jit(solution)/shard_map/all_to_all | solution.py:20
  205.0 9.2 %collective-permute-start.6 = (f32[2,32,256]{2,1,0:T(8,128)S(1)}, f32[2,32,256]{2,1,0:T(8,128)S(1)}, u32[]{:S(2)}, u32[]{:S(2)}) collective-permute-start(f32[2,32,256]{2,1,0:T(8,128)S(1)} %pad_maximum_fusion.5), channel_id=1, source_target_pairs={{0,0},{32,4},{64,8},{96,12},{128,16},{160,20},{192,24},{224,28},{2... | collective-permute-start | bytes 196616 | tf_op jit(solution)/shard_map/ppermute | solution.py:318
  217.4 9.3 %collective-permute-start.7 = (bf16[4,576,256]{2,1,0:T(8,128)(2,1)S(1)}, bf16[4,576,256]{2,1,0:T(8,128)(2,1)S(1)}, u32[]{:S(2)}, u32[]{:S(2)}) collective-permute-start(bf16[4,576,256]{2,1,0:T(8,128)(2,1)S(1)} %all-to-all-done.8), channel_id=1, source_target_pairs={{0,4},{4,0},{1,5},{5,1},{2,6},{6,2},{3,7},{7,3},{8,12},{12,8},{9,1... | collective-permute-start | bytes 3538952 | tf_op jit(solution)/shard_map/ppermute | solution.py:28

commit v6 on v5

--- a/solution.py
+++ b/solution.py
@@ -169,12 +169,19 @@
         inv = inv_ref[rows, :1]
         for k in range(rank):
             fm_grad_ref[pl.ds(k, ROWS, stride=rank), :] = (grads[k] - mean - normed[k] * along) * inv
+        pairs, backs = [], []
         for e in range(0, ROWS, 2):
             fm_grad = fm_grad_ref[pl.ds(e * rank, 2 * rank), :].astype(jnp.bfloat16)
             pair = jnp.concatenate([emb_ref[start + e], emb_ref[start + e + 1]], axis=1)
             back = jnp.dot(fm_grad, pair, preferred_element_type=jnp.float32).astype(jnp.bfloat16)
-            back = jnp.concatenate([back[:rank, :width], back[rank:, width:]], axis=1)
-            proj += lax.dot_general(pair, back, (((1,), (1,)), ((), ())), preferred_element_type=jnp.float32)
+            pairs.append(pair)
+            backs += [back[:rank, :width], back[rank:, width:]]
+        proj += lax.dot_general(
+            jnp.concatenate(pairs, axis=1),
+            jnp.concatenate(backs, axis=1),
+            (((1,), (1,)), ((), ())),
+            preferred_element_type=jnp.float32,
+        )
     proj_ref[...] += proj
 
 

time: 232 us -> 230 us (level)
  no operation moved by 1% of the time
where the time goes in v6:
time: 230 us; the launch traced here: 227 us
  starting transfers between devices  66 us (29%)
  blocking collectives  57.4 us (25%)
  waiting for transfers between devices  52.3 us (23%)
  Pallas kernels  31.1 us (14%)
  local copies, waits for them, and re-layouts  7.49 us (3%)
  matrix products  6.9 us (3%)
  other arithmetic  4.76 us (2%)
    all_to_all x3, blocking collectives, exchange(): return lax.all_to_all(tiles, axis, split_axis=0, concat_axis=0, tiled=True)  57.4 us
    all_to_all x6, waiting for transfers between devices, exchange(): return lax.all_to_all(tiles, axis, split_axis=0, concat_axis=0, tiled=True)  38 us
    all_to_all x6, starting transfers between devices, exchange(): return lax.all_to_all(tiles, axis, split_axis=0, concat_axis=0, tiled=True)  30.1 us
    ppermute x6, starting transfers between devices, swapped(): lax.ppermute(x, axis, [(i, i ^ flip) for i in range(lax.axis_size(axis))])  24 us
    pallas_call x2, Pallas kernels, forward_features(): pl.pallas_call(forward_kernel, grid=(count // GROUP,), in_specs=[pl.Block...  23.3 us
    ppermute x6, waiting for transfers between devices, swapped(): lax.ppermute(x, axis, [(i, i ^ flip) for i in range(lax.axis_size(axis))])  9.29 us
    pallas_call x1, Pallas kernels, backward_features(): pl.pallas_call(backward_kernel, grid=(firsts + 1,), in_specs=[pl.BlockSpe...  7.77 us
    ppermute x1, starting transfers between devices, per_device(): state = lax.ppermute(jnp.stack([new_weight, new_momentum]), DP, to_owner)  6.5 us
  transfers between devices with their start and end apart: 14, of which 10 were waited for; matrix products, arithmetic and copies ran while one was open for 3% of the time, Pallas kernels for 14%

profile of v6, /device:TPU:1, one launch (start us, length us, event | category | flops | bytes accessed | tf_op | source)
XLA Modules:
  0.0 227.1 jit_solution(11621226797713675638)
XLA Ops:
  0.6 1.3 broadcast_in_dim.21
  1.9 10.9 %all-to-all-start = ((bf16[8,16,128]{2,1,0:T(8,128)(2,1)}), bf16[8,16,128]{2,1,0:T(8,128)(2,1)S(1)}, u32[]{:S(2)}, u32[]{:S(2)}) async-start(bf16[8,16,128]{2,1,0:T(8,128)(2,1)} %broadcast_in_dim.21), calls=%async_computation | async-start | bytes 65536 | tf_op jit(solution)/shard_map/all_to_all | solution.py:20
  12.8 0.8 convert_element_type.32
  13.6 6.1 %all-to-all-done = bf16[8,16,128]{2,1,0:T(8,128)(2,1)S(1)} async-done(((bf16[8,16,128]{2,1,0:T(8,128)(2,1)}), bf16[8,16,128]{2,1,0:T(8,128)(2,1)S(1)}, u32[]{:S(2)}, u32[]{:S(2)}) %all-to-all-start) | async-done | bytes 32800 | tf_op jit(solution)/shard_map/all_to_all | solution.py:20
  19.7 0.1 broadcast_in_dim.22
  19.7 18.2 %all_to_all.45 = bf16[8,192,128]{2,1,0:T(8,128)(2,1)S(1)} all-to-all(bf16[8,192,128]{2,1,0:T(8,128)(2,1)S(1)} %broadcast_in_dim.22), channel_id=1, replica_groups=mesh['zl'=2,'y'=8,'x'=4,'c'=2,'mp'=4] {'y'}, dimensions={0} | all-to-all | bytes 786432 | tf_op jit(solution)/shard_map/all_to_all | solution.py:20
  38.0 1.2 broadcast_in_dim.24
  39.2 4.0 %all-to-all-start.2 = ((bf16[4,8,128,128]{3,2,1,0:T(8,128)(2,1)}), bf16[4,8,128,128]{3,2,1,0:T(8,128)(2,1)S(1)}, u32[]{:S(2)}, u32[]{:S(2)}) async-start(bf16[4,8,128,128]{3,2,1,0:T(8,128)(2,1)} %broadcast_in_dim.24), calls=%async_computation.2 | async-start | bytes 2097152 | tf_op jit(solution)/shard_map/all_to_all | solution.py:20
  43.2 0.1 copy.39
  43.3 2.2 collective-permute-start.1
  45.6 3.5 %collective-permute-done.1 = bf16[256,256]{1,0:T(8,128)(2,1)S(1)} collective-permute-done((bf16[256,256]{1,0:T(8,128)(2,1)S(1)}, bf16[256,256]{1,0:T(8,128)(2,1)S(1)}, u32[]{:S(2)}, u32[]{:S(2)}) %collective-permute-start.1) | collective-permute-done | bytes 131104 | tf_op jit(solution)/shard_map/ppermute | solution.py:28
  49.1 0.0 copy-start.3
  49.1 4.6 %all-to-all-done.2 = bf16[4,8,128,128]{3,2,1,0:T(8,128)(2,1)S(1)} async-done(((bf16[4,8,128,128]{3,2,1,0:T(8,128)(2,1)}), bf16[4,8,128,128]{3,2,1,0:T(8,128)(2,1)S(1)}, u32[]{:S(2)}, u32[]{:S(2)}) %all-to-all-start.2) | async-done | bytes 1048608 | tf_op jit(solution)/shard_map/all_to_all | solution.py:20
  53.8 1.1 broadcast_in_dim.23
  54.9 7.4 %collective-permute-start.2 = (bf16[4096,128]{1,0:T(8,128)(2,1)S(1)}, bf16[4096,128]{1,0:T(8,128)(2,1)}, u32[]{:S(2)}, u32[]{:S(2)}) collective-permute-start(bf16[4096,128]{1,0:T(8,128)(2,1)S(1)} %bitcast.98), channel_id=1, source_target_pairs={{0,4},{4,0},{1,5},{5,1},{2,6},{6,2},{3,7},{7,3},{8,12},{12,8},{9,1... | collective-permute-start | bytes 3145736 | tf_op jit(solution)/shard_map/ppermute | solution.py:28
  62.3 3.5 %all-to-all-start.4 = ((bf16[4,512,256]{2,1,0:T(8,128)(2,1)}), bf16[4,512,256]{2,1,0:T(8,128)(2,1)S(1)}, u32[]{:S(2)}, u32[]{:S(2)}) async-start(bf16[4,512,256]{2,1,0:T(8,128)(2,1)} %broadcast_in_dim.23), calls=%async_computation.4 | async-start | bytes 2097152 | tf_op jit(solution)/shard_map/all_to_all | solution.py:20
  65.8 0.8 fusion.17.ids_ref
  66.6 14.4 %all-to-all-done.4 = bf16[4,512,256]{2,1,0:T(8,128)(2,1)S(1)} async-done(((bf16[4,512,256]{2,1,0:T(8,128)(2,1)}), bf16[4,512,256]{2,1,0:T(8,128)(2,1)S(1)}, u32[]{:S(2)}, u32[]{:S(2)}) %all-to-all-start.4) | async-done | bytes 1048608 | tf_op jit(solution)/shard_map/all_to_all | solution.py:20
  81.0 2.8 %collective-permute-start.3 = (bf16[2048,256]{1,0:T(8,128)(2,1)S(1)}, bf16[2048,256]{1,0:T(8,128)(2,1)S(1)}, u32[]{:S(2)}, u32[]{:S(2)}) collective-permute-start(bf16[2048,256]{1,0:T(8,128)(2,1)S(1)} %bitcast.92), channel_id=1, source_target_pairs={{0,4},{4,0},{1,5},{5,1},{2,6},{6,2},{3,7},{7,3},{8,12},{12,8},{9,1... | collective-permute-start | bytes 3145736 | tf_op jit(solution)/shard_map/ppermute | solution.py:28
  83.7 0.0 collective-permute-done.2.far_ref
  83.8 16.9 %fm_forward.2 = (bf16[128,128,128]{2,1,0:T(8,128)(2,1)}, bf16[16,96,256]{2,1,0:T(8,128)(2,1)}, f32[128,128]{1,0:T(8,128)}, f32[32,128]{1,0:T(8,128)}) custom-call(s32[128,128]{1,0:T(8,128)} %fusion.17.ids_ref, bf16[4096,128]{1,0:T(8,128)(2,1)} %bitcast.99, bf16[4096,128]{1,0:T(8,128)(2,1)} %collective-permute-done.2.far_ref, bf16[32,128]{1,0:T(8,128)(2,1)} %bitcast.111, ...), custom_call_target="tpu_custom_call" | custom-call | flops 9600000000 | bytes 5242880 | tf_op jit(solution)/shard_map/fm_forward/pallas_call | solution.py:109
  100.7 6.4 %fm_forward.3 = (bf16[128,128,128]{2,1,0:T(8,128)(2,1)}, bf16[16,32,256]{2,1,0:T(8,128)(2,1)}, f32[128,128]{1,0:T(8,128)}, f32[32,128]{1,0:T(8,128)}) custom-call(s32[128,128]{1,0:T(8,128)} %fusion.17.ids_ref, bf16[4096,128]{1,0:T(8,128)(2,1)} %bitcast.100, ...), custom_call_target="tpu_custom_call", output_to_operand_aliasing={{0}: (5, {}), {2}: (6, {})} | custom-call | flops 3200000000 | bytes 3145728 | tf_op jit(solution)/shard_map/fm_forward/pallas_call | solution.py:109
  107.1 0.0 collective-permute-done.3
  107.1 0.3 fusion
  107.4 0.2 copy.40
  107.7 0.7 copy-done.1
  108.4 0.5 convolution_bitcast_fusion.4
  108.8 1.6 convolution_bitcast_fusion.3
  110.5 0.1 multiply_convert_fusion
  110.6 0.1 pad_maximum_fusion
  110.6 14.6 %all_to_all.46 = bf16[8,192,256]{2,1,0:T(8,128)(2,1)S(1)} all-to-all(bf16[8,192,256]{2,1,0:T(8,128)(2,1)S(1)} %pad_maximum_fusion), channel_id=1, replica_groups=mesh['zl'=2,'y'=8,'x'=4,'c'=2,'mp'=4] {'c','x'}, dimensions={0} | all-to-all | bytes 1572864 | tf_op jit(solution)/shard_map/all_to_all | solution.py:20
  125.2 4.4 %all-to-all-start.3 = ((bf16[8,192,256]{2,1,0:T(8,128)(2,1)}), bf16[8,192,256]{2,1,0:T(8,128)(2,1)}, u32[]{:S(2)}, u32[]{:S(2)}) async-start(bf16[8,192,256]{2,1,0:T(8,128)(2,1)} %bitcast.9), calls=%async_computation.3 | async-start | bytes 1572864 | tf_op jit(solution)/shard_map/all_to_all | solution.py:20
  129.7 2.1 fusion.25.grad_ref
  131.8 0.2 convolution_bitcast_fusion.1
  132.0 0.2 convolution_bitcast_fusion.2
  132.2 9.7 %all-to-all-done.3 = bf16[8,192,256]{2,1,0:T(8,128)(2,1)} async-done(((bf16[8,192,256]{2,1,0:T(8,128)(2,1)}), bf16[8,192,256]{2,1,0:T(8,128)(2,1)}, u32[]{:S(2)}, u32[]{:S(2)}) %all-to-all-start.3) | async-done | bytes 786464 | tf_op jit(solution)/shard_map/all_to_all | solution.py:20
  141.9 2.3 %fusion.2 = bf16[2,256,256]{2,1,0:T(8,128)(2,1)} fusion(bf16[8,2,96,256]{3,2,1,0:T(8,128)(2,1)} %bitcast.10, f32[1,256,256]{2,1,0:T(8,128)S(1)} %convolution_bitcast_fusion.1, f32[1,256,256]{2,1,0:T(8,128)S(1)} %convolution_bitcast_fusion.2, bf16[8,192,256]{2,1,0:T(8,128)(2,1)S(1)} %all_to_all.46), kind=kOutput, calls=%fused_computation.5 | convolution fusion | flops 201719808 | bytes 1966080 | tf_op jit(solution)/shard_map/shbk,sbn->hkn/dot_general | solution.py:295
  144.2 3.7 %all-to-all-start.6 = ((bf16[16,32,256]{2,1,0:T(8,128)(2,1)}), bf16[16,32,256]{2,1,0:T(8,128)(2,1)S(1)}, u32[]{:S(2)}, u32[]{:S(2)}) async-start(bf16[16,32,256]{2,1,0:T(8,128)(2,1)} %bitcast.26), calls=%async_computation.6 | async-start | bytes 524288 | tf_op jit(solution)/shard_map/all_to_all | solution.py:20
  147.9 0.0 copy-start.2
  147.9 0.0 copy-start.5
  148.0 0.0 copy-start.6
  148.0 0.0 copy-start.7
  148.0 7.8 %fm_backward.1 = f32[128,32]{1,0:T(8,128)} custom-call(f32[128,4096]{1,0:T(8,128)} %fusion.25.grad_ref, bf16[16,96,256]{2,1,0:T(8,128)(2,1)} %get-tuple-element.20.first_ref, bf16[16,32,256]{2,1,0:T(8,128)(2,1)} %get-tuple-element.24.last_ref, f32[128,128]{1,0:T(8,128)} %get-tuple-element.25.inv_ref, bf16[128,128,128]{2,1,0:T(8,128)(2,1)} %get-tuple-element.26.emb_ref), custom_call_target="tpu_custom_call" | custom-call | flops 5120000000 | bytes 7340032 | tf_op jit(solution)/shard_map/fm_backward/pallas_call | solution.py:194
  155.7 2.1 collective-permute-start.4
  157.8 4.0 %collective-permute-done.4 = f32[32,128]{0,1:T(8,128)S(1)} collective-permute-done((f32[32,128]{0,1:T(8,128)}, f32[32,128]{0,1:T(8,128)S(1)}, u32[]{:S(2)}, u32[]{:S(2)}) %collective-permute-start.4) | collective-permute-done | bytes 16416 | tf_op jit(solution)/shard_map/ppermute | solution.py:28
  161.9 0.9 bitcast_add_fusion.2
  162.7 2.7 %collective-permute-start.5 = (f32[32,128]{0,1:T(8,128)S(1)}, f32[32,128]{0,1:T(8,128)S(1)}, u32[]{:S(2)}, u32[]{:S(2)}) collective-permute-start(f32[32,128]{0,1:T(8,128)S(1)} %bitcast_add_fusion.2), channel_id=1, source_target_pairs={{0,3},{1,2},{2,1},{3,0},{4,7},{5,6},{6,5},{7,4},{8,11},{9,10},{10,... | collective-permute-start | bytes 49160 | tf_op jit(solution)/shard_map/ppermute | solution.py:28
  165.4 5.5 %collective-permute-start = (f32[2,32,256]{2,1,0:T(8,128)S(1)}, f32[2,32,256]{2,1,0:T(8,128)S(1)}, u32[]{:S(2)}, u32[]{:S(2)}) collective-permute-start(f32[2,32,256]{2,1,0:T(8,128)S(1)} %pad_maximum_fusion.4), channel_id=1, source_target_pairs={{0,0},{4,32},{8,64},{12,96},{16,128},{20,160},{24,192},{28,224},{3... | collective-permute-start | bytes 196616 | tf_op jit(solution)/shard_map/ppermute | solution.py:238
  171.0 0.1 copy.42
  171.1 0.0 all-to-all-done.6
  171.1 2.3 %collective-permute-done = f32[2,32,256]{2,1,0:T(8,128)S(1)} collective-permute-done((f32[2,32,256]{2,1,0:T(8,128)S(1)}, f32[2,32,256]{2,1,0:T(8,128)S(1)}, u32[]{:S(2)}, u32[]{:S(2)}) %collective-permute-start) | collective-permute-done | bytes 65568 | tf_op jit(solution)/shard_map/ppermute | solution.py:238
  173.5 24.6 %all_to_all.47 = bf16[16,64,256]{2,1,0:T(8,128)(2,1)S(1)} all-to-all(bf16[16,64,256]{2,1,0:T(8,128)(2,1)S(1)} %broadcast_in_dim.26), channel_id=1, replica_groups=mesh['zl'=2,'y'=8,'x'=4,'c'=2,'mp'=4] {'zl','y'}, dimensions={0} | all-to-all | bytes 1048576 | tf_op jit(solution)/shard_map/all_to_all | solution.py:20
  198.3 1.1 broadcast_in_dim.27
  199.4 3.5 %all-to-all-start.8 = ((bf16[4,576,256]{2,1,0:T(8,128)(2,1)}), bf16[4,576,256]{2,1,0:T(8,128)(2,1)S(1)}, u32[]{:S(2)}, u32[]{:S(2)}) async-start(bf16[4,576,256]{2,1,0:T(8,128)(2,1)} %broadcast_in_dim.27), calls=%async_computation.8 | async-start | bytes 2359296 | tf_op jit(solution)/shard_map/all_to_all | solution.py:20
  202.9 6.5 %collective-permute-start.6 = (f32[2,32,256]{2,1,0:T(8,128)S(1)}, f32[2,32,256]{2,1,0:T(8,128)S(1)}, u32[]{:S(2)}, u32[]{:S(2)}) collective-permute-start(f32[2,32,256]{2,1,0:T(8,128)S(1)} %pad_maximum_fusion.5), channel_id=1, source_target_pairs={{0,0},{32,4},{64,8},{96,12},{128,16},{160,20},{192,24},{224,28},{2... | collective-permute-start | bytes 196616 | tf_op jit(solution)/shard_map/ppermute | solution.py:325
  209.5 2.7 %collective-permute-done.6 = f32[2,32,256]{2,1,0:T(8,128)S(1)} collective-permute-done((f32[2,32,256]{2,1,0:T(8,128)S(1)}, f32[2,32,256]{2,1,0:T(8,128)S(1)}, u32[]{:S(2)}, u32[]{:S(2)}) %collective-permute-start.6) | collective-permute-done | bytes 65568 | tf_op jit(solution)/shard_map/ppermute | solution.py:325
  212.2 3.2 %all-to-all-done.8 = bf16[4,576,256]{2,1,0:T(8,128)(2,1)S(1)} async-done(((bf16[4,576,256]{2,1,0:T(8,128)(2,1)}), bf16[4,576,256]{2,1,0:T(8,128)(2,1)S(1)}, u32[]{:S(2)}, u32[]{:S(2)}) %all-to-all-start.8) | async-done | bytes 1179680 | tf_op jit(solution)/shard_map/all_to_all | solution.py:20
  215.3 6.9 %collective-permute-start.7 = (bf16[4,576,256]{2,1,0:T(8,128)(2,1)S(1)}, bf16[4,576,256]{2,1,0:T(8,128)(2,1)S(1)}, u32[]{:S(2)}, u32[]{:S(2)}) collective-permute-start(bf16[4,576,256]{2,1,0:T(8,128)(2,1)S(1)} %all-to-all-done.8), channel_id=1, source_target_pairs={{0,4},{4,0},{1,5},{5,1},{2,6},{6,2},{3,7},{7,3},{8,12},{12,8},{9,1... | collective-permute-start | bytes 3538952 | tf_op jit(solution)/shard_map/ppermute | solution.py:28
  222.3 0.6 slice_bitcast_fusion.4
  222.9 0.1 slice_bitcast_fusion.1
  223.0 1.7 collective-permute-done.7
  224.8 0.6 slice_bitcast_fusion.6
  225.4 0.1 slice_bitcast_fusion
  225.4 1.6 maximum_select_fusion.1
  (37 shorter events, 0.5 us)
Async XLA Ops:
  1.9 17.7 %all-to-all-start = ((bf16[8,16,128]{2,1,0:T(8,128)(2,1)}), bf16[8,16,128]{2,1,0:T(8,128)(2,1)S(1)}, u32[]{:S(2)}, u32[]{:S(2)}) async-start(bf16[8,16,128]{2,1,0:T(8,128)(2,1)} %broadcast_in_dim.21), calls=%async_computation | async-start | bytes 65536 | tf_op jit(solution)/shard_map/all_to_all | solution.py:20
  39.2 14.6 %all-to-all-start.2 = ((bf16[4,8,128,128]{3,2,1,0:T(8,128)(2,1)}), bf16[4,8,128,128]{3,2,1,0:T(8,128)(2,1)S(1)}, u32[]{:S(2)}, u32[]{:S(2)}) async-start(bf16[4,8,128,128]{3,2,1,0:T(8,128)(2,1)} %broadcast_in_dim.24), calls=%async_computation.2 | async-start | bytes 2097152 | tf_op jit(solution)/shard_map/all_to_all | solution.py:20
  43.3 5.7 %collective-permute-start.1 = (bf16[256,256]{1,0:T(8,128)(2,1)S(1)}, bf16[256,256]{1,0:T(8,128)(2,1)S(1)}, u32[]{:S(2)}, u32[]{:S(2)}) collective-permute-start(bf16[256,256]{1,0:T(8,128)(2,1)S(1)} %bitcast.107), channel_id=1, source_target_pairs={{0,256},{256,0},{1,257},{257,1},{2,258},{258,2},{3,259},{259,3},{4... | collective-permute-start | bytes 393224 | tf_op jit(solution)/shard_map/ppermute | solution.py:28
  49.1 16.7 %copy-start.3 = (s32[128,128]{1,0:T(8,128)S(1)}, s32[128,128]{1,0:T(8,128)}, u32[]{:S(2)}) copy-start(s32[128,128]{1,0:T(8,128)} %param.7) | copy-start | bytes 196612
  53.8 30.0 %copy-start = (bf16[4,8,128,128]{3,2,1,0:T(8,128)(2,1)}, bf16[4,8,128,128]{3,2,1,0:T(8,128)(2,1)S(1)}, u32[]{:S(2)}) copy-start(bf16[4,8,128,128]{3,2,1,0:T(8,128)(2,1)S(1)} %all-to-all-done.2) | copy-start | bytes 3145732
  54.9 28.8 %collective-permute-start.2 = (bf16[4096,128]{1,0:T(8,128)(2,1)S(1)}, bf16[4096,128]{1,0:T(8,128)(2,1)}, u32[]{:S(2)}, u32[]{:S(2)}) collective-permute-start(bf16[4096,128]{1,0:T(8,128)(2,1)S(1)} %bitcast.98), channel_id=1, source_target_pairs={{0,4},{4,0},{1,5},{5,1},{2,6},{6,2},{3,7},{7,3},{8,12},{12,8},{9,1... | collective-permute-start | bytes 3145736 | tf_op jit(solution)/shard_map/ppermute | solution.py:28
  62.3 18.7 %all-to-all-start.4 = ((bf16[4,512,256]{2,1,0:T(8,128)(2,1)}), bf16[4,512,256]{2,1,0:T(8,128)(2,1)S(1)}, u32[]{:S(2)}, u32[]{:S(2)}) async-start(bf16[4,512,256]{2,1,0:T(8,128)(2,1)} %broadcast_in_dim.23), calls=%async_computation.4 | async-start | bytes 2097152 | tf_op jit(solution)/shard_map/all_to_all | solution.py:20
  81.0 26.1 %collective-permute-start.3 = (bf16[2048,256]{1,0:T(8,128)(2,1)S(1)}, bf16[2048,256]{1,0:T(8,128)(2,1)S(1)}, u32[]{:S(2)}, u32[]{:S(2)}) collective-permute-start(bf16[2048,256]{1,0:T(8,128)(2,1)S(1)} %bitcast.92), channel_id=1, source_target_pairs={{0,4},{4,0},{1,5},{5,1},{2,6},{6,2},{3,7},{7,3},{8,12},{12,8},{9,1... | collective-permute-start | bytes 3145736 | tf_op jit(solution)/shard_map/ppermute | solution.py:28
  107.4 1.0 copy-start.1
  108.4 2.1 copy-start.4
  125.2 16.7 %all-to-all-start.3 = ((bf16[8,192,256]{2,1,0:T(8,128)(2,1)}), bf16[8,192,256]{2,1,0:T(8,128)(2,1)}, u32[]{:S(2)}, u32[]{:S(2)}) async-start(bf16[8,192,256]{2,1,0:T(8,128)(2,1)} %bitcast.9), calls=%async_computation.3 | async-start | bytes 1572864 | tf_op jit(solution)/shard_map/all_to_all | solution.py:20
  144.2 26.9 %all-to-all-start.6 = ((bf16[16,32,256]{2,1,0:T(8,128)(2,1)}), bf16[16,32,256]{2,1,0:T(8,128)(2,1)S(1)}, u32[]{:S(2)}, u32[]{:S(2)}) async-start(bf16[16,32,256]{2,1,0:T(8,128)(2,1)} %bitcast.26), calls=%async_computation.6 | async-start | bytes 524288 | tf_op jit(solution)/shard_map/all_to_all | solution.py:20
  147.9 17.5 %copy-start.2 = (f32[32,256]{1,0:T(8,128)S(1)}, f32[32,256]{1,0:T(8,128)}, u32[]{:S(2)}) copy-start(f32[32,256]{1,0:T(8,128)} %param.10) | copy-start | bytes 98308
  147.9 17.5 %copy-start.5 = (f32[32,256]{1,0:T(8,128)S(1)}, f32[32,256]{1,0:T(8,128)}, u32[]{:S(2)}) copy-start(f32[32,256]{1,0:T(8,128)} %param.11) | copy-start | bytes 98308
  148.0 23.0 %copy-start.6 = (f32[32,128]{1,0:T(8,128)S(1)}, f32[32,128]{1,0:T(8,128)}, u32[]{:S(2)}) copy-start(f32[32,128]{1,0:T(8,128)} %get-tuple-element.27) | copy-start | bytes 49156
  148.0 23.0 %copy-start.7 = (f32[32,128]{1,0:T(8,128)S(1)}, f32[32,128]{1,0:T(8,128)}, u32[]{:S(2)}) copy-start(f32[32,128]{1,0:T(8,128)} %get-tuple-element.28) | copy-start | bytes 49156
  155.7 6.1 %collective-permute-start.4 = (f32[32,128]{0,1:T(8,128)}, f32[32,128]{0,1:T(8,128)S(1)}, u32[]{:S(2)}, u32[]{:S(2)}) collective-permute-start(f32[32,128]{0,1:T(8,128)} %bitcast.109), channel_id=1, source_target_pairs={{0,1},{1,0},{2,3},{3,2},{4,5},{5,4},{6,7},{7,6},{8,9},{9,8},{10,11... | collective-permute-start | bytes 49160 | tf_op jit(solution)/shard_map/ppermute | solution.py:28
  162.7 8.3 %collective-permute-start.5 = (f32[32,128]{0,1:T(8,128)S(1)}, f32[32,128]{0,1:T(8,128)S(1)}, u32[]{:S(2)}, u32[]{:S(2)}) collective-permute-start(f32[32,128]{0,1:T(8,128)S(1)} %bitcast_add_fusion.2), channel_id=1, source_target_pairs={{0,3},{1,2},{2,1},{3,0},{4,7},{5,6},{6,5},{7,4},{8,11},{9,10},{10,... | collective-permute-start | bytes 49160 | tf_op jit(solution)/shard_map/ppermute | solution.py:28
  165.4 8.0 %collective-permute-start = (f32[2,32,256]{2,1,0:T(8,128)S(1)}, f32[2,32,256]{2,1,0:T(8,128)S(1)}, u32[]{:S(2)}, u32[]{:S(2)}) collective-permute-start(f32[2,32,256]{2,1,0:T(8,128)S(1)} %pad_maximum_fusion.4), channel_id=1, source_target_pairs={{0,0},{4,32},{8,64},{12,96},{16,128},{20,160},{24,192},{28,224},{3... | collective-permute-start | bytes 196616 | tf_op jit(solution)/shard_map/ppermute | solution.py:238
  199.4 16.0 %all-to-all-start.8 = ((bf16[4,576,256]{2,1,0:T(8,128)(2,1)}), bf16[4,576,256]{2,1,0:T(8,128)(2,1)S(1)}, u32[]{:S(2)}, u32[]{:S(2)}) async-start(bf16[4,576,256]{2,1,0:T(8,128)(2,1)} %broadcast_in_dim.27), calls=%async_computation.8 | async-start | bytes 2359296 | tf_op jit(solution)/shard_map/all_to_all | solution.py:20
  202.9 9.2 %collective-permute-start.6 = (f32[2,32,256]{2,1,0:T(8,128)S(1)}, f32[2,32,256]{2,1,0:T(8,128)S(1)}, u32[]{:S(2)}, u32[]{:S(2)}) collective-permute-start(f32[2,32,256]{2,1,0:T(8,128)S(1)} %pad_maximum_fusion.5), channel_id=1, source_target_pairs={{0,0},{32,4},{64,8},{96,12},{128,16},{160,20},{192,24},{224,28},{2... | collective-permute-start | bytes 196616 | tf_op jit(solution)/shard_map/ppermute | solution.py:325
  215.3 9.3 %collective-permute-start.7 = (bf16[4,576,256]{2,1,0:T(8,128)(2,1)S(1)}, bf16[4,576,256]{2,1,0:T(8,128)(2,1)S(1)}, u32[]{:S(2)}, u32[]{:S(2)}) collective-permute-start(bf16[4,576,256]{2,1,0:T(8,128)(2,1)S(1)} %all-to-all-done.8), channel_id=1, source_target_pairs={{0,4},{4,0},{1,5},{5,1},{2,6},{6,2},{3,7},{7,3},{8,12},{12,8},{9,1... | collective-permute-start | bytes 3538952 | tf_op jit(solution)/shard_map/ppermute | solution.py:28

commit v7 on v6

--- a/solution.py
+++ b/solution.py
@@ -234,14 +234,13 @@
     to_owner = [(worker, owner) for owner, worker in to_worker]
 
     width = emb_table.shape[1]
-    table = from_everyone(emb_table, ("mp", "zl")).reshape(-1, width)
+    weights = mlp_weight.astype(jnp.bfloat16)
+    table = from_everyone(jnp.concatenate([emb_table, weights[:, :width], weights[:, width:]], axis=0), "y")
+    weights = table[:, own:].reshape(y, hidden // width, -1, width)
+    weights = jnp.swapaxes(weights, 1, 2).reshape(-1, hidden)
+    table = from_everyone(table[:, :own].reshape(-1, width), ("mp", "zl")).reshape(-1, width)
     state = lax.ppermute(jnp.stack([mlp_weight, momentum]), DP, to_worker)
     weight_rows, momentum_rows = state[0], state[1]
-    weights = mlp_weight.astype(jnp.bfloat16)
-    near_rows = table.shape[0]
-    table = from_everyone(jnp.concatenate([table, weights[:, :width], weights[:, width:]], axis=0), "y")
-    weights = table[:, near_rows:].reshape(y, hidden // width, -1, width)
-    weights = jnp.swapaxes(weights, 1, 2).reshape(-1, hidden)
     weights = doubled(weights, "zl", 1)
     weights = jnp.broadcast_to(weights, (x, *weights.shape))
     owner, row = lax.div(feature_ids, own), lax.rem(feature_ids, own)
@@ -249,8 +248,8 @@
     owner, at_c = lax.div(owner, c), lax.rem(owner, c)
     owner, at_x = lax.div(owner, x), lax.rem(owner, x)
     at_zl, at_y = lax.div(owner, y), lax.rem(owner, y)
-    ids = (((((at_c ^ lax.axis_index("c")) * x + at_x) * y + at_y) * mp + at_mp) * zl + at_zl) * own + row
-    table = from_everyone(table[:, :near_rows], "x").reshape(-1, width)
+    ids = (((((at_c ^ lax.axis_index("c")) * x + at_x) * mp + at_mp) * zl + at_zl) * y + at_y) * own + row
+    table = from_everyone(table, "x").reshape(-1, width)
     weights, table = tied(weights, table)
     table_far = swapped(table, "c", 1)
     weights = exchange(weights, "x").reshape(-1, hidden)

time: 230 us -> 229 us (level)
  blocking collectives: 57.4 us -> 74.2 us
  starting transfers between devices: 66 us -> 55.6 us
  waiting for transfers between devices: 52.3 us -> 46.2 us
    all_to_all x3 -> x4, blocking collectives: 57.4 us -> 74.2 us  [exchange(): return lax.all_to_all(tiles, axis, split_axis=0, concat_axis=0, tiled=True)]
    all_to_all x6 -> x5, starting transfers between devices: 30.1 us -> 19.2 us  [exchange(): return lax.all_to_all(tiles, axis, split_axis=0, concat_axis=0, tiled=True)]
    all_to_all x6 -> x5, waiting for transfers between devices: 38 us -> 32.1 us  [exchange(): return lax.all_to_all(tiles, axis, split_axis=0, concat_axis=0, tiled=True)]
  transfers between devices with their start and end apart: 14 -> 13, of which waited for: 10 -> 9; matrix products, arithmetic and copies ran while one was open for 3% -> 2% of each run, Pallas kernels for 14% -> 14%
where the time goes in v7:
time: 229 us; the launch traced here: 227 us
  blocking collectives  74.2 us (32%)
  starting transfers between devices  55.6 us (24%)
  waiting for transfers between devices  46.2 us (20%)
  Pallas kernels  31.1 us (14%)
  matrix products  6.89 us (3%)
  local copies, waits for them, and re-layouts  6.07 us (3%)
  other arithmetic  5.44 us (2%)
    all_to_all x4, blocking collectives, exchange(): return lax.all_to_all(tiles, axis, split_axis=0, concat_axis=0, tiled=True)  74.2 us
    all_to_all x5, waiting for transfers between devices, exchange(): return lax.all_to_all(tiles, axis, split_axis=0, concat_axis=0, tiled=True)  32.1 us
    ppermute x6, starting transfers between devices, swapped(): lax.ppermute(x, axis, [(i, i ^ flip) for i in range(lax.axis_size(axis))])  24.4 us
    pallas_call x2, Pallas kernels, forward_features(): pl.pallas_call(forward_kernel, grid=(count // GROUP,), in_specs=[pl.Block...  23.3 us
    all_to_all x5, starting transfers between devices, exchange(): return lax.all_to_all(tiles, axis, split_axis=0, concat_axis=0, tiled=True)  19.2 us
    ppermute x6, waiting for transfers between devices, swapped(): lax.ppermute(x, axis, [(i, i ^ flip) for i in range(lax.axis_size(axis))])  9.14 us
    pallas_call x1, Pallas kernels, backward_features(): pl.pallas_call(backward_kernel, grid=(firsts + 1,), in_specs=[pl.BlockSpe...  7.76 us
    ppermute x1, starting transfers between devices, per_device(): state = lax.ppermute(jnp.stack([new_weight, new_momentum]), DP, to_owner)  6.48 us
  transfers between devices with their start and end apart: 13, of which 9 were waited for; matrix products, arithmetic and copies ran while one was open for 2% of the time, Pallas kernels for 14%

profile of v7, /device:TPU:1, one launch (start us, length us, event | category | flops | bytes accessed | tf_op | source)
XLA Modules:
  0.0 226.6 jit_solution(64178254888625628)
XLA Ops:
  0.6 0.8 convert_element_type.32
  1.4 0.7 pad_maximum_fusion.8
  2.1 15.8 %all_to_all.45 = bf16[8,80,128]{2,1,0:T(8,128)(2,1)S(1)} all-to-all(bf16[8,80,128]{2,1,0:T(8,128)(2,1)S(1)} %broadcast_in_dim.21), channel_id=1, replica_groups=mesh['zl'=2,'y'=8,'x'=4,'c'=2,'mp'=4] {'y'}, dimensions={0} | all-to-all | bytes 327680 | tf_op jit(solution)/shard_map/all_to_all | solution.py:20
  17.9 19.1 %all_to_all.46 = bf16[8,128,128]{2,1,0:T(8,128)(2,1)S(1)} all-to-all(bf16[8,128,128]{2,1,0:T(8,128)(2,1)S(1)} %broadcast_in_dim.23), channel_id=1, replica_groups=mesh['zl'=2,'y'=8,'x'=4,'c'=2,'mp'=4] {'mp','zl'}, dimensions={0} | all-to-all | bytes 524288 | tf_op jit(solution)/shard_map/all_to_all | solution.py:20
  37.0 1.1 broadcast_in_dim.24
  38.1 4.0 %all-to-all-start.2 = ((bf16[4,1024,128]{2,1,0:T(8,128)(2,1)}), bf16[4,1024,128]{2,1,0:T(8,128)(2,1)S(1)}, u32[]{:S(2)}, u32[]{:S(2)}) async-start(bf16[4,1024,128]{2,1,0:T(8,128)(2,1)} %broadcast_in_dim.24), calls=%async_computation.2 | async-start | bytes 2097152 | tf_op jit(solution)/shard_map/all_to_all | solution.py:20
  42.2 0.1 copy.39
  42.3 2.1 collective-permute-start.1
  44.5 3.6 %collective-permute-done.1 = bf16[256,256]{1,0:T(8,128)(2,1)S(1)} collective-permute-done((bf16[256,256]{1,0:T(8,128)(2,1)S(1)}, bf16[256,256]{1,0:T(8,128)(2,1)S(1)}, u32[]{:S(2)}, u32[]{:S(2)}) %collective-permute-start.1) | collective-permute-done | bytes 131104 | tf_op jit(solution)/shard_map/ppermute | solution.py:28
  48.1 0.0 copy-start.3
  48.1 4.8 %all-to-all-done.2 = bf16[4,1024,128]{2,1,0:T(8,128)(2,1)S(1)} async-done(((bf16[4,1024,128]{2,1,0:T(8,128)(2,1)}), bf16[4,1024,128]{2,1,0:T(8,128)(2,1)S(1)}, u32[]{:S(2)}, u32[]{:S(2)}) %all-to-all-start.2) | async-done | bytes 1048608 | tf_op jit(solution)/shard_map/all_to_all | solution.py:20
  52.9 1.1 broadcast_in_dim.22
  54.0 7.2 %collective-permute-start.2 = (bf16[4096,128]{1,0:T(8,128)(2,1)S(1)}, bf16[4096,128]{1,0:T(8,128)(2,1)}, u32[]{:S(2)}, u32[]{:S(2)}) collective-permute-start(bf16[4096,128]{1,0:T(8,128)(2,1)S(1)} %bitcast.100), channel_id=1, source_target_pairs={{0,4},{4,0},{1,5},{5,1},{2,6},{6,2},{3,7},{7,3},{8,12},{12,8},{9,1... | collective-permute-start | bytes 3145736 | tf_op jit(solution)/shard_map/ppermute | solution.py:28
  61.2 3.5 %all-to-all-start.4 = ((bf16[4,512,256]{2,1,0:T(8,128)(2,1)}), bf16[4,512,256]{2,1,0:T(8,128)(2,1)S(1)}, u32[]{:S(2)}, u32[]{:S(2)}) async-start(bf16[4,512,256]{2,1,0:T(8,128)(2,1)} %broadcast_in_dim.22), calls=%async_computation.4 | async-start | bytes 2097152 | tf_op jit(solution)/shard_map/all_to_all | solution.py:20
  64.8 0.7 fusion.17.ids_ref
  65.5 14.4 %all-to-all-done.4 = bf16[4,512,256]{2,1,0:T(8,128)(2,1)S(1)} async-done(((bf16[4,512,256]{2,1,0:T(8,128)(2,1)}), bf16[4,512,256]{2,1,0:T(8,128)(2,1)S(1)}, u32[]{:S(2)}, u32[]{:S(2)}) %all-to-all-start.4) | async-done | bytes 1048608 | tf_op jit(solution)/shard_map/all_to_all | solution.py:20
  79.9 2.8 %collective-permute-start.3 = (bf16[2048,256]{1,0:T(8,128)(2,1)S(1)}, bf16[2048,256]{1,0:T(8,128)(2,1)S(1)}, u32[]{:S(2)}, u32[]{:S(2)}) collective-permute-start(bf16[2048,256]{1,0:T(8,128)(2,1)S(1)} %bitcast.93), channel_id=1, source_target_pairs={{0,4},{4,0},{1,5},{5,1},{2,6},{6,2},{3,7},{7,3},{8,12},{12,8},{9,1... | collective-permute-start | bytes 3145736 | tf_op jit(solution)/shard_map/ppermute | solution.py:28
  82.7 0.0 collective-permute-done.2.far_ref
  82.7 16.9 %fm_forward.2 = (bf16[128,128,128]{2,1,0:T(8,128)(2,1)}, bf16[16,96,256]{2,1,0:T(8,128)(2,1)}, f32[128,128]{1,0:T(8,128)}, f32[32,128]{1,0:T(8,128)}) custom-call(s32[128,128]{1,0:T(8,128)} %fusion.17.ids_ref, bf16[4096,128]{1,0:T(8,128)(2,1)} %bitcast.101, bf16[4096,128]{1,0:T(8,128)(2,1)} %collective-permute-done.2.far_ref, bf16[32,128]{1,0:T(8,128)(2,1)} %bitcast.113, ...), custom_call_target="tpu_custom_call" | custom-call | flops 9600000000 | bytes 5242880 | tf_op jit(solution)/shard_map/fm_forward/pallas_call | solution.py:109
  99.7 6.4 %fm_forward.3 = (bf16[128,128,128]{2,1,0:T(8,128)(2,1)}, bf16[16,32,256]{2,1,0:T(8,128)(2,1)}, f32[128,128]{1,0:T(8,128)}, f32[32,128]{1,0:T(8,128)}) custom-call(s32[128,128]{1,0:T(8,128)} %fusion.17.ids_ref, bf16[4096,128]{1,0:T(8,128)(2,1)} %bitcast.102, ...), custom_call_target="tpu_custom_call", output_to_operand_aliasing={{0}: (5, {}), {2}: (6, {})} | custom-call | flops 3200000000 | bytes 3145728 | tf_op jit(solution)/shard_map/fm_forward/pallas_call | solution.py:109
  106.0 0.0 collective-permute-done.3
  106.0 0.3 fusion
  106.4 0.2 copy.40
  106.6 0.7 copy-done.1
  107.3 0.5 convolution_bitcast_fusion.4
  107.8 1.6 convolution_bitcast_fusion.3
  109.4 0.0 copy-done.4
  109.4 0.1 multiply_convert_fusion
  109.5 0.1 pad_maximum_fusion
  109.6 14.6 %all_to_all.47 = bf16[8,192,256]{2,1,0:T(8,128)(2,1)S(1)} all-to-all(bf16[8,192,256]{2,1,0:T(8,128)(2,1)S(1)} %pad_maximum_fusion), channel_id=1, replica_groups=mesh['zl'=2,'y'=8,'x'=4,'c'=2,'mp'=4] {'c','x'}, dimensions={0} | all-to-all | bytes 1572864 | tf_op jit(solution)/shard_map/all_to_all | solution.py:20
  124.1 4.4 %all-to-all-start.3 = ((bf16[8,192,256]{2,1,0:T(8,128)(2,1)}), bf16[8,192,256]{2,1,0:T(8,128)(2,1)}, u32[]{:S(2)}, u32[]{:S(2)}) async-start(bf16[8,192,256]{2,1,0:T(8,128)(2,1)} %bitcast.10), calls=%async_computation.3 | async-start | bytes 1572864 | tf_op jit(solution)/shard_map/all_to_all | solution.py:20
  128.6 2.1 fusion.25.grad_ref
  130.7 0.2 convolution_bitcast_fusion.1
  130.9 0.2 convolution_bitcast_fusion.2
  131.2 9.7 %all-to-all-done.3 = bf16[8,192,256]{2,1,0:T(8,128)(2,1)} async-done(((bf16[8,192,256]{2,1,0:T(8,128)(2,1)}), bf16[8,192,256]{2,1,0:T(8,128)(2,1)}, u32[]{:S(2)}, u32[]{:S(2)}) %all-to-all-start.3) | async-done | bytes 786464 | tf_op jit(solution)/shard_map/all_to_all | solution.py:20
  140.9 2.3 fusion.2
  143.1 3.7 %all-to-all-start.6 = ((bf16[16,32,256]{2,1,0:T(8,128)(2,1)}), bf16[16,32,256]{2,1,0:T(8,128)(2,1)S(1)}, u32[]{:S(2)}, u32[]{:S(2)}) async-start(bf16[16,32,256]{2,1,0:T(8,128)(2,1)} %bitcast.27), calls=%async_computation.6 | async-start | bytes 524288 | tf_op jit(solution)/shard_map/all_to_all | solution.py:20
  146.8 0.0 copy-start.2
  146.9 0.0 copy-start.5
  146.9 0.0 copy-start.6
  146.9 0.0 copy-start.7
  146.9 7.8 %fm_backward.1 = f32[128,32]{1,0:T(8,128)} custom-call(f32[128,4096]{1,0:T(8,128)} %fusion.25.grad_ref, bf16[16,96,256]{2,1,0:T(8,128)(2,1)} %get-tuple-element.20.first_ref, bf16[16,32,256]{2,1,0:T(8,128)(2,1)} %get-tuple-element.24.last_ref, f32[128,128]{1,0:T(8,128)} %get-tuple-element.25.inv_ref, bf16[128,128,128]{2,1,0:T(8,128)(2,1)} %get-tuple-element.26.emb_ref), custom_call_target="tpu_custom_call" | custom-call | flops 5120000000 | bytes 7340032 | tf_op jit(solution)/shard_map/fm_backward/pallas_call | solution.py:194
  154.7 2.3 collective-permute-start.4
  156.9 3.8 %collective-permute-done.4 = f32[32,128]{0,1:T(8,128)S(1)} collective-permute-done((f32[32,128]{0,1:T(8,128)}, f32[32,128]{0,1:T(8,128)S(1)}, u32[]{:S(2)}, u32[]{:S(2)}) %collective-permute-start.4) | collective-permute-done | bytes 16416 | tf_op jit(solution)/shard_map/ppermute | solution.py:28
  160.8 0.9 bitcast_add_fusion.2
  161.6 3.2 %collective-permute-start.5 = (f32[32,128]{0,1:T(8,128)S(1)}, f32[32,128]{0,1:T(8,128)S(1)}, u32[]{:S(2)}, u32[]{:S(2)}) collective-permute-start(f32[32,128]{0,1:T(8,128)S(1)} %bitcast_add_fusion.2), channel_id=1, source_target_pairs={{0,3},{1,2},{2,1},{3,0},{4,7},{5,6},{6,5},{7,4},{8,11},{9,10},{10,... | collective-permute-start | bytes 49160 | tf_op jit(solution)/shard_map/ppermute | solution.py:28
  164.9 5.5 %collective-permute-start = (f32[2,32,256]{2,1,0:T(8,128)S(1)}, f32[2,32,256]{2,1,0:T(8,128)S(1)}, u32[]{:S(2)}, u32[]{:S(2)}) collective-permute-start(f32[2,32,256]{2,1,0:T(8,128)S(1)} %pad_maximum_fusion.4), channel_id=1, source_target_pairs={{0,0},{4,32},{8,64},{12,96},{16,128},{20,160},{24,192},{28,224},{3... | collective-permute-start | bytes 196616 | tf_op jit(solution)/shard_map/ppermute | solution.py:242
  170.4 0.0 collective-permute-done.5
  170.4 0.1 copy.42
  170.5 0.0 all-to-all-done.6
  170.6 2.2 collective-permute-done
  172.9 24.8 %all_to_all.48 = bf16[16,64,256]{2,1,0:T(8,128)(2,1)S(1)} all-to-all(bf16[16,64,256]{2,1,0:T(8,128)(2,1)S(1)} %broadcast_in_dim.26), channel_id=1, replica_groups=mesh['zl'=2,'y'=8,'x'=4,'c'=2,'mp'=4] {'zl','y'}, dimensions={0} | all-to-all | bytes 1048576 | tf_op jit(solution)/shard_map/all_to_all | solution.py:20
  197.8 1.1 broadcast_in_dim.27
  198.9 3.5 %all-to-all-start.8 = ((bf16[4,576,256]{2,1,0:T(8,128)(2,1)}), bf16[4,576,256]{2,1,0:T(8,128)(2,1)S(1)}, u32[]{:S(2)}, u32[]{:S(2)}) async-start(bf16[4,576,256]{2,1,0:T(8,128)(2,1)} %broadcast_in_dim.27), calls=%async_computation.8 | async-start | bytes 2359296 | tf_op jit(solution)/shard_map/all_to_all | solution.py:20
  202.4 6.5 %collective-permute-start.6 = (f32[2,32,256]{2,1,0:T(8,128)S(1)}, f32[2,32,256]{2,1,0:T(8,128)S(1)}, u32[]{:S(2)}, u32[]{:S(2)}) collective-permute-start(f32[2,32,256]{2,1,0:T(8,128)S(1)} %pad_maximum_fusion.5), channel_id=1, source_target_pairs={{0,0},{32,4},{64,8},{96,12},{128,16},{160,20},{192,24},{224,28},{2... | collective-permute-start | bytes 196616 | tf_op jit(solution)/shard_map/ppermute | solution.py:324
  208.9 2.7 %collective-permute-done.6 = f32[2,32,256]{2,1,0:T(8,128)S(1)} collective-permute-done((f32[2,32,256]{2,1,0:T(8,128)S(1)}, f32[2,32,256]{2,1,0:T(8,128)S(1)}, u32[]{:S(2)}, u32[]{:S(2)}) %collective-permute-start.6) | collective-permute-done | bytes 65568 | tf_op jit(solution)/shard_map/ppermute | solution.py:324
  211.6 3.3 %all-to-all-done.8 = bf16[4,576,256]{2,1,0:T(8,128)(2,1)S(1)} async-done(((bf16[4,576,256]{2,1,0:T(8,128)(2,1)}), bf16[4,576,256]{2,1,0:T(8,128)(2,1)S(1)}, u32[]{:S(2)}, u32[]{:S(2)}) %all-to-all-start.8) | async-done | bytes 1179680 | tf_op jit(solution)/shard_map/all_to_all | solution.py:20
  214.9 6.8 %collective-permute-start.7 = (bf16[4,576,256]{2,1,0:T(8,128)(2,1)S(1)}, bf16[4,576,256]{2,1,0:T(8,128)(2,1)S(1)}, u32[]{:S(2)}, u32[]{:S(2)}) collective-permute-start(bf16[4,576,256]{2,1,0:T(8,128)(2,1)S(1)} %all-to-all-done.8), channel_id=1, source_target_pairs={{0,4},{4,0},{1,5},{5,1},{2,6},{6,2},{3,7},{7,3},{8,12},{12,8},{9,1... | collective-permute-start | bytes 3538952 | tf_op jit(solution)/shard_map/ppermute | solution.py:28
  221.7 0.6 slice_bitcast_fusion.4
  222.4 0.1 slice_bitcast_fusion.1
  222.4 1.7 collective-permute-done.7
  224.3 0.6 slice_bitcast_fusion.6
  224.9 0.1 slice_bitcast_fusion
  224.9 1.6 maximum_select_fusion.1
  (36 shorter events, 0.5 us)
Async XLA Ops:
  38.1 14.7 %all-to-all-start.2 = ((bf16[4,1024,128]{2,1,0:T(8,128)(2,1)}), bf16[4,1024,128]{2,1,0:T(8,128)(2,1)S(1)}, u32[]{:S(2)}, u32[]{:S(2)}) async-start(bf16[4,1024,128]{2,1,0:T(8,128)(2,1)} %broadcast_in_dim.24), calls=%async_computation.2 | async-start | bytes 2097152 | tf_op jit(solution)/shard_map/all_to_all | solution.py:20
  42.3 5.7 %collective-permute-start.1 = (bf16[256,256]{1,0:T(8,128)(2,1)S(1)}, bf16[256,256]{1,0:T(8,128)(2,1)S(1)}, u32[]{:S(2)}, u32[]{:S(2)}) collective-permute-start(bf16[256,256]{1,0:T(8,128)(2,1)S(1)} %bitcast.109), channel_id=1, source_target_pairs={{0,256},{256,0},{1,257},{257,1},{2,258},{258,2},{3,259},{259,3},{4... | collective-permute-start | bytes 393224 | tf_op jit(solution)/shard_map/ppermute | solution.py:28
  48.1 16.7 %copy-start.3 = (s32[128,128]{1,0:T(8,128)S(1)}, s32[128,128]{1,0:T(8,128)}, u32[]{:S(2)}) copy-start(s32[128,128]{1,0:T(8,128)} %param.7) | copy-start | bytes 196612
  52.9 29.8 %copy-start = (bf16[4,1024,128]{2,1,0:T(8,128)(2,1)}, bf16[4,1024,128]{2,1,0:T(8,128)(2,1)S(1)}, u32[]{:S(2)}) copy-start(bf16[4,1024,128]{2,1,0:T(8,128)(2,1)S(1)} %all-to-all-done.2) | copy-start | bytes 3145732
  54.0 28.7 %collective-permute-start.2 = (bf16[4096,128]{1,0:T(8,128)(2,1)S(1)}, bf16[4096,128]{1,0:T(8,128)(2,1)}, u32[]{:S(2)}, u32[]{:S(2)}) collective-permute-start(bf16[4096,128]{1,0:T(8,128)(2,1)S(1)} %bitcast.100), channel_id=1, source_target_pairs={{0,4},{4,0},{1,5},{5,1},{2,6},{6,2},{3,7},{7,3},{8,12},{12,8},{9,1... | collective-permute-start | bytes 3145736 | tf_op jit(solution)/shard_map/ppermute | solution.py:28
  61.2 18.7 %all-to-all-start.4 = ((bf16[4,512,256]{2,1,0:T(8,128)(2,1)}), bf16[4,512,256]{2,1,0:T(8,128)(2,1)S(1)}, u32[]{:S(2)}, u32[]{:S(2)}) async-start(bf16[4,512,256]{2,1,0:T(8,128)(2,1)} %broadcast_in_dim.22), calls=%async_computation.4 | async-start | bytes 2097152 | tf_op jit(solution)/shard_map/all_to_all | solution.py:20
  79.9 26.1 %collective-permute-start.3 = (bf16[2048,256]{1,0:T(8,128)(2,1)S(1)}, bf16[2048,256]{1,0:T(8,128)(2,1)S(1)}, u32[]{:S(2)}, u32[]{:S(2)}) collective-permute-start(bf16[2048,256]{1,0:T(8,128)(2,1)S(1)} %bitcast.93), channel_id=1, source_target_pairs={{0,4},{4,0},{1,5},{5,1},{2,6},{6,2},{3,7},{7,3},{8,12},{12,8},{9,1... | collective-permute-start | bytes 3145736 | tf_op jit(solution)/shard_map/ppermute | solution.py:28
  106.4 1.0 copy-start.1
  107.3 2.1 copy-start.4
  124.1 16.7 %all-to-all-start.3 = ((bf16[8,192,256]{2,1,0:T(8,128)(2,1)}), bf16[8,192,256]{2,1,0:T(8,128)(2,1)}, u32[]{:S(2)}, u32[]{:S(2)}) async-start(bf16[8,192,256]{2,1,0:T(8,128)(2,1)} %bitcast.10), calls=%async_computation.3 | async-start | bytes 1572864 | tf_op jit(solution)/shard_map/all_to_all | solution.py:20
  143.1 27.4 %all-to-all-start.6 = ((bf16[16,32,256]{2,1,0:T(8,128)(2,1)}), bf16[16,32,256]{2,1,0:T(8,128)(2,1)S(1)}, u32[]{:S(2)}, u32[]{:S(2)}) async-start(bf16[16,32,256]{2,1,0:T(8,128)(2,1)} %bitcast.27), calls=%async_computation.6 | async-start | bytes 524288 | tf_op jit(solution)/shard_map/all_to_all | solution.py:20
  146.8 18.0 %copy-start.2 = (f32[32,256]{1,0:T(8,128)S(1)}, f32[32,256]{1,0:T(8,128)}, u32[]{:S(2)}) copy-start(f32[32,256]{1,0:T(8,128)} %param.10) | copy-start | bytes 98308
  146.9 18.0 %copy-start.5 = (f32[32,256]{1,0:T(8,128)S(1)}, f32[32,256]{1,0:T(8,128)}, u32[]{:S(2)}) copy-start(f32[32,256]{1,0:T(8,128)} %param.11) | copy-start | bytes 98308
  146.9 23.5 %copy-start.6 = (f32[32,128]{1,0:T(8,128)S(1)}, f32[32,128]{1,0:T(8,128)}, u32[]{:S(2)}) copy-start(f32[32,128]{1,0:T(8,128)} %get-tuple-element.27) | copy-start | bytes 49156
  146.9 23.5 %copy-start.7 = (f32[32,128]{1,0:T(8,128)S(1)}, f32[32,128]{1,0:T(8,128)}, u32[]{:S(2)}) copy-start(f32[32,128]{1,0:T(8,128)} %get-tuple-element.28) | copy-start | bytes 49156
  154.7 6.1 %collective-permute-start.4 = (f32[32,128]{0,1:T(8,128)}, f32[32,128]{0,1:T(8,128)S(1)}, u32[]{:S(2)}, u32[]{:S(2)}) collective-permute-start(f32[32,128]{0,1:T(8,128)} %bitcast.111), channel_id=1, source_target_pairs={{0,1},{1,0},{2,3},{3,2},{4,5},{5,4},{6,7},{7,6},{8,9},{9,8},{10,11... | collective-permute-start | bytes 49160 | tf_op jit(solution)/shard_map/ppermute | solution.py:28
  161.6 8.8 %collective-permute-start.5 = (f32[32,128]{0,1:T(8,128)S(1)}, f32[32,128]{0,1:T(8,128)S(1)}, u32[]{:S(2)}, u32[]{:S(2)}) collective-permute-start(f32[32,128]{0,1:T(8,128)S(1)} %bitcast_add_fusion.2), channel_id=1, source_target_pairs={{0,3},{1,2},{2,1},{3,0},{4,7},{5,6},{6,5},{7,4},{8,11},{9,10},{10,... | collective-permute-start | bytes 49160 | tf_op jit(solution)/shard_map/ppermute | solution.py:28
  164.9 7.9 %collective-permute-start = (f32[2,32,256]{2,1,0:T(8,128)S(1)}, f32[2,32,256]{2,1,0:T(8,128)S(1)}, u32[]{:S(2)}, u32[]{:S(2)}) collective-permute-start(f32[2,32,256]{2,1,0:T(8,128)S(1)} %pad_maximum_fusion.4), channel_id=1, source_target_pairs={{0,0},{4,32},{8,64},{12,96},{16,128},{20,160},{24,192},{28,224},{3... | collective-permute-start | bytes 196616 | tf_op jit(solution)/shard_map/ppermute | solution.py:242
  198.9 16.0 %all-to-all-start.8 = ((bf16[4,576,256]{2,1,0:T(8,128)(2,1)}), bf16[4,576,256]{2,1,0:T(8,128)(2,1)S(1)}, u32[]{:S(2)}, u32[]{:S(2)}) async-start(bf16[4,576,256]{2,1,0:T(8,128)(2,1)} %broadcast_in_dim.27), calls=%async_computation.8 | async-start | bytes 2359296 | tf_op jit(solution)/shard_map/all_to_all | solution.py:20
  202.4 9.2 %collective-permute-start.6 = (f32[2,32,256]{2,1,0:T(8,128)S(1)}, f32[2,32,256]{2,1,0:T(8,128)S(1)}, u32[]{:S(2)}, u32[]{:S(2)}) collective-permute-start(f32[2,32,256]{2,1,0:T(8,128)S(1)} %pad_maximum_fusion.5), channel_id=1, source_target_pairs={{0,0},{32,4},{64,8},{96,12},{128,16},{160,20},{192,24},{224,28},{2... | collective-permute-start | bytes 196616 | tf_op jit(solution)/shard_map/ppermute | solution.py:324
  214.9 9.3 %collective-permute-start.7 = (bf16[4,576,256]{2,1,0:T(8,128)(2,1)S(1)}, bf16[4,576,256]{2,1,0:T(8,128)(2,1)S(1)}, u32[]{:S(2)}, u32[]{:S(2)}) collective-permute-start(bf16[4,576,256]{2,1,0:T(8,128)(2,1)S(1)} %all-to-all-done.8), channel_id=1, source_target_pairs={{0,4},{4,0},{1,5},{5,1},{2,6},{6,2},{3,7},{7,3},{8,12},{12,8},{9,1... | collective-permute-start | bytes 3538952 | tf_op jit(solution)/shard_map/ppermute | solution.py:28

commit v8 on v7

--- a/solution.py
+++ b/solution.py
@@ -291,21 +291,23 @@
     normed_part = lax.dot_general(preact_grad, weights, (((1,), (1,)), ((), ())), preferred_element_type=jnp.float32)
     proj_part = backward_features(normed_part, normed_a, normed_b, inv_scale, embedded)
     (start_a, count_a), (start_b, count_b) = shares
-    weight_grad = jnp.einsum(
-        "shbk,sbn->hkn",
-        columns_a.reshape(c * x, 2, count_a, -1),
-        group_grad[:, :count_a],
-        preferred_element_type=jnp.float32,
-    ) + jnp.stack(
+    weight_grad = jnp.concatenate(
         [
-            jnp.einsum(
-                "sbk,sbn->kn",
-                group_grad[:, at : at + count_b],
-                group_grad[:, start_b:examples],
-                preferred_element_type=jnp.float32,
+            sum(
+                jnp.einsum(
+                    "sbk,sbn->kn",
+                    part[:, at : at + count],
+                    group_grad[:, start : start + count],
+                    preferred_element_type=jnp.float32,
+                )
+                for part, at, start, count in (
+                    (columns_a, half * count_a, start_a, count_a),
+                    (group_grad, examples + half * count_b, start_b, count_b),
+                )
             )
-            for at in (examples, examples + count_b)
-        ]
+            for half in range(2)
+        ],
+        axis=0,
     )
     arrived = exchange(weight_grad.astype(jnp.bfloat16).reshape(zl * y, -1, hidden), ZY)
     small = proj_part.T

time: 229 us -> 230 us (level)
  no operation moved by 1% of the time
where the time goes in v8:
time: 230 us; the launch traced here: 228 us
  blocking collectives  74.1 us (32%)
  starting transfers between devices  55.8 us (24%)
  waiting for transfers between devices  46.1 us (20%)
  Pallas kernels  31.1 us (14%)
  matrix products  7.25 us (3%)
  other arithmetic  6.17 us (3%)
  local copies, waits for them, and re-layouts  6.07 us (3%)
    all_to_all x4, blocking collectives, exchange(): return lax.all_to_all(tiles, axis, split_axis=0, concat_axis=0, tiled=True)  74.1 us
    all_to_all x5, waiting for transfers between devices, exchange(): return lax.all_to_all(tiles, axis, split_axis=0, concat_axis=0, tiled=True)  32 us
    ppermute x6, starting transfers between devices, swapped(): lax.ppermute(x, axis, [(i, i ^ flip) for i in range(lax.axis_size(axis))])  24.5 us
    pallas_call x2, Pallas kernels, forward_features(): pl.pallas_call(forward_kernel, grid=(count // GROUP,), in_specs=[pl.Block...  23.3 us
    all_to_all x5, starting transfers between devices, exchange(): return lax.all_to_all(tiles, axis, split_axis=0, concat_axis=0, tiled=True)  19.2 us
    ppermute x6, waiting for transfers between devices, swapped(): lax.ppermute(x, axis, [(i, i ^ flip) for i in range(lax.axis_size(axis))])  9.14 us
    pallas_call x1, Pallas kernels, backward_features(): pl.pallas_call(backward_kernel, grid=(firsts + 1,), in_specs=[pl.BlockSpe...  7.76 us
    ppermute x1, starting transfers between devices, per_device(): state = lax.ppermute(jnp.stack([new_weight, new_momentum]), DP, to_owner)  6.53 us
  transfers between devices with their start and end apart: 13, of which 9 were waited for; matrix products, arithmetic and copies ran while one was open for 2% of the time, Pallas kernels for 14%

profile of v8, /device:TPU:1, one launch (start us, length us, event | category | flops | bytes accessed | tf_op | source)
XLA Modules:
  0.0 227.6 jit_solution(7863848239733652971)
XLA Ops:
  0.6 0.8 convert_element_type.34
  1.4 0.7 pad_maximum_fusion.9
  2.1 15.8 %all_to_all.45 = bf16[8,80,128]{2,1,0:T(8,128)(2,1)S(1)} all-to-all(bf16[8,80,128]{2,1,0:T(8,128)(2,1)S(1)} %broadcast_in_dim.21), channel_id=1, replica_groups=mesh['zl'=2,'y'=8,'x'=4,'c'=2,'mp'=4] {'y'}, dimensions={0} | all-to-all | bytes 327680 | tf_op jit(solution)/shard_map/all_to_all | solution.py:20
  17.9 19.1 %all_to_all.46 = bf16[8,128,128]{2,1,0:T(8,128)(2,1)S(1)} all-to-all(bf16[8,128,128]{2,1,0:T(8,128)(2,1)S(1)} %broadcast_in_dim.23), channel_id=1, replica_groups=mesh['zl'=2,'y'=8,'x'=4,'c'=2,'mp'=4] {'mp','zl'}, dimensions={0} | all-to-all | bytes 524288 | tf_op jit(solution)/shard_map/all_to_all | solution.py:20
  37.0 1.1 broadcast_in_dim.24
  38.1 4.0 %all-to-all-start.2 = ((bf16[4,1024,128]{2,1,0:T(8,128)(2,1)}), bf16[4,1024,128]{2,1,0:T(8,128)(2,1)S(1)}, u32[]{:S(2)}, u32[]{:S(2)}) async-start(bf16[4,1024,128]{2,1,0:T(8,128)(2,1)} %broadcast_in_dim.24), calls=%async_computation.2 | async-start | bytes 2097152 | tf_op jit(solution)/shard_map/all_to_all | solution.py:20
  42.2 0.1 copy.38
  42.3 2.1 collective-permute-start.1
  44.5 3.6 %collective-permute-done.1 = bf16[256,256]{1,0:T(8,128)(2,1)S(1)} collective-permute-done((bf16[256,256]{1,0:T(8,128)(2,1)S(1)}, bf16[256,256]{1,0:T(8,128)(2,1)S(1)}, u32[]{:S(2)}, u32[]{:S(2)}) %collective-permute-start.1) | collective-permute-done | bytes 131104 | tf_op jit(solution)/shard_map/ppermute | solution.py:28
  48.1 0.0 copy-start.3
  48.1 4.8 %all-to-all-done.2 = bf16[4,1024,128]{2,1,0:T(8,128)(2,1)S(1)} async-done(((bf16[4,1024,128]{2,1,0:T(8,128)(2,1)}), bf16[4,1024,128]{2,1,0:T(8,128)(2,1)S(1)}, u32[]{:S(2)}, u32[]{:S(2)}) %all-to-all-start.2) | async-done | bytes 1048608 | tf_op jit(solution)/shard_map/all_to_all | solution.py:20
  52.9 1.1 broadcast_in_dim.22
  54.0 7.2 %collective-permute-start.2 = (bf16[4096,128]{1,0:T(8,128)(2,1)S(1)}, bf16[4096,128]{1,0:T(8,128)(2,1)}, u32[]{:S(2)}, u32[]{:S(2)}) collective-permute-start(bf16[4096,128]{1,0:T(8,128)(2,1)S(1)} %bitcast.97), channel_id=1, source_target_pairs={{0,4},{4,0},{1,5},{5,1},{2,6},{6,2},{3,7},{7,3},{8,12},{12,8},{9,1... | collective-permute-start | bytes 3145736 | tf_op jit(solution)/shard_map/ppermute | solution.py:28
  61.2 3.5 %all-to-all-start.4 = ((bf16[4,512,256]{2,1,0:T(8,128)(2,1)}), bf16[4,512,256]{2,1,0:T(8,128)(2,1)S(1)}, u32[]{:S(2)}, u32[]{:S(2)}) async-start(bf16[4,512,256]{2,1,0:T(8,128)(2,1)} %broadcast_in_dim.22), calls=%async_computation.4 | async-start | bytes 2097152 | tf_op jit(solution)/shard_map/all_to_all | solution.py:20
  64.8 0.7 fusion.23.ids_ref
  65.5 14.4 %all-to-all-done.4 = bf16[4,512,256]{2,1,0:T(8,128)(2,1)S(1)} async-done(((bf16[4,512,256]{2,1,0:T(8,128)(2,1)}), bf16[4,512,256]{2,1,0:T(8,128)(2,1)S(1)}, u32[]{:S(2)}, u32[]{:S(2)}) %all-to-all-start.4) | async-done | bytes 1048608 | tf_op jit(solution)/shard_map/all_to_all | solution.py:20
  79.9 2.8 %collective-permute-start.3 = (bf16[2048,256]{1,0:T(8,128)(2,1)S(1)}, bf16[2048,256]{1,0:T(8,128)(2,1)S(1)}, u32[]{:S(2)}, u32[]{:S(2)}) collective-permute-start(bf16[2048,256]{1,0:T(8,128)(2,1)S(1)} %bitcast.90), channel_id=1, source_target_pairs={{0,4},{4,0},{1,5},{5,1},{2,6},{6,2},{3,7},{7,3},{8,12},{12,8},{9,1... | collective-permute-start | bytes 3145736 | tf_op jit(solution)/shard_map/ppermute | solution.py:28
  82.7 16.9 %fm_forward.2 = (bf16[128,128,128]{2,1,0:T(8,128)(2,1)}, bf16[16,96,256]{2,1,0:T(8,128)(2,1)}, f32[128,128]{1,0:T(8,128)}, f32[32,128]{1,0:T(8,128)}) custom-call(s32[128,128]{1,0:T(8,128)} %fusion.23.ids_ref, bf16[4096,128]{1,0:T(8,128)(2,1)} %bitcast.98, bf16[4096,128]{1,0:T(8,128)(2,1)} %collective-permute-done.2.far_ref, bf16[32,128]{1,0:T(8,128)(2,1)} %bitcast.110, ...), custom_call_target="tpu_custom_call" | custom-call | flops 9600000000 | bytes 5242880 | tf_op jit(solution)/shard_map/fm_forward/pallas_call | solution.py:109
  99.7 6.4 %fm_forward.3 = (bf16[128,128,128]{2,1,0:T(8,128)(2,1)}, bf16[16,32,256]{2,1,0:T(8,128)(2,1)}, f32[128,128]{1,0:T(8,128)}, f32[32,128]{1,0:T(8,128)}) custom-call(s32[128,128]{1,0:T(8,128)} %fusion.23.ids_ref, bf16[4096,128]{1,0:T(8,128)(2,1)} %bitcast.99, ...), custom_call_target="tpu_custom_call", output_to_operand_aliasing={{0}: (5, {}), {2}: (6, {})} | custom-call | flops 3200000000 | bytes 3145728 | tf_op jit(solution)/shard_map/fm_forward/pallas_call | solution.py:109
  106.0 0.0 collective-permute-done.3
  106.0 0.3 fusion
  106.4 0.2 copy.39
  106.6 0.7 copy-done.1
  107.3 0.5 convolution_bitcast_fusion.5
  107.8 1.6 convolution_bitcast_fusion.4
  109.4 0.1 multiply_convert_fusion
  109.5 0.1 pad_maximum_fusion
  109.6 14.6 %all_to_all.47 = bf16[8,192,256]{2,1,0:T(8,128)(2,1)S(1)} all-to-all(bf16[8,192,256]{2,1,0:T(8,128)(2,1)S(1)} %pad_maximum_fusion), channel_id=1, replica_groups=mesh['zl'=2,'y'=8,'x'=4,'c'=2,'mp'=4] {'c','x'}, dimensions={0} | all-to-all | bytes 1572864 | tf_op jit(solution)/shard_map/all_to_all | solution.py:20
  124.1 4.4 %all-to-all-start.3 = ((bf16[8,192,256]{2,1,0:T(8,128)(2,1)}), bf16[8,192,256]{2,1,0:T(8,128)(2,1)}, u32[]{:S(2)}, u32[]{:S(2)}) async-start(bf16[8,192,256]{2,1,0:T(8,128)(2,1)} %bitcast.10), calls=%async_computation.3 | async-start | bytes 1572864 | tf_op jit(solution)/shard_map/all_to_all | solution.py:20
  128.6 2.1 fusion.31.grad_ref
  130.7 0.2 convolution_bitcast_fusion.3
  130.9 0.2 convolution_bitcast_fusion.2
  131.2 9.7 %all-to-all-done.3 = bf16[8,192,256]{2,1,0:T(8,128)(2,1)} async-done(((bf16[8,192,256]{2,1,0:T(8,128)(2,1)}), bf16[8,192,256]{2,1,0:T(8,128)(2,1)}, u32[]{:S(2)}, u32[]{:S(2)}) %all-to-all-start.3) | async-done | bytes 786464 | tf_op jit(solution)/shard_map/all_to_all | solution.py:20
  140.9 1.3 fusion.4
  142.2 1.3 fusion.3
  143.5 0.7 pad_maximum_fusion.3
  144.2 3.7 %all-to-all-start.6 = ((bf16[16,32,256]{2,1,0:T(8,128)(2,1)}), bf16[16,32,256]{2,1,0:T(8,128)(2,1)S(1)}, u32[]{:S(2)}, u32[]{:S(2)}) async-start(bf16[16,32,256]{2,1,0:T(8,128)(2,1)} %bitcast.23), calls=%async_computation.6 | async-start | bytes 524288 | tf_op jit(solution)/shard_map/all_to_all | solution.py:20
  147.9 0.0 copy-start.2
  148.0 0.0 copy-start.5
  148.0 0.0 copy-start.6
  148.0 0.0 copy-start.7
  148.0 7.8 %fm_backward.1 = f32[128,32]{1,0:T(8,128)} custom-call(f32[128,4096]{1,0:T(8,128)} %fusion.31.grad_ref, bf16[16,96,256]{2,1,0:T(8,128)(2,1)} %get-tuple-element.20.first_ref, bf16[16,32,256]{2,1,0:T(8,128)(2,1)} %get-tuple-element.24.last_ref, f32[128,128]{1,0:T(8,128)} %get-tuple-element.25.inv_ref, bf16[128,128,128]{2,1,0:T(8,128)(2,1)} %get-tuple-element.26.emb_ref), custom_call_target="tpu_custom_call" | custom-call | flops 5120000000 | bytes 7340032 | tf_op jit(solution)/shard_map/fm_backward/pallas_call | solution.py:194
  155.8 2.3 collective-permute-start.4
  158.0 3.8 %collective-permute-done.4 = f32[32,128]{0,1:T(8,128)S(1)} collective-permute-done((f32[32,128]{0,1:T(8,128)}, f32[32,128]{0,1:T(8,128)S(1)}, u32[]{:S(2)}, u32[]{:S(2)}) %collective-permute-start.4) | collective-permute-done | bytes 16416 | tf_op jit(solution)/shard_map/ppermute | solution.py:28
  161.9 0.9 bitcast_add_fusion.2
  162.7 3.2 %collective-permute-start.5 = (f32[32,128]{0,1:T(8,128)S(1)}, f32[32,128]{0,1:T(8,128)S(1)}, u32[]{:S(2)}, u32[]{:S(2)}) collective-permute-start(f32[32,128]{0,1:T(8,128)S(1)} %bitcast_add_fusion.2), channel_id=1, source_target_pairs={{0,3},{1,2},{2,1},{3,0},{4,7},{5,6},{6,5},{7,4},{8,11},{9,10},{10,... | collective-permute-start | bytes 49160 | tf_op jit(solution)/shard_map/ppermute | solution.py:28
  166.0 5.5 %collective-permute-start = (f32[2,32,256]{2,1,0:T(8,128)S(1)}, f32[2,32,256]{2,1,0:T(8,128)S(1)}, u32[]{:S(2)}, u32[]{:S(2)}) collective-permute-start(f32[2,32,256]{2,1,0:T(8,128)S(1)} %pad_maximum_fusion.5), channel_id=1, source_target_pairs={{0,0},{4,32},{8,64},{12,96},{16,128},{20,160},{24,192},{28,224},{3... | collective-permute-start | bytes 196616 | tf_op jit(solution)/shard_map/ppermute | solution.py:242
  171.5 0.0 collective-permute-done.5
  171.6 0.1 copy.41
  171.6 0.0 all-to-all-done.6
  171.7 2.2 collective-permute-done
  174.0 24.7 %all_to_all.48 = bf16[16,64,256]{2,1,0:T(8,128)(2,1)S(1)} all-to-all(bf16[16,64,256]{2,1,0:T(8,128)(2,1)S(1)} %broadcast_in_dim.26), channel_id=1, replica_groups=mesh['zl'=2,'y'=8,'x'=4,'c'=2,'mp'=4] {'zl','y'}, dimensions={0} | all-to-all | bytes 1048576 | tf_op jit(solution)/shard_map/all_to_all | solution.py:20
  198.8 1.1 broadcast_in_dim.27
  199.9 3.5 %all-to-all-start.8 = ((bf16[4,576,256]{2,1,0:T(8,128)(2,1)}), bf16[4,576,256]{2,1,0:T(8,128)(2,1)S(1)}, u32[]{:S(2)}, u32[]{:S(2)}) async-start(bf16[4,576,256]{2,1,0:T(8,128)(2,1)} %broadcast_in_dim.27), calls=%async_computation.8 | async-start | bytes 2359296 | tf_op jit(solution)/shard_map/all_to_all | solution.py:20
  203.5 6.5 %collective-permute-start.6 = (f32[2,32,256]{2,1,0:T(8,128)S(1)}, f32[2,32,256]{2,1,0:T(8,128)S(1)}, u32[]{:S(2)}, u32[]{:S(2)}) collective-permute-start(f32[2,32,256]{2,1,0:T(8,128)S(1)} %pad_maximum_fusion.6), channel_id=1, source_target_pairs={{0,0},{32,4},{64,8},{96,12},{128,16},{160,20},{192,24},{224,28},{2... | collective-permute-start | bytes 196616 | tf_op jit(solution)/shard_map/ppermute | solution.py:326
  210.0 2.7 %collective-permute-done.6 = f32[2,32,256]{2,1,0:T(8,128)S(1)} collective-permute-done((f32[2,32,256]{2,1,0:T(8,128)S(1)}, f32[2,32,256]{2,1,0:T(8,128)S(1)}, u32[]{:S(2)}, u32[]{:S(2)}) %collective-permute-start.6) | collective-permute-done | bytes 65568 | tf_op jit(solution)/shard_map/ppermute | solution.py:326
  212.7 3.1 %all-to-all-done.8 = bf16[4,576,256]{2,1,0:T(8,128)(2,1)S(1)} async-done(((bf16[4,576,256]{2,1,0:T(8,128)(2,1)}), bf16[4,576,256]{2,1,0:T(8,128)(2,1)S(1)}, u32[]{:S(2)}, u32[]{:S(2)}) %all-to-all-start.8) | async-done | bytes 1179680 | tf_op jit(solution)/shard_map/all_to_all | solution.py:20
  215.8 6.9 %collective-permute-start.7 = (bf16[4,576,256]{2,1,0:T(8,128)(2,1)S(1)}, bf16[4,576,256]{2,1,0:T(8,128)(2,1)S(1)}, u32[]{:S(2)}, u32[]{:S(2)}) collective-permute-start(bf16[4,576,256]{2,1,0:T(8,128)(2,1)S(1)} %all-to-all-done.8), channel_id=1, source_target_pairs={{0,4},{4,0},{1,5},{5,1},{2,6},{6,2},{3,7},{7,3},{8,12},{12,8},{9,1... | collective-permute-start | bytes 3538952 | tf_op jit(solution)/shard_map/ppermute | solution.py:28
  222.8 0.6 slice_bitcast_fusion.2
  223.4 0.1 slice_bitcast_fusion.1
  223.5 1.7 collective-permute-done.7
  225.3 0.6 slice_bitcast_fusion.4
  225.9 0.1 slice_bitcast_fusion
  226.0 1.6 maximum_select_fusion.1
  (38 shorter events, 0.5 us)
Async XLA Ops:
  38.1 14.7 %all-to-all-start.2 = ((bf16[4,1024,128]{2,1,0:T(8,128)(2,1)}), bf16[4,1024,128]{2,1,0:T(8,128)(2,1)S(1)}, u32[]{:S(2)}, u32[]{:S(2)}) async-start(bf16[4,1024,128]{2,1,0:T(8,128)(2,1)} %broadcast_in_dim.24), calls=%async_computation.2 | async-start | bytes 2097152 | tf_op jit(solution)/shard_map/all_to_all | solution.py:20
  42.3 5.7 %collective-permute-start.1 = (bf16[256,256]{1,0:T(8,128)(2,1)S(1)}, bf16[256,256]{1,0:T(8,128)(2,1)S(1)}, u32[]{:S(2)}, u32[]{:S(2)}) collective-permute-start(bf16[256,256]{1,0:T(8,128)(2,1)S(1)} %bitcast.106), channel_id=1, source_target_pairs={{0,256},{256,0},{1,257},{257,1},{2,258},{258,2},{3,259},{259,3},{4... | collective-permute-start | bytes 393224 | tf_op jit(solution)/shard_map/ppermute | solution.py:28
  48.1 16.7 %copy-start.3 = (s32[128,128]{1,0:T(8,128)S(1)}, s32[128,128]{1,0:T(8,128)}, u32[]{:S(2)}) copy-start(s32[128,128]{1,0:T(8,128)} %param.7) | copy-start | bytes 196612
  52.9 29.8 %copy-start = (bf16[4,1024,128]{2,1,0:T(8,128)(2,1)}, bf16[4,1024,128]{2,1,0:T(8,128)(2,1)S(1)}, u32[]{:S(2)}) copy-start(bf16[4,1024,128]{2,1,0:T(8,128)(2,1)S(1)} %all-to-all-done.2) | copy-start | bytes 3145732
  54.0 28.7 %collective-permute-start.2 = (bf16[4096,128]{1,0:T(8,128)(2,1)S(1)}, bf16[4096,128]{1,0:T(8,128)(2,1)}, u32[]{:S(2)}, u32[]{:S(2)}) collective-permute-start(bf16[4096,128]{1,0:T(8,128)(2,1)S(1)} %bitcast.97), channel_id=1, source_target_pairs={{0,4},{4,0},{1,5},{5,1},{2,6},{6,2},{3,7},{7,3},{8,12},{12,8},{9,1... | collective-permute-start | bytes 3145736 | tf_op jit(solution)/shard_map/ppermute | solution.py:28
  61.2 18.7 %all-to-all-start.4 = ((bf16[4,512,256]{2,1,0:T(8,128)(2,1)}), bf16[4,512,256]{2,1,0:T(8,128)(2,1)S(1)}, u32[]{:S(2)}, u32[]{:S(2)}) async-start(bf16[4,512,256]{2,1,0:T(8,128)(2,1)} %broadcast_in_dim.22), calls=%async_computation.4 | async-start | bytes 2097152 | tf_op jit(solution)/shard_map/all_to_all | solution.py:20
  79.9 26.1 %collective-permute-start.3 = (bf16[2048,256]{1,0:T(8,128)(2,1)S(1)}, bf16[2048,256]{1,0:T(8,128)(2,1)S(1)}, u32[]{:S(2)}, u32[]{:S(2)}) collective-permute-start(bf16[2048,256]{1,0:T(8,128)(2,1)S(1)} %bitcast.90), channel_id=1, source_target_pairs={{0,4},{4,0},{1,5},{5,1},{2,6},{6,2},{3,7},{7,3},{8,12},{12,8},{9,1... | collective-permute-start | bytes 3145736 | tf_op jit(solution)/shard_map/ppermute | solution.py:28
  106.4 1.0 copy-start.1
  107.3 2.1 copy-start.4
  124.1 16.7 %all-to-all-start.3 = ((bf16[8,192,256]{2,1,0:T(8,128)(2,1)}), bf16[8,192,256]{2,1,0:T(8,128)(2,1)}, u32[]{:S(2)}, u32[]{:S(2)}) async-start(bf16[8,192,256]{2,1,0:T(8,128)(2,1)} %bitcast.10), calls=%async_computation.3 | async-start | bytes 1572864 | tf_op jit(solution)/shard_map/all_to_all | solution.py:20
  144.2 27.4 %all-to-all-start.6 = ((bf16[16,32,256]{2,1,0:T(8,128)(2,1)}), bf16[16,32,256]{2,1,0:T(8,128)(2,1)S(1)}, u32[]{:S(2)}, u32[]{:S(2)}) async-start(bf16[16,32,256]{2,1,0:T(8,128)(2,1)} %bitcast.23), calls=%async_computation.6 | async-start | bytes 524288 | tf_op jit(solution)/shard_map/all_to_all | solution.py:20
  147.9 18.0 %copy-start.2 = (f32[32,256]{1,0:T(8,128)S(1)}, f32[32,256]{1,0:T(8,128)}, u32[]{:S(2)}) copy-start(f32[32,256]{1,0:T(8,128)} %param.10) | copy-start | bytes 98308
  148.0 18.0 %copy-start.5 = (f32[32,256]{1,0:T(8,128)S(1)}, f32[32,256]{1,0:T(8,128)}, u32[]{:S(2)}) copy-start(f32[32,256]{1,0:T(8,128)} %param.11) | copy-start | bytes 98308
  148.0 23.5 %copy-start.6 = (f32[32,128]{1,0:T(8,128)S(1)}, f32[32,128]{1,0:T(8,128)}, u32[]{:S(2)}) copy-start(f32[32,128]{1,0:T(8,128)} %get-tuple-element.27) | copy-start | bytes 49156
  148.0 23.5 %copy-start.7 = (f32[32,128]{1,0:T(8,128)S(1)}, f32[32,128]{1,0:T(8,128)}, u32[]{:S(2)}) copy-start(f32[32,128]{1,0:T(8,128)} %get-tuple-element.28) | copy-start | bytes 49156
  155.8 6.1 %collective-permute-start.4 = (f32[32,128]{0,1:T(8,128)}, f32[32,128]{0,1:T(8,128)S(1)}, u32[]{:S(2)}, u32[]{:S(2)}) collective-permute-start(f32[32,128]{0,1:T(8,128)} %bitcast.108), channel_id=1, source_target_pairs={{0,1},{1,0},{2,3},{3,2},{4,5},{5,4},{6,7},{7,6},{8,9},{9,8},{10,11... | collective-permute-start | bytes 49160 | tf_op jit(solution)/shard_map/ppermute | solution.py:28
  162.7 8.8 %collective-permute-start.5 = (f32[32,128]{0,1:T(8,128)S(1)}, f32[32,128]{0,1:T(8,128)S(1)}, u32[]{:S(2)}, u32[]{:S(2)}) collective-permute-start(f32[32,128]{0,1:T(8,128)S(1)} %bitcast_add_fusion.2), channel_id=1, source_target_pairs={{0,3},{1,2},{2,1},{3,0},{4,7},{5,6},{6,5},{7,4},{8,11},{9,10},{10,... | collective-permute-start | bytes 49160 | tf_op jit(solution)/shard_map/ppermute | solution.py:28
  166.0 7.9 %collective-permute-start = (f32[2,32,256]{2,1,0:T(8,128)S(1)}, f32[2,32,256]{2,1,0:T(8,128)S(1)}, u32[]{:S(2)}, u32[]{:S(2)}) collective-permute-start(f32[2,32,256]{2,1,0:T(8,128)S(1)} %pad_maximum_fusion.5), channel_id=1, source_target_pairs={{0,0},{4,32},{8,64},{12,96},{16,128},{20,160},{24,192},{28,224},{3... | collective-permute-start | bytes 196616 | tf_op jit(solution)/shard_map/ppermute | solution.py:242
  199.9 15.9 %all-to-all-start.8 = ((bf16[4,576,256]{2,1,0:T(8,128)(2,1)}), bf16[4,576,256]{2,1,0:T(8,128)(2,1)S(1)}, u32[]{:S(2)}, u32[]{:S(2)}) async-start(bf16[4,576,256]{2,1,0:T(8,128)(2,1)} %broadcast_in_dim.27), calls=%async_computation.8 | async-start | bytes 2359296 | tf_op jit(solution)/shard_map/all_to_all | solution.py:20
  203.5 9.2 %collective-permute-start.6 = (f32[2,32,256]{2,1,0:T(8,128)S(1)}, f32[2,32,256]{2,1,0:T(8,128)S(1)}, u32[]{:S(2)}, u32[]{:S(2)}) collective-permute-start(f32[2,32,256]{2,1,0:T(8,128)S(1)} %pad_maximum_fusion.6), channel_id=1, source_target_pairs={{0,0},{32,4},{64,8},{96,12},{128,16},{160,20},{192,24},{224,28},{2... | collective-permute-start | bytes 196616 | tf_op jit(solution)/shard_map/ppermute | solution.py:326
  215.8 9.4 %collective-permute-start.7 = (bf16[4,576,256]{2,1,0:T(8,128)(2,1)S(1)}, bf16[4,576,256]{2,1,0:T(8,128)(2,1)S(1)}, u32[]{:S(2)}, u32[]{:S(2)}) collective-permute-start(bf16[4,576,256]{2,1,0:T(8,128)(2,1)S(1)} %all-to-all-done.8), channel_id=1, source_target_pairs={{0,4},{4,0},{1,5},{5,1},{2,6},{6,2},{3,7},{7,3},{8,12},{12,8},{9,1... | collective-permute-start | bytes 3538952 | tf_op jit(solution)/shard_map/ppermute | solution.py:28
